TPU v7x, 32 devices: a whole 2x2x4 slice. The times are simulated.
32 devices in a mesh: rows: 8 (over z, x), width: 4 (over y, core).
Axes of the slice: x: 2, y: 2, z: 4, core: 2. Of those that a mesh axis runs over, the one named last changes fastest.
Arguments:
- w_gate: float32 [3072, 8192], P('rows', 'width'), may hold values from -0.15625 to 0.15625
- avg_gate: float32 [3072, 8192], P('rows', 'width'), may hold values from -0.109375 to 0.109375
- w_up: float32 [3072, 8192], P('rows', 'width'), may hold values from -0.15625 to 0.15625
- avg_up: float32 [3072, 8192], P('rows', 'width'), may hold values from -0.109375 to 0.109375
- norm_gain: float32 [3072], P('rows'), may hold values from 0.25 to 1.75
Outputs:
- serve_gate: bfloat16 [3072, 8192], P(None, 'width')
- serve_up: bfloat16 [3072, 8192], P(None, 'width')
- factor_gate: float32 [8192], P('width')
- factor_up: float32 [8192], P('width')
All inputs are finite; a program needn't handle non-finite values. Where the computation divides by a largest or mean magnitude, that divisor is 1e-20 or more.
Results may differ from a plain program's by a relative error of at most 0.001.
Values may be sent and summed in bfloat16 or wider, within the bound.
No kernel may reach another device: no remote copies, remote signals or barrier semaphores. Data moves between devices by JAX's collectives and lax.ppermute only.
A program may use at most 128 MiB of HBM per device.

v0:
```python
import functools

import jax
import jax.numpy as jnp
from jax import lax
from jax.experimental import pallas as pl
from jax.experimental.pallas import tpu as pltpu
from jax.sharding import PartitionSpec as P


keep_rate = 0.7

SPAN = 250.0


def gained(w_ref, a_ref, gain):
    fresh = keep_rate * a_ref[...] + (1.0 - keep_rate) * w_ref[...]
    return fresh * gain


def tall_gain(gain_ref, width):
    rows = gain_ref.shape[0]
    lanes = jnp.broadcast_to(gain_ref[...].reshape(1, rows), (128, rows)).T
    return jnp.concatenate([lanes] * (width // 128), axis=1)


def coded(x):
    size = jnp.abs(x)
    m = jnp.max(size, axis=0, keepdims=True)
    y = jnp.exp2(size * (SPAN / jnp.maximum(m, 1e-30)) - SPAN / 2)
    return jnp.where(x < 0, -y, y).astype(jnp.bfloat16), m


def encode_body(gain_ref, *refs, picks, earlier):
    count = len(picks)
    ins, outs = refs[: 2 * count], refs[2 * count + earlier :]
    half_rows, width = ins[0].shape
    tall = tall_gain(gain_ref, width)
    for i, half in enumerate(picks):
        gain = tall[half * half_rows : (half + 1) * half_rows]
        y, m = coded(gained(ins[2 * i], ins[2 * i + 1], gain))
        outs[i][...] = y
        outs[count][earlier + i] = m
    if earlier:
        outs[count][0] = refs[2 * count][0]


def encode(chunks, gain, block, maxima=None):
    half_rows, columns = chunks[0][0].shape[0] // 2, chunks[0][0].shape[1]
    operands, in_specs, out_shape, out_specs = [gain], [pl.BlockSpec(gain.shape, lambda j: (0,))], [], []
    earlier = 0 if maxima is None else 1
    for w, avg, half in chunks:
        operands += [w, avg]
        in_specs += [pl.BlockSpec((half_rows, block), lambda j, half=half: (half, j))] * 2
        out_shape.append(jax.ShapeDtypeStruct((half_rows, columns), jnp.bfloat16))
        out_specs.append(pl.BlockSpec((half_rows, block), lambda j: (0, j)))
    if earlier:
        operands.append(maxima)
        in_specs.append(pl.BlockSpec((1, 1, block), lambda j: (0, 0, j)))
    count = earlier + len(chunks)
    return pl.pallas_call(
        functools.partial(encode_body, picks=[half for _, _, half in chunks], earlier=earlier),
        grid=(columns // block,),
        in_specs=in_specs,
        out_specs=out_specs + [pl.BlockSpec((count, 1, block), lambda j: (0, 0, j))],
        out_shape=out_shape + [jax.ShapeDtypeStruct((count, 1, columns), jnp.float32)],
        name="encode",
    )(*operands)


def own_body(me_ref, wg_ref, ag_ref, wu_ref, au_ref, g_ref, f_ref, og_ref, ou_ref, token_ref):
    del me_ref
    gain = tall_gain(g_ref, wg_ref.shape[1])
    og_ref[...] = (gained(wg_ref, ag_ref, gain) / f_ref[0:1, :]).astype(jnp.bfloat16)
    ou_ref[...] = (gained(wu_ref, au_ref, gain) / f_ref[1:2, :]).astype(jnp.bfloat16)
    token_ref[...] = jnp.zeros_like(token_ref)


def own_share(me, shards, w_gate, avg_gate, w_up, avg_up, gain, factors, block):
    rows, columns = w_gate.shape
    tile = pl.BlockSpec((rows, block), lambda j, me: (0, j))
    landed = pl.BlockSpec((rows, block), lambda j, me: (me[0], j))
    out = jax.ShapeDtypeStruct((rows * shards, columns), jnp.bfloat16)
    return pl.pallas_call(
        own_body,
        grid_spec=pltpu.PrefetchScalarGridSpec(
            num_scalar_prefetch=1,
            grid=(columns // block,),
            in_specs=[tile] * 4
            + [
                pl.BlockSpec(gain.shape, lambda j, me: (0,)),
                pl.BlockSpec((2, block), lambda j, me: (0, j)),
            ],
            out_specs=[landed, landed, pl.BlockSpec((8, 128), lambda j, me: (0, 0))],
        ),
        out_shape=[out, out, jax.ShapeDtypeStruct((8, 128), jnp.float32)],
        name="own_share",
    )(me, w_gate, avg_gate, w_up, avg_up, gain, factors)


def ratios_body(*refs):
    tables, (ratio_ref, factor_ref) = refs[:-2], refs[-2:]
    order = [0, 2, 4, 6, 1, 3, 5, 7]
    rows = [ref[i] for ref in tables for i in range(ref.shape[0])]
    for t in range(2):
        mine = [rows[4 * place + c] for place in range(8) for c in (t, t + 2)]
        factor = functools.reduce(jnp.maximum, mine)
        factor_ref[t : t + 1, :] = factor
        for place, shard in enumerate(order):
            for c in (t, t + 2):
                ratio_ref[4 * shard + c] = rows[4 * place + c] / factor


def ratios_of(tables):
    columns = tables[0].shape[-1]
    return pl.pallas_call(
        ratios_body,
        out_shape=[
            jax.ShapeDtypeStruct((32, 1, columns), jnp.float32),
            jax.ShapeDtypeStruct((2, columns), jnp.float32),
        ],
        name="ratios",
    )(*tables)


def decoded(y, ratio):
    y = y.astype(jnp.float32)
    x = jnp.log2(jnp.abs(y)) * (ratio * (1.0 / SPAN)) + ratio * 0.5
    return jnp.where(y < 0, -x, x).astype(jnp.bfloat16)


def decode_body(me_ref, y_ref, r_ref, whole_ref, out_ref, token_ref):
    del me_ref, whole_ref
    out_ref[...] = decoded(y_ref[...], r_ref[0])
    token_ref[...] = jnp.zeros_like(token_ref)


def decode(whole, chunk, ratios, me, shard_of, c, block):
    half_rows, columns = chunk.shape
    return pl.pallas_call(
        decode_body,
        grid_spec=pltpu.PrefetchScalarGridSpec(
            num_scalar_prefetch=1,
            grid=(columns // block,),
            in_specs=[
                pl.BlockSpec((half_rows, block), lambda j, me: (0, j)),
                pl.BlockSpec((1, 1, block), lambda j, me: ((shard_of(me[0]) ^ me[0]) * 4 + c, 0, j)),
                pl.BlockSpec(memory_space=pl.ANY),
            ],
            out_specs=[
                pl.BlockSpec((half_rows, block), lambda j, me: (2 * shard_of(me[0]) + c // 2, j)),
                pl.BlockSpec((8, 128), lambda j, me: (0, 0)),
            ],
        ),
        out_shape=[
            jax.ShapeDtypeStruct(whole.shape, whole.dtype),
            jax.ShapeDtypeStruct((8, 128), jnp.float32),
        ],
        input_output_aliases={3: 0},
        name="decode",
    )(me, chunk, ratios, whole)


def last_body(me_ref, y0_ref, y1_ref, r0_ref, r1_ref, whole_ref, out_ref, buffer, sems, *, starts_of, pieces):
    del whole_ref
    rows = y0_ref.shape[0] // pieces
    copies = []
    for i, (y_ref, r_ref) in enumerate(((y0_ref, r0_ref), (y1_ref, r1_ref))):
        start = starts_of[i](me_ref[0]) * y_ref.shape[0]
        for p in range(pieces):
            part = pl.ds(p * rows, rows)
            buffer[i, part] = decoded(y_ref[part], r_ref[0])
            copies.append(
                pltpu.make_async_copy(buffer.at[i, part], out_ref.at[pl.ds(start + p * rows, rows)], sems.at[i, p])
            )
            copies[-1].start()
    for copy in copies:
        copy.wait()


def decode_last(whole, chunks, ratios, me, shards_of, cs, pieces=4):
    half_rows, columns = chunks[0].shape
    kept = pl.BlockSpec(memory_space=pltpu.VMEM)
    ratio = lambda shard_of, c: pl.BlockSpec(
        (1, 1, columns), lambda j, me: ((shard_of(me[0]) ^ me[0]) * 4 + c, 0, 0)
    )
    starts_of = [lambda me, at=at, c=c: 2 * at(me) + c // 2 for at, c in zip(shards_of, cs)]
    return pl.pallas_call(
        functools.partial(last_body, starts_of=starts_of, pieces=pieces),
        grid_spec=pltpu.PrefetchScalarGridSpec(
            num_scalar_prefetch=1,
            grid=(1,),
            in_specs=[kept, kept, *map(ratio, shards_of, cs), pl.BlockSpec(memory_space=pl.ANY)],
            out_specs=pl.BlockSpec(memory_space=pl.ANY),
            scratch_shapes=[
                pltpu.VMEM((2, half_rows, columns), whole.dtype),
                pltpu.SemaphoreType.DMA((2, pieces)),
            ],
        ),
        out_shape=jax.ShapeDtypeStruct(whole.shape, whole.dtype),
        input_output_aliases={5: 0},
        name="decode_last",
    )(me, *chunks, ratios, ratios, whole)


def after(value, *tokens):
    return lax.optimization_barrier((value, *tokens))[0]


def across_of(me):
    return me ^ 1


def buddy_of(me):
    return me ^ 2


def diagonal_of(me):
    return me ^ 3


def near_of(me):
    return jnp.where(me < 4, 4, 2) + (me & 1)


def far_of(me):
    return jnp.where(me < 4, 6, 0) + (me & 1)


def near_across_of(me):
    return near_of(me) ^ 1


def far_across_of(me):
    return far_of(me) ^ 1


def local_plane(w_gate, avg_gate, w_up, avg_up, norm_gain):
    block = min(w_gate.shape[1], 1024)
    index = lax.axis_index("rows")
    outer = (index < 2) | (index >= 6)
    me = jnp.reshape(index, (1,)).astype(jnp.int32)

    def hop(value, pairs):
        both = [(2 * a + side, 2 * b + side) for a, b in pairs for side in (0, 1)]
        return lax.ppermute(value, "rows", both)

    across = lambda value: lax.ppermute(value, "rows", [(i, i ^ 1) for i in range(8)])
    buddies = lambda value: hop(value, [(0, 1), (1, 0), (2, 3), (3, 2)])
    outward = lambda value: hop(value, [(1, 0), (2, 3)])
    middle = lambda value: hop(value, [(1, 2), (2, 1)])
    skip = lambda value: hop(value, [(0, 2), (2, 0), (1, 3), (3, 1)])

    first, maxima = encode([(w_gate, avg_gate, 0)], norm_gain, block)
    others = [(w_up, avg_up, 0), (w_gate, avg_gate, 1), (w_up, avg_up, 1)]
    *rest, maxima = encode(others, norm_gain, block // 2, maxima)
    own = [first, *rest]

    X, B, M, O, V, F = {}, {}, {}, {}, {}, {}
    tables = [maxima]
    factors = ratios = None
    wholes, tokens, waiting = [None, None], [], []

    def arrived(k):
        got = [X[k]]
        if k < 4:
            got += [B[k], M[k]]
            waiting.extend([(X[k], across_of, k), (B[k], buddy_of, k)])
        elif k < 8:
            got += [O[k], M[k]]
        elif k < 12:
            got += [O[k]]
        else:
            got += [F[k - 12]]
            waiting.append((F[k - 12], diagonal_of, k - 12))
        if 4 <= k < 6:
            waiting.append((X[k], diagonal_of, k - 2))
        if 6 <= k < 10:
            waiting.append((X[k], near_across_of, k - 6))
        if 10 <= k:
            waiting.append((X[k], far_across_of, k - 10))
        if 4 <= k < 12:
            j = k - 4
            V[j] = jnp.where(outer, O[k], M[j])
            waiting.append((V[j], near_of if j < 4 else far_of, j % 4))
        return got

    def send(k, *ties):
        tie = lambda value: after(value, *ties) if ties else value
        if k < 4:
            X[k] = across(tie(own[k]))
        elif k < 6:
            X[k] = across(tie(B[k - 2]))
        else:
            X[k] = across(tie(V[k - 6]))
        if k < 4:
            B[k] = buddies(tie(own[k]))
        elif k < 12:
            O[k] = outward(tie(M[k - 4]))
        else:
            F[k - 12] = buddies(tie(X[k - 12]))
        if k < 4:
            M[k] = middle(tie(own[k]))
        elif k < 8:
            M[k] = middle(tie(B[k - 4]))

    def settle(count):
        done = []
        for _ in range(min(count, len(waiting))):
            chunk, shard_of, c = waiting.pop(0)
            wholes[c % 2], token = decode(wholes[c % 2], chunk, ratios, me, shard_of, c, block)
            done.append(token)
        return done

    send(0)
    tables.append(buddies(maxima))
    send(1)
    for k in range(14):
        got = arrived(k)
        if k == 0:
            got.append(tables[1])
            tables.append(skip(after(jnp.concatenate(tables, axis=0), *got)))
        if k == 1:
            got.append(tables[2])
            tables.append(across(after(jnp.concatenate(tables, axis=0), *got)))
        if k == 2:
            got.append(tables[3])
            ratios, factors = ratios_of(tables)
        if k + 2 < 14:
            send(k + 2, *got, *tokens)
        if k == 2:
            *wholes, token = own_share(me, 8, w_gate, avg_gate, w_up, avg_up, norm_gain, factors, block // 2)
            tokens = [token]
        if k >= 3:
            tokens = settle(3 if k < 13 else len(waiting) - 2)
    chunks, shards_of, cs = zip(*waiting)
    t = cs[0] % 2
    wholes[t] = decode_last(wholes[t], chunks, ratios, me, shards_of, cs)
    return (*wholes, factors[0], factors[1])


def local_any(w_gate, avg_gate, w_up, avg_up, norm_gain):
    fresh_gained_gate = (keep_rate * avg_gate + (1.0 - keep_rate) * w_gate) * norm_gain[:, None]
    fresh_gained_up = (keep_rate * avg_up + (1.0 - keep_rate) * w_up) * norm_gain[:, None]
    factor_gate, factor_up = lax.pmax(
        (jnp.max(jnp.abs(fresh_gained_gate), axis=0), jnp.max(jnp.abs(fresh_gained_up), axis=0)),
        "rows",
    )
    serve_gate = lax.all_gather((fresh_gained_gate / factor_gate).astype(jnp.bfloat16), "rows", axis=0, tiled=True)
    serve_up = lax.all_gather((fresh_gained_up / factor_up).astype(jnp.bfloat16), "rows", axis=0, tiled=True)
    return serve_gate, serve_up, factor_gate, factor_up


def solution(mesh):
    plane = mesh.shape["rows"] == 8

    def local(*args):
        return (local_plane if plane else local_any)(*args)

    return jax.shard_map(
        local,
        mesh=mesh,
        in_specs=(P("rows", "width"),) * 4 + (P("rows"),),
        out_specs=(P(None, "width"), P(None, "width"), P("width"), P("width")),
        check_vma=False,
    )
```

profile of v0, /device:TPU:0, one launch (start us, length us, event | category | flops | bytes accessed | tf_op | source)
XLA Modules:
  0.0 279.9 jit_solution(16273054882056172301)
XLA Ops:
  0.6 3.1 %encode.2 = (bf16[192,2048]{1,0:T(8,128)(2,1)}, f32[1,1,2048]{2,1,0:T(1,128)}) custom-call(f32[384]{0:T(512)} %g_ref.1, f32[384,2048]{1,0:T(8,128)} %wg_ref.1, f32[384,2048]{1,0:T(8,128)} %ag_ref.1), custom_call_target="tpu_custom_call" | custom-call | tf_op jit(solution)/shard_map/encode/pallas_call | solution.py:61
  3.8 3.0 %collective-permute-start = (bf16[192,2048]{1,0:T(8,128)(2,1)}, bf16[192,2048]{1,0:T(8,128)(2,1)}, u32[]{:S(2)}, u32[]{:S(2)}) collective-permute-start(bf16[192,2048]{1,0:T(8,128)(2,1)} %get-tuple-element.93), channel_id=1, source_target_pairs={{0,4},{4,0},{8,12},{12,8},{16,20},{20,16},{24,28},{28,24},{1,5},{5... | collective-permute-start | bytes 2359304 | tf_op jit(solution)/shard_map/ppermute | solution.py:248
  6.7 1.6 collective-permute-start.1
  9.0 6.7 %encode.3 = (bf16[192,2048]{1,0:T(8,128)(2,1)}, bf16[192,2048]{1,0:T(8,128)(2,1)}, bf16[192,2048]{1,0:T(8,128)(2,1)}, f32[4,1,2048]{2,1,0:T(1,128)}) custom-call(f32[384]{0:T(512)} %g_ref.1, f32[384,2048]{1,0:T(8,128)} %wu_ref.1, f32[384,2048]{1,0:T(8,128)} %au_ref.1, f32[384,2048]{1,0:T(8,128)} %wg_ref.1, f32[384,2048]{1,0:T(8,128)} %ag_ref.1, ...), custom_call_target="tpu_custom_call" | custom-call | tf_op jit(solution)/shard_map/encode/pallas_call | solution.py:61
  16.5 5.6 %collective-permute-start.3 = (f32[4,1,2048]{2,1,0:T(1,128)}, f32[4,1,2048]{2,1,0:T(1,128)S(1)}, u32[]{:S(2)}, u32[]{:S(2)}) collective-permute-start(f32[4,1,2048]{2,1,0:T(1,128)} %get-tuple-element.94.refs_0_), channel_id=1, source_target_pairs={{0,8},{4,12},{8,0},{12,4},{16,24},{20,28},{24,16},{28,20},{1,9},{5... | collective-permute-start | bytes 98312 | tf_op jit(solution)/shard_map/ppermute | solution.py:246
  22.1 4.5 %collective-permute-done.3.refs_1_ = f32[4,1,2048]{2,1,0:T(1,128)S(1)} collective-permute-done((f32[4,1,2048]{2,1,0:T(1,128)}, f32[4,1,2048]{2,1,0:T(1,128)S(1)}, u32[]{:S(2)}, u32[]{:S(2)}) %collective-permute-start.3) | collective-permute-done | bytes 32800 | tf_op jit(solution)/shard_map/ppermute | solution.py:246
  27.1 1.7 collective-permute-start.9
  28.8 1.6 collective-permute-start.5
  30.3 2.2 collective-permute-start.4
  34.0 13.4 %collective-permute-done.8.y_ref = bf16[192,2048]{1,0:T(8,128)(2,1)} collective-permute-done((bf16[192,2048]{1,0:T(8,128)(2,1)}, bf16[192,2048]{1,0:T(8,128)(2,1)}, u32[]{:S(2)}, u32[]{:S(2)}) %collective-permute-start.8) | collective-permute-done | bytes 786464 | tf_op jit(solution)/shard_map/ppermute | solution.py:248
  47.4 4.3 %collective-permute-start.7 = (f32[8,1,2048]{2,1,0:T(1,128)S(1)}, f32[8,1,2048]{2,1,0:T(1,128)S(1)}, u32[]{:S(2)}, u32[]{:S(2)}) collective-permute-start(f32[8,1,2048]{2,1,0:T(1,128)S(1)} %pad_maximum_fusion.1), channel_id=1, source_target_pairs={{0,16},{4,20},{16,0},{20,4},{8,24},{12,28},{24,8},{28,12},{1,17},{... | collective-permute-start | bytes 196616 | tf_op jit(solution)/shard_map/ppermute | solution.py:246
  51.7 18.3 %collective-permute-done.7.refs_2_ = f32[8,1,2048]{2,1,0:T(1,128)S(1)} collective-permute-done((f32[8,1,2048]{2,1,0:T(1,128)S(1)}, f32[8,1,2048]{2,1,0:T(1,128)S(1)}, u32[]{:S(2)}, u32[]{:S(2)}) %collective-permute-start.7) | collective-permute-done | bytes 65568 | tf_op jit(solution)/shard_map/ppermute | solution.py:246
  71.4 1.6 collective-permute-start.11
  73.0 17.2 %collective-permute-done.11.refs_3_ = f32[16,1,2048]{2,1,0:T(1,128)S(1)} collective-permute-done((f32[16,1,2048]{2,1,0:T(1,128)S(1)}, f32[16,1,2048]{2,1,0:T(1,128)S(1)}, u32[]{:S(2)}, u32[]{:S(2)}) %collective-permute-start.11) | collective-permute-done | bytes 131104 | tf_op jit(solution)/shard_map/ppermute | solution.py:248
  90.1 1.5 collective-permute-start.22
  93.6 1.5 collective-permute-start.14
  95.1 1.8 ratios.1
  96.9 7.2 %own_share.1 = (bf16[3072,2048]{1,0:T(8,128)(2,1)}, bf16[3072,2048]{1,0:T(8,128)(2,1)}, f32[8,128]{1,0:T(8,128)}) custom-call(s32[1]{0:T(128)} %bitcast.me_ref, f32[384,2048]{1,0:T(8,128)} %wg_ref.1, f32[384,2048]{1,0:T(8,128)} %ag_ref.1, f32[384,2048]{1,0:T(8,128)} %wu_ref.1, f32[384,2048]{1,0:T(8,128)} %au_ref.1, f32[384]{0:T(512)} %g_ref.1, ...), custom_call_target="tpu_custom_call" | custom-call | tf_op jit(solution)/shard_map/own_share/pallas_call | solution.py:84
  104.1 6.7 %collective-permute-done.19.y_ref = bf16[192,2048]{1,0:T(8,128)(2,1)} collective-permute-done((bf16[192,2048]{1,0:T(8,128)(2,1)}, bf16[192,2048]{1,0:T(8,128)(2,1)}, u32[]{:S(2)}, u32[]{:S(2)}) %collective-permute-start.19) | collective-permute-done | bytes 786464 | tf_op jit(solution)/shard_map/ppermute | solution.py:246
  112.1 1.5 collective-permute-start.25
  113.7 13.9 %collective-permute-done.13 = bf16[192,2048]{1,0:T(8,128)(2,1)S(1)} collective-permute-done((bf16[192,2048]{1,0:T(8,128)(2,1)S(1)}, bf16[192,2048]{1,0:T(8,128)(2,1)S(1)}, u32[]{:S(2)}, u32[]{:S(2)}) %collective-permute-start.13) | collective-permute-done | bytes 786464 | tf_op jit(solution)/shard_map/ppermute | solution.py:246
  128.1 2.2 decode.26
  130.3 2.2 decode.27
  132.6 2.2 decode.28
  136.0 1.6 collective-permute-start.17
  137.6 2.2 decode.29
  139.8 2.2 decode.32
  142.0 2.2 decode.33
  145.5 1.6 collective-permute-start.15
  147.8 1.5 collective-permute-start.30
  151.8 10.5 %collective-permute-done.17.y_ref = bf16[192,2048]{1,0:T(8,128)(2,1)} collective-permute-done((bf16[192,2048]{1,0:T(8,128)(2,1)S(1)}, bf16[192,2048]{1,0:T(8,128)(2,1)}, u32[]{:S(2)}, u32[]{:S(2)}) %collective-permute-start.17) | collective-permute-done | bytes 786464 | tf_op jit(solution)/shard_map/ppermute | solution.py:248
  162.9 2.2 decode.30
  165.1 2.2 decode.31
  167.3 2.2 decode.34
  169.6 2.2 decode.35
  171.8 2.2 decode.38
  174.0 2.2 decode.39
  178.8 1.6 collective-permute-start.20
  180.3 2.2 decode.36
  186.6 2.2 decode.37
  188.8 2.2 decode.40
  191.0 7.8 %collective-permute-done.21 = bf16[192,2048]{1,0:T(8,128)(2,1)} collective-permute-done((bf16[192,2048]{1,0:T(8,128)(2,1)}, bf16[192,2048]{1,0:T(8,128)(2,1)}, u32[]{:S(2)}, u32[]{:S(2)}) %collective-permute-start.21) | collective-permute-done | bytes 786464 | tf_op jit(solution)/shard_map/ppermute | solution.py:246
  200.1 1.6 collective-permute-start.28
  202.9 2.2 decode.41
  205.2 2.2 decode.44
  207.4 2.2 decode.45
  209.6 6.0 %collective-permute-done.32 = bf16[192,2048]{1,0:T(8,128)(2,1)S(1)} collective-permute-done((bf16[192,2048]{1,0:T(8,128)(2,1)}, bf16[192,2048]{1,0:T(8,128)(2,1)S(1)}, u32[]{:S(2)}, u32[]{:S(2)}) %collective-permute-start.32) | collective-permute-done | bytes 786464 | tf_op jit(solution)/shard_map/ppermute | solution.py:246
  216.2 1.5 collective-permute-start.36
  217.8 1.6 collective-permute-start.35
  219.3 2.2 decode.42
  221.6 2.2 decode.43
  223.8 9.3 %collective-permute-done.28.y_ref = bf16[192,2048]{1,0:T(8,128)(2,1)} collective-permute-done((bf16[192,2048]{1,0:T(8,128)(2,1)S(1)}, bf16[192,2048]{1,0:T(8,128)(2,1)}, u32[]{:S(2)}, u32[]{:S(2)}) %collective-permute-start.28) | collective-permute-done | bytes 786464 | tf_op jit(solution)/shard_map/ppermute | solution.py:248
  233.1 2.4 collective-permute-start.34
  235.5 2.2 decode.46
  238.7 2.3 decode.47
  241.9 7.5 %collective-permute-done.36 = bf16[192,2048]{1,0:T(8,128)(2,1)} collective-permute-done((bf16[192,2048]{1,0:T(8,128)(2,1)}, bf16[192,2048]{1,0:T(8,128)(2,1)}, u32[]{:S(2)}, u32[]{:S(2)}) %collective-permute-start.36) | collective-permute-done | bytes 786464 | tf_op jit(solution)/shard_map/ppermute | solution.py:246
  250.6 1.6 collective-permute-start.38
  253.9 2.2 decode.50
  256.1 2.2 decode.51
  258.4 7.9 %collective-permute-done.34.y_ref = bf16[192,2048]{1,0:T(8,128)(2,1)} collective-permute-done((bf16[192,2048]{1,0:T(8,128)(2,1)}, bf16[192,2048]{1,0:T(8,128)(2,1)}, u32[]{:S(2)}, u32[]{:S(2)}) %collective-permute-start.34) | collective-permute-done | bytes 786464 | tf_op jit(solution)/shard_map/ppermute | solution.py:246
  266.3 2.2 decode.48
  268.5 2.2 decode.49
  270.7 4.8 %collective-permute-done.38.y1_ref = bf16[192,2048]{1,0:T(8,128)(2,1)S(1)} collective-permute-done((bf16[192,2048]{1,0:T(8,128)(2,1)S(1)}, bf16[192,2048]{1,0:T(8,128)(2,1)S(1)}, u32[]{:S(2)}, u32[]{:S(2)}) %collective-permute-start.38) | collective-permute-done | bytes 786464 | tf_op jit(solution)/shard_map/ppermute | solution.py:248
  276.7 3.0 %decode_last.1 = bf16[3072,2048]{1,0:T(8,128)(2,1)} custom-call(s32[1]{0:T(128)} %bitcast.me_ref, bf16[192,2048]{1,0:T(8,128)(2,1)} %copy-done.9, bf16[192,2048]{1,0:T(8,128)(2,1)} %copy-done.8, f32[32,1,2048]{2,1,0:T(1,128)} %get-tuple-element.102.r_ref.r0_ref.r1_ref, ...), custom_call_target="tpu_custom_call", output_to_operand_aliasing={{}: (5, {})} | custom-call | tf_op jit(solution)/shard_map/decode_last/pallas_call | solution.py:188
  (92 shorter events, 30.5 us)
Async XLA Ops:
  3.8 23.3 %collective-permute-start = (bf16[192,2048]{1,0:T(8,128)(2,1)}, bf16[192,2048]{1,0:T(8,128)(2,1)}, u32[]{:S(2)}, u32[]{:S(2)}) collective-permute-start(bf16[192,2048]{1,0:T(8,128)(2,1)} %get-tuple-element.93), channel_id=1, source_target_pairs={{0,4},{4,0},{8,12},{12,8},{16,20},{20,16},{24,28},{28,24},{1,5},{5... | collective-permute-start | bytes 2359304 | tf_op jit(solution)/shard_map/ppermute | solution.py:248
  6.7 22.0 %collective-permute-start.1 = (bf16[192,2048]{1,0:T(8,128)(2,1)}, bf16[192,2048]{1,0:T(8,128)(2,1)S(1)}, u32[]{:S(2)}, u32[]{:S(2)}) collective-permute-start(bf16[192,2048]{1,0:T(8,128)(2,1)} %get-tuple-element.93), channel_id=1, source_target_pairs={{0,8},{4,12},{8,0},{12,4},{16,24},{20,28},{24,16},{28,20},{1,9},{5... | collective-permute-start | bytes 2359304 | tf_op jit(solution)/shard_map/ppermute | solution.py:246
  8.3 20.5 %collective-permute-start.2 = (bf16[192,2048]{1,0:T(8,128)(2,1)}, bf16[192,2048]{1,0:T(8,128)(2,1)S(1)}, u32[]{:S(2)}, u32[]{:S(2)}) collective-permute-start(bf16[192,2048]{1,0:T(8,128)(2,1)} %get-tuple-element.93), channel_id=1, source_target_pairs={{8,16},{12,20},{16,8},{20,12},{9,17},{13,21},{17,9},{21,13},{10,18... | collective-permute-start | bytes 2359304 | tf_op jit(solution)/shard_map/ppermute | solution.py:246
  15.8 16.7 %collective-permute-start.10 = (bf16[192,2048]{1,0:T(8,128)(2,1)}, bf16[192,2048]{1,0:T(8,128)(2,1)S(1)}, u32[]{:S(2)}, u32[]{:S(2)}) collective-permute-start(bf16[192,2048]{1,0:T(8,128)(2,1)} %get-tuple-element.97), channel_id=1, source_target_pairs={{8,16},{12,20},{16,8},{20,12},{9,17},{13,21},{17,9},{21,13},{10,18... | collective-permute-start | bytes 2359304 | tf_op jit(solution)/shard_map/ppermute | solution.py:246
  16.5 10.2 %collective-permute-start.3 = (f32[4,1,2048]{2,1,0:T(1,128)}, f32[4,1,2048]{2,1,0:T(1,128)S(1)}, u32[]{:S(2)}, u32[]{:S(2)}) collective-permute-start(f32[4,1,2048]{2,1,0:T(1,128)} %get-tuple-element.94.refs_0_), channel_id=1, source_target_pairs={{0,8},{4,12},{8,0},{12,4},{16,24},{20,28},{24,16},{28,20},{1,9},{5... | collective-permute-start | bytes 98312 | tf_op jit(solution)/shard_map/ppermute | solution.py:246
  26.7 68.5 %copy-start.14 = (f32[4,1,2048]{2,1,0:T(1,128)}, f32[4,1,2048]{2,1,0:T(1,128)S(1)}, u32[]{:S(2)}) copy-start(f32[4,1,2048]{2,1,0:T(1,128)S(1)} %collective-permute-done.3.refs_1_) | copy-start | bytes 98308
  26.7 20.7 %collective-permute-start.8 = (bf16[192,2048]{1,0:T(8,128)(2,1)}, bf16[192,2048]{1,0:T(8,128)(2,1)}, u32[]{:S(2)}, u32[]{:S(2)}) collective-permute-start(bf16[192,2048]{1,0:T(8,128)(2,1)} %get-tuple-element.97), channel_id=1, source_target_pairs={{0,4},{4,0},{8,12},{12,8},{16,20},{20,16},{24,28},{28,24},{1,5},{5... | collective-permute-start | bytes 2359304 | tf_op jit(solution)/shard_map/ppermute | solution.py:248
  27.1 24.6 %collective-permute-start.9 = (bf16[192,2048]{1,0:T(8,128)(2,1)}, bf16[192,2048]{1,0:T(8,128)(2,1)}, u32[]{:S(2)}, u32[]{:S(2)}) collective-permute-start(bf16[192,2048]{1,0:T(8,128)(2,1)} %get-tuple-element.97), channel_id=1, source_target_pairs={{0,8},{4,12},{8,0},{12,4},{16,24},{20,28},{24,16},{28,20},{1,9},{5... | collective-permute-start | bytes 2359304 | tf_op jit(solution)/shard_map/ppermute | solution.py:246
  28.8 3.7 %copy-start.11 = (bf16[192,2048]{1,0:T(8,128)(2,1)}, bf16[192,2048]{1,0:T(8,128)(2,1)S(1)}, u32[]{:S(2)}) copy-start(bf16[192,2048]{1,0:T(8,128)(2,1)S(1)} %collective-permute-done.1.y_ref) | copy-start | bytes 2359300
  28.8 61.3 %collective-permute-start.5 = (bf16[192,2048]{1,0:T(8,128)(2,1)}, bf16[192,2048]{1,0:T(8,128)(2,1)S(1)}, u32[]{:S(2)}, u32[]{:S(2)}) collective-permute-start(bf16[192,2048]{1,0:T(8,128)(2,1)} %get-tuple-element.95), channel_id=1, source_target_pairs={{0,4},{4,0},{8,12},{12,8},{16,20},{20,16},{24,28},{28,24},{1,5},{5... | collective-permute-start | bytes 2359304 | tf_op jit(solution)/shard_map/ppermute | solution.py:248
  30.3 61.3 %collective-permute-start.4 = (bf16[192,2048]{1,0:T(8,128)(2,1)}, bf16[192,2048]{1,0:T(8,128)(2,1)}, u32[]{:S(2)}, u32[]{:S(2)}) collective-permute-start(bf16[192,2048]{1,0:T(8,128)(2,1)} %get-tuple-element.95), channel_id=1, source_target_pairs={{0,8},{4,12},{8,0},{12,4},{16,24},{20,28},{24,16},{28,20},{1,9},{5... | collective-permute-start | bytes 2359304 | tf_op jit(solution)/shard_map/ppermute | solution.py:246
  32.5 59.2 %collective-permute-start.6 = (bf16[192,2048]{1,0:T(8,128)(2,1)}, bf16[192,2048]{1,0:T(8,128)(2,1)S(1)}, u32[]{:S(2)}, u32[]{:S(2)}) collective-permute-start(bf16[192,2048]{1,0:T(8,128)(2,1)} %get-tuple-element.95), channel_id=1, source_target_pairs={{8,16},{12,20},{16,8},{20,12},{9,17},{13,21},{17,9},{21,13},{10,18... | collective-permute-start | bytes 2359304 | tf_op jit(solution)/shard_map/ppermute | solution.py:246
  47.4 22.6 %collective-permute-start.7 = (f32[8,1,2048]{2,1,0:T(1,128)S(1)}, f32[8,1,2048]{2,1,0:T(1,128)S(1)}, u32[]{:S(2)}, u32[]{:S(2)}) collective-permute-start(f32[8,1,2048]{2,1,0:T(1,128)S(1)} %pad_maximum_fusion.1), channel_id=1, source_target_pairs={{0,16},{4,20},{16,0},{20,4},{8,24},{12,28},{24,8},{28,12},{1,17},{... | collective-permute-start | bytes 196616 | tf_op jit(solution)/shard_map/ppermute | solution.py:246
  70.0 25.1 %copy-start.15 = (f32[8,1,2048]{2,1,0:T(1,128)}, f32[8,1,2048]{2,1,0:T(1,128)S(1)}, u32[]{:S(2)}) copy-start(f32[8,1,2048]{2,1,0:T(1,128)S(1)} %collective-permute-done.7.refs_2_) | copy-start | bytes 196612
  70.0 23.6 %collective-permute-start.18 = (bf16[192,2048]{1,0:T(8,128)(2,1)}, bf16[192,2048]{1,0:T(8,128)(2,1)}, u32[]{:S(2)}, u32[]{:S(2)}) collective-permute-start(bf16[192,2048]{1,0:T(8,128)(2,1)} %get-tuple-element.114), channel_id=1, source_target_pairs={{0,4},{4,0},{8,12},{12,8},{16,20},{20,16},{24,28},{28,24},{1,5},{5... | collective-permute-start | bytes 2359304 | tf_op jit(solution)/shard_map/ppermute | solution.py:248
  71.4 18.7 %collective-permute-start.11 = (f32[16,1,2048]{2,1,0:T(1,128)S(1)}, f32[16,1,2048]{2,1,0:T(1,128)S(1)}, u32[]{:S(2)}, u32[]{:S(2)}) collective-permute-start(f32[16,1,2048]{2,1,0:T(1,128)S(1)} %pad_maximum_fusion), channel_id=1, source_target_pairs={{0,4},{4,0},{8,12},{12,8},{16,20},{20,16},{24,28},{28,24},{1,5},{5... | collective-permute-start | bytes 393224 | tf_op jit(solution)/shard_map/ppermute | solution.py:248
  90.1 5.0 %copy-start.16 = (f32[16,1,2048]{2,1,0:T(1,128)}, f32[16,1,2048]{2,1,0:T(1,128)S(1)}, u32[]{:S(2)}) copy-start(f32[16,1,2048]{2,1,0:T(1,128)S(1)} %collective-permute-done.11.refs_3_) | copy-start | bytes 393220
  90.1 20.7 %collective-permute-start.19 = (bf16[192,2048]{1,0:T(8,128)(2,1)}, bf16[192,2048]{1,0:T(8,128)(2,1)}, u32[]{:S(2)}, u32[]{:S(2)}) collective-permute-start(bf16[192,2048]{1,0:T(8,128)(2,1)} %get-tuple-element.114), channel_id=1, source_target_pairs={{0,8},{4,12},{8,0},{12,4},{16,24},{20,28},{24,16},{28,20},{1,9},{5... | collective-permute-start | bytes 2359304 | tf_op jit(solution)/shard_map/ppermute | solution.py:246
  90.1 1.6 copy-start.12
  90.1 20.7 %collective-permute-start.22 = (bf16[192,2048]{1,0:T(8,128)(2,1)}, bf16[192,2048]{1,0:T(8,128)(2,1)}, u32[]{:S(2)}, u32[]{:S(2)}) collective-permute-start(bf16[192,2048]{1,0:T(8,128)(2,1)} %get-tuple-element.114), channel_id=1, source_target_pairs={{8,16},{12,20},{16,8},{20,12},{9,17},{13,21},{17,9},{21,13},{10,18... | collective-permute-start | bytes 2359304 | tf_op jit(solution)/shard_map/ppermute | solution.py:246
  91.7 35.9 %collective-permute-start.13 = (bf16[192,2048]{1,0:T(8,128)(2,1)S(1)}, bf16[192,2048]{1,0:T(8,128)(2,1)S(1)}, u32[]{:S(2)}, u32[]{:S(2)}) collective-permute-start(bf16[192,2048]{1,0:T(8,128)(2,1)S(1)} %collective-permute-done.2), channel_id=1, source_target_pairs={{8,0},{12,4},{16,24},{20,28},{9,1},{13,5},{17,25},{21,29},{10,2},{... | collective-permute-start | bytes 2359304 | tf_op jit(solution)/shard_map/ppermute | solution.py:246
  93.0 43.0 %collective-permute-start.12 = (bf16[192,2048]{1,0:T(8,128)(2,1)}, bf16[192,2048]{1,0:T(8,128)(2,1)}, u32[]{:S(2)}, u32[]{:S(2)}) collective-permute-start(bf16[192,2048]{1,0:T(8,128)(2,1)} %collective-permute-done.4.y_ref), channel_id=1, source_target_pairs={{0,4},{4,0},{8,12},{12,8},{16,20},{20,16},{24,28},{28,24},{1,5},{5... | collective-permute-start | bytes 2359304 | tf_op jit(solution)/shard_map/ppermute | solution.py:248
  93.6 42.4 %collective-permute-start.14 = (bf16[192,2048]{1,0:T(8,128)(2,1)}, bf16[192,2048]{1,0:T(8,128)(2,1)}, u32[]{:S(2)}, u32[]{:S(2)}) collective-permute-start(bf16[192,2048]{1,0:T(8,128)(2,1)} %copy-done.11), channel_id=1, source_target_pairs={{8,16},{12,20},{16,8},{20,12},{9,17},{13,21},{17,9},{21,13},{10,18... | collective-permute-start | bytes 2359304 | tf_op jit(solution)/shard_map/ppermute | solution.py:246
  110.9 34.7 %collective-permute-start.23 = (bf16[192,2048]{1,0:T(8,128)(2,1)S(1)}, bf16[192,2048]{1,0:T(8,128)(2,1)}, u32[]{:S(2)}, u32[]{:S(2)}) collective-permute-start(bf16[192,2048]{1,0:T(8,128)(2,1)S(1)} %collective-permute-done.10), channel_id=1, source_target_pairs={{8,0},{12,4},{16,24},{20,28},{9,1},{13,5},{17,25},{21,29},{10,2},{... | collective-permute-start | bytes 2359304 | tf_op jit(solution)/shard_map/ppermute | solution.py:246
  112.1 35.0 %collective-permute-start.25 = (bf16[192,2048]{1,0:T(8,128)(2,1)}, bf16[192,2048]{1,0:T(8,128)(2,1)}, u32[]{:S(2)}, u32[]{:S(2)}) collective-permute-start(bf16[192,2048]{1,0:T(8,128)(2,1)} %collective-permute-done.9.y_ref), channel_id=1, source_target_pairs={{8,16},{12,20},{16,8},{20,12},{9,17},{13,21},{17,9},{21,13},{10,18... | collective-permute-start | bytes 2359304 | tf_op jit(solution)/shard_map/ppermute | solution.py:246
  127.6 5.0 %copy-start.10 = (bf16[192,2048]{1,0:T(8,128)(2,1)}, bf16[192,2048]{1,0:T(8,128)(2,1)S(1)}, u32[]{:S(2)}) copy-start(bf16[192,2048]{1,0:T(8,128)(2,1)S(1)} %collective-permute-done.13) | copy-start | bytes 2359300
  127.6 20.2 %collective-permute-start.24 = (bf16[192,2048]{1,0:T(8,128)(2,1)}, bf16[192,2048]{1,0:T(8,128)(2,1)}, u32[]{:S(2)}, u32[]{:S(2)}) collective-permute-start(bf16[192,2048]{1,0:T(8,128)(2,1)} %collective-permute-done.19.y_ref), channel_id=1, source_target_pairs={{0,4},{4,0},{8,12},{12,8},{16,20},{20,16},{24,28},{28,24},{1,5},{5... | collective-permute-start | bytes 2359304 | tf_op jit(solution)/shard_map/ppermute | solution.py:248
  136.0 6.0 %copy-start = (bf16[192,2048]{1,0:T(8,128)(2,1)}, bf16[192,2048]{1,0:T(8,128)(2,1)S(1)}, u32[]{:S(2)}) copy-start(bf16[192,2048]{1,0:T(8,128)(2,1)S(1)} %broadcast_select_fusion.6.y_ref) | copy-start | bytes 2359300
  136.0 26.3 %collective-permute-start.17 = (bf16[192,2048]{1,0:T(8,128)(2,1)S(1)}, bf16[192,2048]{1,0:T(8,128)(2,1)}, u32[]{:S(2)}, u32[]{:S(2)}) collective-permute-start(bf16[192,2048]{1,0:T(8,128)(2,1)S(1)} %broadcast_select_fusion.6.y_ref), channel_id=1, source_target_pairs={{0,4},{4,0},{8,12},{12,8},{16,20},{20,16},{24,28},{28,24},{1,5},{5... | collective-permute-start | bytes 2359304 | tf_op jit(solution)/shard_map/ppermute | solution.py:248
  144.2 32.0 %collective-permute-start.16 = (bf16[192,2048]{1,0:T(8,128)(2,1)S(1)}, bf16[192,2048]{1,0:T(8,128)(2,1)}, u32[]{:S(2)}, u32[]{:S(2)}) collective-permute-start(bf16[192,2048]{1,0:T(8,128)(2,1)S(1)} %collective-permute-done.6), channel_id=1, source_target_pairs={{8,0},{12,4},{16,24},{20,28},{9,1},{13,5},{17,25},{21,29},{10,2},{... | collective-permute-start | bytes 2359304 | tf_op jit(solution)/shard_map/ppermute | solution.py:246
  145.5 30.7 %collective-permute-start.15 = (bf16[192,2048]{1,0:T(8,128)(2,1)}, bf16[192,2048]{1,0:T(8,128)(2,1)}, u32[]{:S(2)}, u32[]{:S(2)}) collective-permute-start(bf16[192,2048]{1,0:T(8,128)(2,1)} %collective-permute-done.4.y_ref), channel_id=1, source_target_pairs={{8,16},{12,20},{16,8},{20,12},{9,17},{13,21},{17,9},{21,13},{10,18... | collective-permute-start | bytes 2359304 | tf_op jit(solution)/shard_map/ppermute | solution.py:246
  147.8 34.8 %collective-permute-start.30 = (bf16[192,2048]{1,0:T(8,128)(2,1)}, bf16[192,2048]{1,0:T(8,128)(2,1)}, u32[]{:S(2)}, u32[]{:S(2)}) collective-permute-start(bf16[192,2048]{1,0:T(8,128)(2,1)} %collective-permute-done.19.y_ref), channel_id=1, source_target_pairs={{8,16},{12,20},{16,8},{20,12},{9,17},{13,21},{17,9},{21,13},{10,18... | collective-permute-start | bytes 2359304 | tf_op jit(solution)/shard_map/ppermute | solution.py:246
  149.3 33.2 %collective-permute-start.29 = (bf16[192,2048]{1,0:T(8,128)(2,1)}, bf16[192,2048]{1,0:T(8,128)(2,1)}, u32[]{:S(2)}, u32[]{:S(2)}) collective-permute-start(bf16[192,2048]{1,0:T(8,128)(2,1)} %collective-permute-done.22), channel_id=1, source_target_pairs={{8,0},{12,4},{16,24},{20,28},{9,1},{13,5},{17,25},{21,29},{10,2},{... | collective-permute-start | bytes 2359304 | tf_op jit(solution)/shard_map/ppermute | solution.py:246
  151.8 15.5 %copy-start.1 = (bf16[192,2048]{1,0:T(8,128)(2,1)}, bf16[192,2048]{1,0:T(8,128)(2,1)S(1)}, u32[]{:S(2)}) copy-start(bf16[192,2048]{1,0:T(8,128)(2,1)S(1)} %broadcast_select_fusion.5.y_ref) | copy-start | bytes 2359300
  162.4 20.2 %collective-permute-start.26 = (bf16[192,2048]{1,0:T(8,128)(2,1)S(1)}, bf16[192,2048]{1,0:T(8,128)(2,1)S(1)}, u32[]{:S(2)}, u32[]{:S(2)}) collective-permute-start(bf16[192,2048]{1,0:T(8,128)(2,1)S(1)} %broadcast_select_fusion.5.y_ref), channel_id=1, source_target_pairs={{0,4},{4,0},{8,12},{12,8},{16,20},{20,16},{24,28},{28,24},{1,5},{5... | collective-permute-start | bytes 2359304 | tf_op jit(solution)/shard_map/ppermute | solution.py:248
  176.2 22.6 %collective-permute-start.21 = (bf16[192,2048]{1,0:T(8,128)(2,1)}, bf16[192,2048]{1,0:T(8,128)(2,1)}, u32[]{:S(2)}, u32[]{:S(2)}) collective-permute-start(bf16[192,2048]{1,0:T(8,128)(2,1)} %collective-permute-done.14), channel_id=1, source_target_pairs={{8,0},{12,4},{16,24},{20,28},{9,1},{13,5},{17,25},{21,29},{10,2},{... | collective-permute-start | bytes 2359304 | tf_op jit(solution)/shard_map/ppermute | solution.py:246
  178.7 7.8 %copy-start.6 = (bf16[192,2048]{1,0:T(8,128)(2,1)}, bf16[192,2048]{1,0:T(8,128)(2,1)S(1)}, u32[]{:S(2)}) copy-start(bf16[192,2048]{1,0:T(8,128)(2,1)S(1)} %broadcast_select_fusion.7.y_ref) | copy-start | bytes 2359300
  178.8 21.3 %collective-permute-start.20 = (bf16[192,2048]{1,0:T(8,128)(2,1)S(1)}, bf16[192,2048]{1,0:T(8,128)(2,1)}, u32[]{:S(2)}, u32[]{:S(2)}) collective-permute-start(bf16[192,2048]{1,0:T(8,128)(2,1)S(1)} %broadcast_select_fusion.7.y_ref), channel_id=1, source_target_pairs={{0,4},{4,0},{8,12},{12,8},{16,20},{20,16},{24,28},{28,24},{1,5},{5... | collective-permute-start | bytes 2359304 | tf_op jit(solution)/shard_map/ppermute | solution.py:248
  182.6 0.9 copy-start.13
  183.5 32.1 %collective-permute-start.32 = (bf16[192,2048]{1,0:T(8,128)(2,1)}, bf16[192,2048]{1,0:T(8,128)(2,1)S(1)}, u32[]{:S(2)}, u32[]{:S(2)}) collective-permute-start(bf16[192,2048]{1,0:T(8,128)(2,1)} %collective-permute-done.25), channel_id=1, source_target_pairs={{8,0},{12,4},{16,24},{20,28},{9,1},{13,5},{17,25},{21,29},{10,2},{... | collective-permute-start | bytes 2359304 | tf_op jit(solution)/shard_map/ppermute | solution.py:246
  186.0 5.1 %copy-start.3 = (bf16[192,2048]{1,0:T(8,128)(2,1)}, bf16[192,2048]{1,0:T(8,128)(2,1)S(1)}, u32[]{:S(2)}) copy-start(bf16[192,2048]{1,0:T(8,128)(2,1)S(1)} %broadcast_select_fusion.2.y_ref) | copy-start | bytes 2359300
  186.0 30.2 %collective-permute-start.31 = (bf16[192,2048]{1,0:T(8,128)(2,1)S(1)}, bf16[192,2048]{1,0:T(8,128)(2,1)}, u32[]{:S(2)}, u32[]{:S(2)}) collective-permute-start(bf16[192,2048]{1,0:T(8,128)(2,1)S(1)} %broadcast_select_fusion.2.y_ref), channel_id=1, source_target_pairs={{0,4},{4,0},{8,12},{12,8},{16,20},{20,16},{24,28},{28,24},{1,5},{5... | collective-permute-start | bytes 2359304 | tf_op jit(solution)/shard_map/ppermute | solution.py:248
  200.1 7.3 %copy-start.2 = (bf16[192,2048]{1,0:T(8,128)(2,1)}, bf16[192,2048]{1,0:T(8,128)(2,1)S(1)}, u32[]{:S(2)}) copy-start(bf16[192,2048]{1,0:T(8,128)(2,1)S(1)} %broadcast_select_fusion.3.y_ref) | copy-start | bytes 2359300
  200.1 33.0 %collective-permute-start.28 = (bf16[192,2048]{1,0:T(8,128)(2,1)S(1)}, bf16[192,2048]{1,0:T(8,128)(2,1)}, u32[]{:S(2)}, u32[]{:S(2)}) collective-permute-start(bf16[192,2048]{1,0:T(8,128)(2,1)S(1)} %broadcast_select_fusion.3.y_ref), channel_id=1, source_target_pairs={{0,4},{4,0},{8,12},{12,8},{16,20},{20,16},{24,28},{28,24},{1,5},{5... | collective-permute-start | bytes 2359304 | tf_op jit(solution)/shard_map/ppermute | solution.py:248
  201.6 31.4 %collective-permute-start.27 = (bf16[192,2048]{1,0:T(8,128)(2,1)}, bf16[192,2048]{1,0:T(8,128)(2,1)S(1)}, u32[]{:S(2)}, u32[]{:S(2)}) collective-permute-start(bf16[192,2048]{1,0:T(8,128)(2,1)} %collective-permute-done.15), channel_id=1, source_target_pairs={{8,0},{12,4},{16,24},{20,28},{9,1},{13,5},{17,25},{21,29},{10,2},{... | collective-permute-start | bytes 2359304 | tf_op jit(solution)/shard_map/ppermute | solution.py:246
  216.2 33.2 %collective-permute-start.36 = (bf16[192,2048]{1,0:T(8,128)(2,1)}, bf16[192,2048]{1,0:T(8,128)(2,1)}, u32[]{:S(2)}, u32[]{:S(2)}) collective-permute-start(bf16[192,2048]{1,0:T(8,128)(2,1)} %collective-permute-done.30), channel_id=1, source_target_pairs={{8,0},{12,4},{16,24},{20,28},{9,1},{13,5},{17,25},{21,29},{10,2},{... | collective-permute-start | bytes 2359304 | tf_op jit(solution)/shard_map/ppermute | solution.py:246
  217.8 3.8 %copy-start.5 = (bf16[192,2048]{1,0:T(8,128)(2,1)}, bf16[192,2048]{1,0:T(8,128)(2,1)S(1)}, u32[]{:S(2)}) copy-start(bf16[192,2048]{1,0:T(8,128)(2,1)S(1)} %broadcast_select_fusion.1.y_ref) | copy-start | bytes 2359300
  217.8 32.9 %collective-permute-start.35 = (bf16[192,2048]{1,0:T(8,128)(2,1)S(1)}, bf16[192,2048]{1,0:T(8,128)(2,1)}, u32[]{:S(2)}, u32[]{:S(2)}) collective-permute-start(bf16[192,2048]{1,0:T(8,128)(2,1)S(1)} %broadcast_select_fusion.1.y_ref), channel_id=1, source_target_pairs={{0,4},{4,0},{8,12},{12,8},{16,20},{20,16},{24,28},{28,24},{1,5},{5... | collective-permute-start | bytes 2359304 | tf_op jit(solution)/shard_map/ppermute | solution.py:248
  233.1 33.2 %collective-permute-start.34 = (bf16[192,2048]{1,0:T(8,128)(2,1)}, bf16[192,2048]{1,0:T(8,128)(2,1)}, u32[]{:S(2)}, u32[]{:S(2)}) collective-permute-start(bf16[192,2048]{1,0:T(8,128)(2,1)} %collective-permute-done.y_ref), channel_id=1, source_target_pairs={{0,8},{4,12},{8,0},{12,4},{16,24},{20,28},{24,16},{28,20},{1,9},{5... | collective-permute-start | bytes 2359304 | tf_op jit(solution)/shard_map/ppermute | solution.py:246
  237.7 15.6 %copy-start.17 = (f32[2,2048]{1,0:T(2,128)S(1)}, f32[2,2048]{1,0:T(2,128)}, u32[]{:S(2)}) copy-start(f32[2,2048]{1,0:T(2,128)} %get-tuple-element.103.f_ref) | copy-start | bytes 49156
  238.7 2.3 copy-start.4
  241.0 27.5 %collective-permute-start.33 = (bf16[192,2048]{1,0:T(8,128)(2,1)S(1)}, bf16[192,2048]{1,0:T(8,128)(2,1)}, u32[]{:S(2)}, u32[]{:S(2)}) collective-permute-start(bf16[192,2048]{1,0:T(8,128)(2,1)S(1)} %copy-done.4), channel_id=1, source_target_pairs={{0,4},{4,0},{8,12},{12,8},{16,20},{20,16},{24,28},{28,24},{1,5},{5... | collective-permute-start | bytes 2359304 | tf_op jit(solution)/shard_map/ppermute | solution.py:248
  250.6 5.5 %copy-start.7 = (bf16[192,2048]{1,0:T(8,128)(2,1)}, bf16[192,2048]{1,0:T(8,128)(2,1)S(1)}, u32[]{:S(2)}) copy-start(bf16[192,2048]{1,0:T(8,128)(2,1)S(1)} %broadcast_select_fusion.y_ref) | copy-start | bytes 2359300
  250.6 24.8 %collective-permute-start.38 = (bf16[192,2048]{1,0:T(8,128)(2,1)S(1)}, bf16[192,2048]{1,0:T(8,128)(2,1)S(1)}, u32[]{:S(2)}, u32[]{:S(2)}) collective-permute-start(bf16[192,2048]{1,0:T(8,128)(2,1)S(1)} %broadcast_select_fusion.y_ref), channel_id=1, source_target_pairs={{0,4},{4,0},{8,12},{12,8},{16,20},{20,16},{24,28},{28,24},{1,5},{5... | collective-permute-start | bytes 2359304 | tf_op jit(solution)/shard_map/ppermute | solution.py:248
  252.2 23.3 %collective-permute-start.37 = (bf16[192,2048]{1,0:T(8,128)(2,1)}, bf16[192,2048]{1,0:T(8,128)(2,1)S(1)}, u32[]{:S(2)}, u32[]{:S(2)}) collective-permute-start(bf16[192,2048]{1,0:T(8,128)(2,1)} %collective-permute-done.8.y_ref), channel_id=1, source_target_pairs={{0,8},{4,12},{8,0},{12,4},{16,24},{20,28},{24,16},{28,20},{1,9},{5... | collective-permute-start | bytes 2359304 | tf_op jit(solution)/shard_map/ppermute | solution.py:246
  275.5 0.9 copy-start.8
  275.5 1.2 copy-start.9
where the time goes:
time: 281 us; the launch traced here: 280 us
  waiting for transfers between devices  129 us (46%)
  Pallas kernels  79.7 us (28%)
  starting transfers between devices  57.2 us (20%)
  other arithmetic  10.1 us (4%)
    ppermute x24, waiting for transfers between devices, hop(): return lax.ppermute(value, 'rows', both)  72.7 us
    pallas_call x26, Pallas kernels, decode(): pl.pallas_call(decode_body, grid_spec=pltpu.PrefetchScalarGridSpec(num_sc...  57.8 us
    ppermute x15, waiting for transfers between devices, local_plane(): lax.ppermute(value, 'rows', [(i, i ^ 1) for i in range(8)])  56.3 us
    ppermute x24, starting transfers between devices, hop(): return lax.ppermute(value, 'rows', both)  39.2 us
    ppermute x15, starting transfers between devices, local_plane(): lax.ppermute(value, 'rows', [(i, i ^ 1) for i in range(8)])  18 us
    pallas_call x2, Pallas kernels, encode(): pl.pallas_call(functools.partial(encode_body, picks=[half for _, _, half...  9.89 us
    select_n x8, other arithmetic, arrived(): V[j] = jnp.where(outer, O[k], M[j])  8.39 us
    pallas_call x1, Pallas kernels, own_share(): pl.pallas_call(own_body, grid_spec=pltpu.PrefetchScalarGridSpec(num_scala...  7.23 us
  transfers between devices with their start and end apart: 39, of which 15 were waited for; matrix products, arithmetic and copies ran while one was open for 4% of the time, Pallas kernels for 26%

commit v1 on v0

--- a/solution.py
+++ b/solution.py
@@ -11,6 +11,17 @@
 keep_rate = 0.7
 
 SPAN = 250.0
+
+
+KERNEL_VMEM = 14 * 2**20
+
+
+def near_by(value):
+    return pltpu.with_memory_space_constraint(value, pltpu.VMEM)
+
+
+def stay_out(value):
+    return pltpu.with_memory_space_constraint(value, pltpu.HBM)
 
 
 def gained(w_ref, a_ref, gain):
@@ -50,7 +61,7 @@
     operands, in_specs, out_shape, out_specs = [gain], [pl.BlockSpec(gain.shape, lambda j: (0,))], [], []
     earlier = 0 if maxima is None else 1
     for w, avg, half in chunks:
-        operands += [w, avg]
+        operands += [stay_out(w), stay_out(avg)]
         in_specs += [pl.BlockSpec((half_rows, block), lambda j, half=half: (half, j))] * 2
         out_shape.append(jax.ShapeDtypeStruct((half_rows, columns), jnp.bfloat16))
         out_specs.append(pl.BlockSpec((half_rows, block), lambda j: (0, j)))
@@ -64,8 +75,54 @@
         in_specs=in_specs,
         out_specs=out_specs + [pl.BlockSpec((count, 1, block), lambda j: (0, 0, j))],
         out_shape=out_shape + [jax.ShapeDtypeStruct((count, 1, columns), jnp.float32)],
+        compiler_params=pltpu.CompilerParams(vmem_limit_bytes=KERNEL_VMEM),
         name="encode",
     )(*operands)
+
+
+def encode_first_body(g_ref, w_ref, a_ref, y_ref, m_ref, gain_ref, ws, avgs, sems, *, half):
+    half_rows, _ = y_ref.shape
+    steps, _, width = ws.shape
+    copies = []
+    gain_copy = pltpu.make_async_copy(g_ref, gain_ref, sems.at[2, 0])
+    gain_copy.start()
+    for j in range(steps):
+        source = (pl.ds(half * half_rows, half_rows), pl.ds(j * width, width))
+        pair = [
+            pltpu.make_async_copy(ref.at[source], held.at[j], sems.at[i, j])
+            for i, (ref, held) in enumerate(((w_ref, ws), (a_ref, avgs)))
+        ]
+        for copy in pair:
+            copy.start()
+        copies.append(pair)
+    gain_copy.wait()
+    gain = tall_gain(gain_ref, width)[half * half_rows : (half + 1) * half_rows]
+    for j, pair in enumerate(copies):
+        for copy in pair:
+            copy.wait()
+        part = pl.ds(j * width, width)
+        y, m = coded(gained(ws.at[j], avgs.at[j], gain))
+        y_ref[:, part] = y
+        m_ref[0, :, part] = m
+
+
+def encode_first(w, avg, gain, half, width):
+    half_rows, columns = w.shape[0] // 2, w.shape[1]
+    here = pl.BlockSpec(memory_space=pltpu.VMEM)
+    there = pl.BlockSpec(memory_space=pl.ANY)
+    held = pltpu.VMEM((columns // width, half_rows, width), jnp.float32)
+    return pl.pallas_call(
+        functools.partial(encode_first_body, half=half),
+        in_specs=[there, there, there],
+        out_specs=[here, here],
+        out_shape=[
+            pltpu.VMEM((half_rows, columns), jnp.bfloat16),
+            pltpu.VMEM((1, 1, columns), jnp.float32),
+        ],
+        scratch_shapes=[pltpu.VMEM(gain.shape, gain.dtype), held, held, pltpu.SemaphoreType.DMA((3, columns // width))],
+        compiler_params=pltpu.CompilerParams(vmem_limit_bytes=KERNEL_VMEM),
+        name="encode_first",
+    )(stay_out(gain), stay_out(w), stay_out(avg))
 
 
 def own_body(me_ref, wg_ref, ag_ref, wu_ref, au_ref, g_ref, f_ref, og_ref, ou_ref, token_ref):
@@ -94,8 +151,9 @@
             out_specs=[landed, landed, pl.BlockSpec((8, 128), lambda j, me: (0, 0))],
         ),
         out_shape=[out, out, jax.ShapeDtypeStruct((8, 128), jnp.float32)],
+        compiler_params=pltpu.CompilerParams(vmem_limit_bytes=KERNEL_VMEM),
         name="own_share",
-    )(me, w_gate, avg_gate, w_up, avg_up, gain, factors)
+    )(me, *map(stay_out, (w_gate, avg_gate, w_up, avg_up)), gain, factors)
 
 
 def ratios_body(*refs):
@@ -116,11 +174,12 @@
     return pl.pallas_call(
         ratios_body,
         out_shape=[
-            jax.ShapeDtypeStruct((32, 1, columns), jnp.float32),
+            pltpu.VMEM((32, 1, columns), jnp.float32),
             jax.ShapeDtypeStruct((2, columns), jnp.float32),
         ],
+        compiler_params=pltpu.CompilerParams(vmem_limit_bytes=KERNEL_VMEM),
         name="ratios",
-    )(*tables)
+    )(*map(near_by, tables))
 
 
 def decoded(y, ratio):
@@ -129,78 +188,47 @@
     return jnp.where(y < 0, -x, x).astype(jnp.bfloat16)
 
 
-def decode_body(me_ref, y_ref, r_ref, whole_ref, out_ref, token_ref):
-    del me_ref, whole_ref
-    out_ref[...] = decoded(y_ref[...], r_ref[0])
-    token_ref[...] = jnp.zeros_like(token_ref)
-
-
-def decode(whole, chunk, ratios, me, shard_of, c, block):
-    half_rows, columns = chunk.shape
-    return pl.pallas_call(
-        decode_body,
-        grid_spec=pltpu.PrefetchScalarGridSpec(
-            num_scalar_prefetch=1,
-            grid=(columns // block,),
-            in_specs=[
-                pl.BlockSpec((half_rows, block), lambda j, me: (0, j)),
-                pl.BlockSpec((1, 1, block), lambda j, me: ((shard_of(me[0]) ^ me[0]) * 4 + c, 0, j)),
-                pl.BlockSpec(memory_space=pl.ANY),
-            ],
-            out_specs=[
-                pl.BlockSpec((half_rows, block), lambda j, me: (2 * shard_of(me[0]) + c // 2, j)),
-                pl.BlockSpec((8, 128), lambda j, me: (0, 0)),
-            ],
-        ),
-        out_shape=[
-            jax.ShapeDtypeStruct(whole.shape, whole.dtype),
-            jax.ShapeDtypeStruct((8, 128), jnp.float32),
-        ],
-        input_output_aliases={3: 0},
-        name="decode",
-    )(me, chunk, ratios, whole)
-
-
-def last_body(me_ref, y0_ref, y1_ref, r0_ref, r1_ref, whole_ref, out_ref, buffer, sems, *, starts_of, pieces):
-    del whole_ref
-    rows = y0_ref.shape[0] // pieces
+def decode_body(me_ref, r_ref, *refs, places, pieces):
+    count = len(places)
+    chunks, (out_ref, token_ref, buffer, sems) = refs[:count], refs[count + 1 :]
+    rows = chunks[0].shape[0] // pieces
+    me = me_ref[0]
     copies = []
-    for i, (y_ref, r_ref) in enumerate(((y0_ref, r0_ref), (y1_ref, r1_ref))):
-        start = starts_of[i](me_ref[0]) * y_ref.shape[0]
+    for i, (shard_of, c) in enumerate(places):
+        shard = shard_of(me)
+        ratio = r_ref[(shard ^ me) * 4 + c]
+        start = (2 * shard + c // 2) * chunks[0].shape[0]
         for p in range(pieces):
             part = pl.ds(p * rows, rows)
-            buffer[i, part] = decoded(y_ref[part], r_ref[0])
+            buffer[i, part] = decoded(chunks[i][part], ratio)
             copies.append(
                 pltpu.make_async_copy(buffer.at[i, part], out_ref.at[pl.ds(start + p * rows, rows)], sems.at[i, p])
             )
             copies[-1].start()
+    token_ref[...] = jnp.zeros_like(token_ref)
     for copy in copies:
         copy.wait()
 
 
-def decode_last(whole, chunks, ratios, me, shards_of, cs, pieces=4):
-    half_rows, columns = chunks[0].shape
-    kept = pl.BlockSpec(memory_space=pltpu.VMEM)
-    ratio = lambda shard_of, c: pl.BlockSpec(
-        (1, 1, columns), lambda j, me: ((shard_of(me[0]) ^ me[0]) * 4 + c, 0, 0)
-    )
-    starts_of = [lambda me, at=at, c=c: 2 * at(me) + c // 2 for at, c in zip(shards_of, cs)]
-    return pl.pallas_call(
-        functools.partial(last_body, starts_of=starts_of, pieces=pieces),
-        grid_spec=pltpu.PrefetchScalarGridSpec(
-            num_scalar_prefetch=1,
-            grid=(1,),
-            in_specs=[kept, kept, *map(ratio, shards_of, cs), pl.BlockSpec(memory_space=pl.ANY)],
-            out_specs=pl.BlockSpec(memory_space=pl.ANY),
-            scratch_shapes=[
-                pltpu.VMEM((2, half_rows, columns), whole.dtype),
-                pltpu.SemaphoreType.DMA((2, pieces)),
-            ],
-        ),
-        out_shape=jax.ShapeDtypeStruct(whole.shape, whole.dtype),
-        input_output_aliases={5: 0},
-        name="decode_last",
-    )(me, *chunks, ratios, ratios, whole)
+def decode(whole, chunks, ratios, me, places, pieces=4):
+    here = pl.BlockSpec(memory_space=pltpu.VMEM)
+    there = pl.BlockSpec(memory_space=pl.ANY)
+    return pl.pallas_call(
+        functools.partial(decode_body, places=places, pieces=pieces),
+        in_specs=[pl.BlockSpec(memory_space=pltpu.SMEM), here] + [here] * len(chunks) + [there],
+        out_specs=[there, here],
+        out_shape=[
+            jax.ShapeDtypeStruct(whole.shape, whole.dtype),
+            pltpu.VMEM((8, 128), jnp.float32),
+        ],
+        scratch_shapes=[
+            pltpu.VMEM((len(chunks), *chunks[0].shape), whole.dtype),
+            pltpu.SemaphoreType.DMA((len(chunks), pieces)),
+        ],
+        input_output_aliases={2 + len(chunks): 0},
+        compiler_params=pltpu.CompilerParams(vmem_limit_bytes=KERNEL_VMEM),
+        name="decode",
+    )(me, near_by(ratios), *map(near_by, chunks), whole)
 
 
 def after(value, *tokens):
@@ -251,9 +279,9 @@
     middle = lambda value: hop(value, [(1, 2), (2, 1)])
     skip = lambda value: hop(value, [(0, 2), (2, 0), (1, 3), (3, 1)])
 
-    first, maxima = encode([(w_gate, avg_gate, 0)], norm_gain, block)
+    first, maxima = encode_first(w_gate, avg_gate, norm_gain, 0, block // 4)
     others = [(w_up, avg_up, 0), (w_gate, avg_gate, 1), (w_up, avg_up, 1)]
-    *rest, maxima = encode(others, norm_gain, block // 2, maxima)
+    *rest, maxima = encode(others, norm_gain, block // 2, near_by(maxima))
     own = [first, *rest]
 
     X, B, M, O, V, F = {}, {}, {}, {}, {}, {}
@@ -308,7 +336,7 @@
         done = []
         for _ in range(min(count, len(waiting))):
             chunk, shard_of, c = waiting.pop(0)
-            wholes[c % 2], token = decode(wholes[c % 2], chunk, ratios, me, shard_of, c, block)
+            wholes[c % 2], token = decode(wholes[c % 2], [chunk], ratios, me, [(shard_of, c)])
             done.append(token)
         return done
 
@@ -335,7 +363,7 @@
             tokens = settle(3 if k < 13 else len(waiting) - 2)
     chunks, shards_of, cs = zip(*waiting)
     t = cs[0] % 2
-    wholes[t] = decode_last(wholes[t], chunks, ratios, me, shards_of, cs)
+    wholes[t], _ = decode(wholes[t], chunks, ratios, me, list(zip(shards_of, cs)))
     return (*wholes, factors[0], factors[1])
 
 

time: 281 us -> 276 us (0.982)
  waiting for transfers between devices: 129 us -> 152 us
  Pallas kernels: 79.7 us -> 66.9 us
  other arithmetic: 10.1 us -> 2.05 us
  starting transfers between devices: 57.2 us -> 49.7 us
    ppermute x24, waiting for transfers between devices: 72.7 us -> 96.9 us  [hop(): return lax.ppermute(value, 'rows', both)]
    pallas_call x28 -> x29, Pallas kernels: 62.6 us -> 53.6 us  [the longest x27 51.3 us: decode(): pl.pallas_call(functools.partial(decode_body, places=places, pieces=piece...]
    ppermute x24, starting transfers between devices: 39.2 us -> 32.2 us  [hop(): return lax.ppermute(value, 'rows', both)]
    select_n x8, other arithmetic: 8.39 us -> 1.87 us  [arrived(): V[j] = jnp.where(outer, O[k], M[j])]
    pallas_call x2 -> x1, Pallas kernels: 9.89 us -> 6.25 us  [encode(): pl.pallas_call(functools.partial(encode_body, picks=[half for _, _, half...]
  transfers between devices with their start and end apart: 39 -> 39, of which waited for: 15 -> 18; matrix products, arithmetic and copies ran while one was open for 4% -> 1% of each run, Pallas kernels for 26% -> 23%
where the time goes in v1:
time: 276 us; the launch traced here: 275 us
  waiting for transfers between devices  152 us (55%)
  Pallas kernels  66.9 us (24%)
  starting transfers between devices  49.7 us (18%)
  local copies, waits for them, and re-layouts  3.15 us (1%)
    ppermute x24, waiting for transfers between devices, hop(): return lax.ppermute(value, 'rows', both)  96.9 us
    ppermute x15, waiting for transfers between devices, local_plane(): lax.ppermute(value, 'rows', [(i, i ^ 1) for i in range(8)])  55.1 us
    pallas_call x27, Pallas kernels, decode(): pl.pallas_call(functools.partial(decode_body, places=places, pieces=piece...  51.3 us
    ppermute x24, starting transfers between devices, hop(): return lax.ppermute(value, 'rows', both)  32.2 us
    ppermute x15, starting transfers between devices, local_plane(): lax.ppermute(value, 'rows', [(i, i ^ 1) for i in range(8)])  17.4 us
    pallas_call x1, Pallas kernels, own_share(): pl.pallas_call(own_body, grid_spec=pltpu.PrefetchScalarGridSpec(num_scala...  7 us
    pallas_call x1, Pallas kernels, encode(): pl.pallas_call(functools.partial(encode_body, picks=[half for _, _, half...  6.25 us
  transfers between devices with their start and end apart: 39, of which 18 were waited for; matrix products, arithmetic and copies ran while one was open for 1% of the time, Pallas kernels for 23%

profile of v1, /device:TPU:0, one launch (start us, length us, event | category | flops | bytes accessed | tf_op | source)
XLA Modules:
  0.0 275.1 jit_solution(6756869806639829263)
XLA Ops:
  0.6 2.3 encode_first.1
  2.9 3.0 %collective-permute-start.1 = (bf16[192,2048]{1,0:T(8,128)(2,1)S(1)}, bf16[192,2048]{1,0:T(8,128)(2,1)S(1)}, u32[]{:S(2)}, u32[]{:S(2)}) collective-permute-start(bf16[192,2048]{1,0:T(8,128)(2,1)S(1)} %get-tuple-element.94), channel_id=1, source_target_pairs={{0,4},{4,0},{8,12},{12,8},{16,20},{20,16},{24,28},{28,24},{1,5},{5... | collective-permute-start | bytes 2359304 | tf_op jit(solution)/shard_map/ppermute | solution.py:276
  6.0 1.6 collective-permute-start.2
  7.6 1.6 collective-permute-start.3
  9.8 6.3 %encode.1 = (bf16[192,2048]{1,0:T(8,128)(2,1)S(1)}, bf16[192,2048]{1,0:T(8,128)(2,1)S(1)}, bf16[192,2048]{1,0:T(8,128)(2,1)}, f32[4,1,2048]{2,1,0:T(1,128)S(1)}) custom-call(f32[384]{0:T(512)S(1)} %copy-done.4, f32[384,2048]{1,0:T(8,128)} %wu_ref.1, f32[384,2048]{1,0:T(8,128)} %au_ref.1, f32[384,2048]{1,0:T(8,128)} %wg_ref.1, f32[384,2048]{1,0:T(8,128)} %ag_ref.1, ...), custom_call_target="tpu_custom_call" | custom-call | tf_op jit(solution)/shard_map/encode/pallas_call | solution.py:72
  16.6 3.5 %collective-permute-start = (f32[4,1,2048]{2,1,0:T(1,128)S(1)}, f32[4,1,2048]{2,1,0:T(1,128)S(1)}, u32[]{:S(2)}, u32[]{:S(2)}) collective-permute-start(f32[4,1,2048]{2,1,0:T(1,128)S(1)} %get-tuple-element.93.refs_0_), channel_id=1, source_target_pairs={{0,8},{4,12},{8,0},{12,4},{16,24},{20,28},{24,16},{28,20},{1,9},{5... | collective-permute-start | bytes 98312 | tf_op jit(solution)/shard_map/ppermute | solution.py:274
  20.1 5.6 %collective-permute-done.refs_1_ = f32[4,1,2048]{2,1,0:T(1,128)S(1)} collective-permute-done((f32[4,1,2048]{2,1,0:T(1,128)S(1)}, f32[4,1,2048]{2,1,0:T(1,128)S(1)}, u32[]{:S(2)}, u32[]{:S(2)}) %collective-permute-start) | collective-permute-done | bytes 32800 | tf_op jit(solution)/shard_map/ppermute | solution.py:274
  25.7 1.6 collective-permute-start.6
  28.6 4.3 %collective-permute-start.9 = (bf16[192,2048]{1,0:T(8,128)(2,1)S(1)}, bf16[192,2048]{1,0:T(8,128)(2,1)S(1)}, u32[]{:S(2)}, u32[]{:S(2)}) collective-permute-start(bf16[192,2048]{1,0:T(8,128)(2,1)S(1)} %get-tuple-element.100), channel_id=1, source_target_pairs={{0,8},{4,12},{8,0},{12,4},{16,24},{20,28},{24,16},{28,20},{1,9},{5... | collective-permute-start | bytes 2359304 | tf_op jit(solution)/shard_map/ppermute | solution.py:274
  32.9 8.3 %collective-permute-done.5.refs_0_ = bf16[192,2048]{1,0:T(8,128)(2,1)S(1)} collective-permute-done((bf16[192,2048]{1,0:T(8,128)(2,1)S(1)}, bf16[192,2048]{1,0:T(8,128)(2,1)S(1)}, u32[]{:S(2)}, u32[]{:S(2)}) %collective-permute-start.5) | collective-permute-done | bytes 786464 | tf_op jit(solution)/shard_map/ppermute | solution.py:276
  42.0 4.2 %collective-permute-done.6.refs_0_ = bf16[192,2048]{1,0:T(8,128)(2,1)} collective-permute-done((bf16[192,2048]{1,0:T(8,128)(2,1)S(1)}, bf16[192,2048]{1,0:T(8,128)(2,1)}, u32[]{:S(2)}, u32[]{:S(2)}) %collective-permute-start.6) | collective-permute-done | bytes 786464 | tf_op jit(solution)/shard_map/ppermute | solution.py:274
  46.2 2.6 collective-permute-start.4
  48.8 18.8 %collective-permute-done.4.refs_2_ = f32[8,1,2048]{2,1,0:T(1,128)S(1)} collective-permute-done((f32[8,1,2048]{2,1,0:T(1,128)S(1)}, f32[8,1,2048]{2,1,0:T(1,128)S(1)}, u32[]{:S(2)}, u32[]{:S(2)}) %collective-permute-start.4) | collective-permute-done | bytes 65568 | tf_op jit(solution)/shard_map/ppermute | solution.py:274
  68.3 1.6 collective-permute-start.8
  69.8 17.9 %collective-permute-done.8.refs_3_ = f32[16,1,2048]{2,1,0:T(1,128)S(1)} collective-permute-done((f32[16,1,2048]{2,1,0:T(1,128)S(1)}, f32[16,1,2048]{2,1,0:T(1,128)S(1)}, u32[]{:S(2)}, u32[]{:S(2)}) %collective-permute-start.8) | collective-permute-done | bytes 131104 | tf_op jit(solution)/shard_map/ppermute | solution.py:276
  88.7 1.5 collective-permute-start.22
  90.2 1.3 collective-permute-start.13
  93.4 1.5 collective-permute-start.14
  95.0 7.0 %own_share.1 = (bf16[3072,2048]{1,0:T(8,128)(2,1)}, bf16[3072,2048]{1,0:T(8,128)(2,1)}, f32[8,128]{1,0:T(8,128)}) custom-call(s32[1]{0:T(128)} %bitcast.me_ref, f32[384,2048]{1,0:T(8,128)} %wg_ref.1, f32[384,2048]{1,0:T(8,128)} %ag_ref.1, f32[384,2048]{1,0:T(8,128)} %wu_ref.1, f32[384,2048]{1,0:T(8,128)} %au_ref.1, f32[384]{0:T(512)S(1)} %copy-done.5, ...), custom_call_target="tpu_custom_call" | custom-call | tf_op jit(solution)/shard_map/own_share/pallas_call | solution.py:141
  102.0 6.4 %collective-permute-done.19.refs_0_ = bf16[192,2048]{1,0:T(8,128)(2,1)S(1)} collective-permute-done((bf16[192,2048]{1,0:T(8,128)(2,1)}, bf16[192,2048]{1,0:T(8,128)(2,1)S(1)}, u32[]{:S(2)}, u32[]{:S(2)}) %collective-permute-start.19) | collective-permute-done | bytes 786464 | tf_op jit(solution)/shard_map/ppermute | solution.py:274
  108.4 1.3 collective-permute-start.23
  110.4 14.9 %collective-permute-done.13 = bf16[192,2048]{1,0:T(8,128)(2,1)} collective-permute-done((bf16[192,2048]{1,0:T(8,128)(2,1)}, bf16[192,2048]{1,0:T(8,128)(2,1)}, u32[]{:S(2)}, u32[]{:S(2)}) %collective-permute-start.13) | collective-permute-done | bytes 786464 | tf_op jit(solution)/shard_map/ppermute | solution.py:274
  126.2 1.8 decode.27
  128.0 2.9 %decode.28 = (bf16[3072,2048]{1,0:T(8,128)(2,1)}, f32[8,128]{1,0:T(8,128)}) custom-call(s32[1]{0:T(128)} %bitcast.me_ref, f32[32,1,2048]{2,1,0:T(1,128)S(1)} %get-tuple-element.98.r_ref, bf16[192,2048]{1,0:T(8,128)(2,1)} %collective-permute-done.2.refs_0_, bf16[3072,2048]{1,0:T(8,128)(2,1)} %get-tuple-element.107.refs_1_), custom_call_target="tpu_custom_call", output_to_operand_aliasing={{0}: (3, {})} | custom-call | tf_op jit(solution)/shard_map/decode/pallas_call | solution.py:216
  130.9 1.8 decode.29
  135.1 2.9 %decode.30 = (bf16[3072,2048]{1,0:T(8,128)(2,1)}, f32[8,128]{1,0:T(8,128)}) custom-call(s32[1]{0:T(128)} %bitcast.me_ref, f32[32,1,2048]{2,1,0:T(1,128)S(1)} %get-tuple-element.98.r_ref, bf16[192,2048]{1,0:T(8,128)(2,1)} %collective-permute-done.6.refs_0_, bf16[3072,2048]{1,0:T(8,128)(2,1)} %get-tuple-element.116.refs_1_), custom_call_target="tpu_custom_call", output_to_operand_aliasing={{0}: (3, {})} | custom-call | tf_op jit(solution)/shard_map/decode/pallas_call | solution.py:216
  138.1 1.8 decode.33
  139.8 1.8 decode.34
  141.6 1.3 collective-permute-start.16
  143.6 2.0 collective-permute-done.24.refs_0_
  146.3 1.3 collective-permute-start.29
  147.7 12.2 %collective-permute-done.17.refs_0_ = bf16[192,2048]{1,0:T(8,128)(2,1)S(1)} collective-permute-done((bf16[192,2048]{1,0:T(8,128)(2,1)S(1)}, bf16[192,2048]{1,0:T(8,128)(2,1)S(1)}, u32[]{:S(2)}, u32[]{:S(2)}) %collective-permute-start.17) | collective-permute-done | bytes 786464 | tf_op jit(solution)/shard_map/ppermute | solution.py:276
  160.8 1.8 decode.31
  162.5 1.8 decode.32
  164.3 2.9 %decode.35 = (bf16[3072,2048]{1,0:T(8,128)(2,1)}, f32[8,128]{1,0:T(8,128)}) custom-call(s32[1]{0:T(128)} %bitcast.me_ref, f32[32,1,2048]{2,1,0:T(1,128)S(1)} %get-tuple-element.98.r_ref, bf16[192,2048]{1,0:T(8,128)(2,1)} %collective-permute-done.12.refs_0_, bf16[3072,2048]{1,0:T(8,128)(2,1)} %get-tuple-element.123.refs_1_), custom_call_target="tpu_custom_call", output_to_operand_aliasing={{0}: (3, {})} | custom-call | tf_op jit(solution)/shard_map/decode/pallas_call | solution.py:216
  167.2 1.8 decode.36
  169.0 1.8 decode.39
  170.7 1.8 decode.40
  172.5 1.5 collective-permute-start.21
  175.3 1.8 decode.37
  177.1 3.4 %collective-permute-done.29 = bf16[192,2048]{1,0:T(8,128)(2,1)S(1)} collective-permute-done((bf16[192,2048]{1,0:T(8,128)(2,1)}, bf16[192,2048]{1,0:T(8,128)(2,1)S(1)}, u32[]{:S(2)}, u32[]{:S(2)}) %collective-permute-start.29) | collective-permute-done | bytes 786464 | tf_op jit(solution)/shard_map/ppermute | solution.py:274
  180.5 1.3 collective-permute-start.32
  183.1 1.8 decode.38
  184.9 1.8 decode.41
  186.6 10.7 %collective-permute-done.21 = bf16[192,2048]{1,0:T(8,128)(2,1)S(1)} collective-permute-done((bf16[192,2048]{1,0:T(8,128)(2,1)}, bf16[192,2048]{1,0:T(8,128)(2,1)S(1)}, u32[]{:S(2)}, u32[]{:S(2)}) %collective-permute-start.21) | collective-permute-done | bytes 786464 | tf_op jit(solution)/shard_map/ppermute | solution.py:274
  198.7 1.3 collective-permute-start.27
  200.0 1.8 decode.42
  201.7 1.8 decode.45
  203.5 1.8 decode.46
  205.3 8.9 %collective-permute-done.32 = bf16[192,2048]{1,0:T(8,128)(2,1)S(1)} collective-permute-done((bf16[192,2048]{1,0:T(8,128)(2,1)S(1)}, bf16[192,2048]{1,0:T(8,128)(2,1)S(1)}, u32[]{:S(2)}, u32[]{:S(2)}) %collective-permute-start.32) | collective-permute-done | bytes 786464 | tf_op jit(solution)/shard_map/ppermute | solution.py:274
  214.2 1.3 collective-permute-start.36
  216.8 1.8 decode.43
  218.6 1.8 decode.44
  220.3 10.6 %collective-permute-done.28.refs_0_ = bf16[192,2048]{1,0:T(8,128)(2,1)S(1)} collective-permute-done((bf16[192,2048]{1,0:T(8,128)(2,1)S(1)}, bf16[192,2048]{1,0:T(8,128)(2,1)S(1)}, u32[]{:S(2)}, u32[]{:S(2)}) %collective-permute-start.28) | collective-permute-done | bytes 786464 | tf_op jit(solution)/shard_map/ppermute | solution.py:276
  231.1 1.8 decode.47
  232.9 1.8 decode.48
  235.9 12.0 %collective-permute-done.36 = bf16[192,2048]{1,0:T(8,128)(2,1)S(1)} collective-permute-done((bf16[192,2048]{1,0:T(8,128)(2,1)S(1)}, bf16[192,2048]{1,0:T(8,128)(2,1)S(1)}, u32[]{:S(2)}, u32[]{:S(2)}) %collective-permute-start.36) | collective-permute-done | bytes 786464 | tf_op jit(solution)/shard_map/ppermute | solution.py:274
  249.8 1.7 decode.51
  251.6 1.8 decode.52
  253.3 11.0 %collective-permute-done.34.refs_0_ = bf16[192,2048]{1,0:T(8,128)(2,1)S(1)} collective-permute-done((bf16[192,2048]{1,0:T(8,128)(2,1)S(1)}, bf16[192,2048]{1,0:T(8,128)(2,1)S(1)}, u32[]{:S(2)}, u32[]{:S(2)}) %collective-permute-start.34) | collective-permute-done | bytes 786464 | tf_op jit(solution)/shard_map/ppermute | solution.py:274
  264.3 1.8 decode.49
  266.1 1.8 decode.50
  267.9 4.2 %collective-permute-done.38.refs_1_ = bf16[192,2048]{1,0:T(8,128)(2,1)S(1)} collective-permute-done((bf16[192,2048]{1,0:T(8,128)(2,1)S(1)}, bf16[192,2048]{1,0:T(8,128)(2,1)S(1)}, u32[]{:S(2)}, u32[]{:S(2)}) %collective-permute-start.38) | collective-permute-done | bytes 786464 | tf_op jit(solution)/shard_map/ppermute | solution.py:276
  272.7 2.2 decode.53
  (76 shorter events, 22.6 us)
Async XLA Ops:
  0.6 94.4 %copy-start.5 = (f32[384]{0:T(512)S(1)}, f32[384]{0:T(512)}, u32[]{:S(2)}) copy-start(f32[384]{0:T(512)} %g_ref.3) | copy-start | bytes 4612
  2.9 24.3 %collective-permute-start.1 = (bf16[192,2048]{1,0:T(8,128)(2,1)S(1)}, bf16[192,2048]{1,0:T(8,128)(2,1)S(1)}, u32[]{:S(2)}, u32[]{:S(2)}) collective-permute-start(bf16[192,2048]{1,0:T(8,128)(2,1)S(1)} %get-tuple-element.94), channel_id=1, source_target_pairs={{0,4},{4,0},{8,12},{12,8},{16,20},{20,16},{24,28},{28,24},{1,5},{5... | collective-permute-start | bytes 2359304 | tf_op jit(solution)/shard_map/ppermute | solution.py:276
  6.0 22.0 %collective-permute-start.2 = (bf16[192,2048]{1,0:T(8,128)(2,1)S(1)}, bf16[192,2048]{1,0:T(8,128)(2,1)}, u32[]{:S(2)}, u32[]{:S(2)}) collective-permute-start(bf16[192,2048]{1,0:T(8,128)(2,1)S(1)} %get-tuple-element.94), channel_id=1, source_target_pairs={{0,8},{4,12},{8,0},{12,4},{16,24},{20,28},{24,16},{28,20},{1,9},{5... | collective-permute-start | bytes 2359304 | tf_op jit(solution)/shard_map/ppermute | solution.py:274
  7.6 20.4 %collective-permute-start.3 = (bf16[192,2048]{1,0:T(8,128)(2,1)S(1)}, bf16[192,2048]{1,0:T(8,128)(2,1)}, u32[]{:S(2)}, u32[]{:S(2)}) collective-permute-start(bf16[192,2048]{1,0:T(8,128)(2,1)S(1)} %get-tuple-element.94), channel_id=1, source_target_pairs={{8,16},{12,20},{16,8},{20,12},{9,17},{13,21},{17,9},{21,13},{10,18... | collective-permute-start | bytes 2359304 | tf_op jit(solution)/shard_map/ppermute | solution.py:274
  9.1 0.7 copy-start.4
  16.0 25.2 %collective-permute-start.5 = (bf16[192,2048]{1,0:T(8,128)(2,1)S(1)}, bf16[192,2048]{1,0:T(8,128)(2,1)S(1)}, u32[]{:S(2)}, u32[]{:S(2)}) collective-permute-start(bf16[192,2048]{1,0:T(8,128)(2,1)S(1)} %get-tuple-element.96), channel_id=1, source_target_pairs={{0,4},{4,0},{8,12},{12,8},{16,20},{20,16},{24,28},{28,24},{1,5},{5... | collective-permute-start | bytes 2359304 | tf_op jit(solution)/shard_map/ppermute | solution.py:276
  16.6 9.1 %collective-permute-start = (f32[4,1,2048]{2,1,0:T(1,128)S(1)}, f32[4,1,2048]{2,1,0:T(1,128)S(1)}, u32[]{:S(2)}, u32[]{:S(2)}) collective-permute-start(f32[4,1,2048]{2,1,0:T(1,128)S(1)} %get-tuple-element.93.refs_0_), channel_id=1, source_target_pairs={{0,8},{4,12},{8,0},{12,4},{16,24},{20,28},{24,16},{28,20},{1,9},{5... | collective-permute-start | bytes 98312 | tf_op jit(solution)/shard_map/ppermute | solution.py:274
  25.7 20.5 %collective-permute-start.6 = (bf16[192,2048]{1,0:T(8,128)(2,1)S(1)}, bf16[192,2048]{1,0:T(8,128)(2,1)}, u32[]{:S(2)}, u32[]{:S(2)}) collective-permute-start(bf16[192,2048]{1,0:T(8,128)(2,1)S(1)} %get-tuple-element.96), channel_id=1, source_target_pairs={{0,8},{4,12},{8,0},{12,4},{16,24},{20,28},{24,16},{28,20},{1,9},{5... | collective-permute-start | bytes 2359304 | tf_op jit(solution)/shard_map/ppermute | solution.py:274
  27.3 21.5 %collective-permute-start.7 = (bf16[192,2048]{1,0:T(8,128)(2,1)S(1)}, bf16[192,2048]{1,0:T(8,128)(2,1)S(1)}, u32[]{:S(2)}, u32[]{:S(2)}) collective-permute-start(bf16[192,2048]{1,0:T(8,128)(2,1)S(1)} %get-tuple-element.96), channel_id=1, source_target_pairs={{8,16},{12,20},{16,8},{20,12},{9,17},{13,21},{17,9},{21,13},{10,18... | collective-permute-start | bytes 2359304 | tf_op jit(solution)/shard_map/ppermute | solution.py:274
  28.0 59.8 %collective-permute-start.10 = (bf16[192,2048]{1,0:T(8,128)(2,1)S(1)}, bf16[192,2048]{1,0:T(8,128)(2,1)S(1)}, u32[]{:S(2)}, u32[]{:S(2)}) collective-permute-start(bf16[192,2048]{1,0:T(8,128)(2,1)S(1)} %get-tuple-element.100), channel_id=1, source_target_pairs={{0,4},{4,0},{8,12},{12,8},{16,20},{20,16},{24,28},{28,24},{1,5},{5... | collective-permute-start | bytes 2359304 | tf_op jit(solution)/shard_map/ppermute | solution.py:276
  28.6 61.6 %collective-permute-start.9 = (bf16[192,2048]{1,0:T(8,128)(2,1)S(1)}, bf16[192,2048]{1,0:T(8,128)(2,1)S(1)}, u32[]{:S(2)}, u32[]{:S(2)}) collective-permute-start(bf16[192,2048]{1,0:T(8,128)(2,1)S(1)} %get-tuple-element.100), channel_id=1, source_target_pairs={{0,8},{4,12},{8,0},{12,4},{16,24},{20,28},{24,16},{28,20},{1,9},{5... | collective-permute-start | bytes 2359304 | tf_op jit(solution)/shard_map/ppermute | solution.py:274
  41.2 49.0 %collective-permute-start.11 = (bf16[192,2048]{1,0:T(8,128)(2,1)S(1)}, bf16[192,2048]{1,0:T(8,128)(2,1)S(1)}, u32[]{:S(2)}, u32[]{:S(2)}) collective-permute-start(bf16[192,2048]{1,0:T(8,128)(2,1)S(1)} %get-tuple-element.100), channel_id=1, source_target_pairs={{8,16},{12,20},{16,8},{20,12},{9,17},{13,21},{17,9},{21,13},{10,18... | collective-permute-start | bytes 2359304 | tf_op jit(solution)/shard_map/ppermute | solution.py:274
  46.2 21.4 %collective-permute-start.4 = (f32[8,1,2048]{2,1,0:T(1,128)S(1)}, f32[8,1,2048]{2,1,0:T(1,128)S(1)}, u32[]{:S(2)}, u32[]{:S(2)}) collective-permute-start(f32[8,1,2048]{2,1,0:T(1,128)S(1)} %pad_maximum_fusion.1), channel_id=1, source_target_pairs={{0,16},{4,20},{16,0},{20,4},{8,24},{12,28},{24,8},{28,12},{1,17},{... | collective-permute-start | bytes 196616 | tf_op jit(solution)/shard_map/ppermute | solution.py:274
  48.8 18.8 %copy-start.8 = (bf16[192,2048]{1,0:T(8,128)(2,1)}, bf16[192,2048]{1,0:T(8,128)(2,1)S(1)}, u32[]{:S(2)}) copy-start(bf16[192,2048]{1,0:T(8,128)(2,1)S(1)} %collective-permute-done.7) | copy-start | bytes 2359300
  67.6 24.8 %collective-permute-start.18 = (bf16[192,2048]{1,0:T(8,128)(2,1)}, bf16[192,2048]{1,0:T(8,128)(2,1)S(1)}, u32[]{:S(2)}, u32[]{:S(2)}) collective-permute-start(bf16[192,2048]{1,0:T(8,128)(2,1)} %get-tuple-element.115), channel_id=1, source_target_pairs={{0,4},{4,0},{8,12},{12,8},{16,20},{20,16},{24,28},{28,24},{1,5},{5... | collective-permute-start | bytes 2359304 | tf_op jit(solution)/shard_map/ppermute | solution.py:276
  68.3 19.5 %collective-permute-start.8 = (f32[16,1,2048]{2,1,0:T(1,128)S(1)}, f32[16,1,2048]{2,1,0:T(1,128)S(1)}, u32[]{:S(2)}, u32[]{:S(2)}) collective-permute-start(f32[16,1,2048]{2,1,0:T(1,128)S(1)} %pad_maximum_fusion), channel_id=1, source_target_pairs={{0,4},{4,0},{8,12},{12,8},{16,20},{20,16},{24,28},{28,24},{1,5},{5... | collective-permute-start | bytes 393224 | tf_op jit(solution)/shard_map/ppermute | solution.py:276
  87.8 20.6 %collective-permute-start.19 = (bf16[192,2048]{1,0:T(8,128)(2,1)}, bf16[192,2048]{1,0:T(8,128)(2,1)S(1)}, u32[]{:S(2)}, u32[]{:S(2)}) collective-permute-start(bf16[192,2048]{1,0:T(8,128)(2,1)} %get-tuple-element.115), channel_id=1, source_target_pairs={{0,8},{4,12},{8,0},{12,4},{16,24},{20,28},{24,16},{28,20},{1,9},{5... | collective-permute-start | bytes 2359304 | tf_op jit(solution)/shard_map/ppermute | solution.py:274
  87.8 0.9 copy-start.2
  88.7 19.7 %collective-permute-start.22 = (bf16[192,2048]{1,0:T(8,128)(2,1)}, bf16[192,2048]{1,0:T(8,128)(2,1)}, u32[]{:S(2)}, u32[]{:S(2)}) collective-permute-start(bf16[192,2048]{1,0:T(8,128)(2,1)} %get-tuple-element.115), channel_id=1, source_target_pairs={{8,16},{12,20},{16,8},{20,12},{9,17},{13,21},{17,9},{21,13},{10,18... | collective-permute-start | bytes 2359304 | tf_op jit(solution)/shard_map/ppermute | solution.py:274
  90.2 2.2 copy-start.6
  90.2 35.1 %collective-permute-start.13 = (bf16[192,2048]{1,0:T(8,128)(2,1)}, bf16[192,2048]{1,0:T(8,128)(2,1)}, u32[]{:S(2)}, u32[]{:S(2)}) collective-permute-start(bf16[192,2048]{1,0:T(8,128)(2,1)} %collective-permute-done.3), channel_id=1, source_target_pairs={{8,0},{12,4},{16,24},{20,28},{9,1},{13,5},{17,25},{21,29},{10,2},{... | collective-permute-start | bytes 2359304 | tf_op jit(solution)/shard_map/ppermute | solution.py:274
  91.5 42.4 %collective-permute-start.12 = (bf16[192,2048]{1,0:T(8,128)(2,1)S(1)}, bf16[192,2048]{1,0:T(8,128)(2,1)}, u32[]{:S(2)}, u32[]{:S(2)}) collective-permute-start(bf16[192,2048]{1,0:T(8,128)(2,1)S(1)} %collective-permute-done.9.refs_0_), channel_id=1, source_target_pairs={{0,4},{4,0},{8,12},{12,8},{16,20},{20,16},{24,28},{28,24},{1,5},{5... | collective-permute-start | bytes 2359304 | tf_op jit(solution)/shard_map/ppermute | solution.py:276
  92.5 0.9 copy-start
  93.4 40.5 %collective-permute-start.14 = (bf16[192,2048]{1,0:T(8,128)(2,1)}, bf16[192,2048]{1,0:T(8,128)(2,1)}, u32[]{:S(2)}, u32[]{:S(2)}) collective-permute-start(bf16[192,2048]{1,0:T(8,128)(2,1)} %collective-permute-done.2.refs_0_), channel_id=1, source_target_pairs={{8,16},{12,20},{16,8},{20,12},{9,17},{13,21},{17,9},{21,13},{10,18... | collective-permute-start | bytes 2359304 | tf_op jit(solution)/shard_map/ppermute | solution.py:274
  94.9 13.4 %copy-start.9 = (bf16[192,2048]{1,0:T(8,128)(2,1)S(1)}, bf16[192,2048]{1,0:T(8,128)(2,1)}, u32[]{:S(2)}) copy-start(bf16[192,2048]{1,0:T(8,128)(2,1)} %copy-done.8) | copy-start | bytes 2359300
  108.4 34.5 %collective-permute-start.23 = (bf16[192,2048]{1,0:T(8,128)(2,1)S(1)}, bf16[192,2048]{1,0:T(8,128)(2,1)S(1)}, u32[]{:S(2)}, u32[]{:S(2)}) collective-permute-start(bf16[192,2048]{1,0:T(8,128)(2,1)S(1)} %copy-done.9), channel_id=1, source_target_pairs={{8,0},{12,4},{16,24},{20,28},{9,1},{13,5},{17,25},{21,29},{10,2},{... | collective-permute-start | bytes 2359304 | tf_op jit(solution)/shard_map/ppermute | solution.py:274
  109.7 33.9 %collective-permute-start.25 = (bf16[192,2048]{1,0:T(8,128)(2,1)}, bf16[192,2048]{1,0:T(8,128)(2,1)S(1)}, u32[]{:S(2)}, u32[]{:S(2)}) collective-permute-start(bf16[192,2048]{1,0:T(8,128)(2,1)} %collective-permute-done.6.refs_0_), channel_id=1, source_target_pairs={{8,16},{12,20},{16,8},{20,12},{9,17},{13,21},{17,9},{21,13},{10,18... | collective-permute-start | bytes 2359304 | tf_op jit(solution)/shard_map/ppermute | solution.py:274
  125.3 20.3 %collective-permute-start.24 = (bf16[192,2048]{1,0:T(8,128)(2,1)S(1)}, bf16[192,2048]{1,0:T(8,128)(2,1)S(1)}, u32[]{:S(2)}, u32[]{:S(2)}) collective-permute-start(bf16[192,2048]{1,0:T(8,128)(2,1)S(1)} %collective-permute-done.19.refs_0_), channel_id=1, source_target_pairs={{0,4},{4,0},{8,12},{12,8},{16,20},{20,16},{24,28},{28,24},{1,5},{5... | collective-permute-start | bytes 2359304 | tf_op jit(solution)/shard_map/ppermute | solution.py:276
  130.9 7.1 %copy-start.3 = (bf16[192,2048]{1,0:T(8,128)(2,1)S(1)}, bf16[192,2048]{1,0:T(8,128)(2,1)}, u32[]{:S(2)}) copy-start(bf16[192,2048]{1,0:T(8,128)(2,1)} %copy-done.2) | copy-start | bytes 2359300
  133.9 26.0 %collective-permute-start.17 = (bf16[192,2048]{1,0:T(8,128)(2,1)S(1)}, bf16[192,2048]{1,0:T(8,128)(2,1)S(1)}, u32[]{:S(2)}, u32[]{:S(2)}) collective-permute-start(bf16[192,2048]{1,0:T(8,128)(2,1)S(1)} %broadcast_select_fusion.6.refs_0_), channel_id=1, source_target_pairs={{0,4},{4,0},{8,12},{12,8},{16,20},{20,16},{24,28},{28,24},{1,5},{5... | collective-permute-start | bytes 2359304 | tf_op jit(solution)/shard_map/ppermute | solution.py:276
  138.0 3.6 %copy-start.7 = (bf16[192,2048]{1,0:T(8,128)(2,1)S(1)}, bf16[192,2048]{1,0:T(8,128)(2,1)}, u32[]{:S(2)}) copy-start(bf16[192,2048]{1,0:T(8,128)(2,1)} %copy-done.6) | copy-start | bytes 2359300
  138.0 22.7 %copy-start.1 = (bf16[192,2048]{1,0:T(8,128)(2,1)S(1)}, bf16[192,2048]{1,0:T(8,128)(2,1)}, u32[]{:S(2)}) copy-start(bf16[192,2048]{1,0:T(8,128)(2,1)} %copy-done) | copy-start | bytes 2359300
  141.6 30.9 %collective-permute-start.16 = (bf16[192,2048]{1,0:T(8,128)(2,1)S(1)}, bf16[192,2048]{1,0:T(8,128)(2,1)S(1)}, u32[]{:S(2)}, u32[]{:S(2)}) collective-permute-start(bf16[192,2048]{1,0:T(8,128)(2,1)S(1)} %copy-done.7), channel_id=1, source_target_pairs={{8,0},{12,4},{16,24},{20,28},{9,1},{13,5},{17,25},{21,29},{10,2},{... | collective-permute-start | bytes 2359304 | tf_op jit(solution)/shard_map/ppermute | solution.py:274
  142.9 29.6 %collective-permute-start.15 = (bf16[192,2048]{1,0:T(8,128)(2,1)S(1)}, bf16[192,2048]{1,0:T(8,128)(2,1)S(1)}, u32[]{:S(2)}, u32[]{:S(2)}) collective-permute-start(bf16[192,2048]{1,0:T(8,128)(2,1)S(1)} %collective-permute-done.9.refs_0_), channel_id=1, source_target_pairs={{8,16},{12,20},{16,8},{20,12},{9,17},{13,21},{17,9},{21,13},{10,18... | collective-permute-start | bytes 2359304 | tf_op jit(solution)/shard_map/ppermute | solution.py:274
  145.6 31.5 %collective-permute-start.30 = (bf16[192,2048]{1,0:T(8,128)(2,1)S(1)}, bf16[192,2048]{1,0:T(8,128)(2,1)S(1)}, u32[]{:S(2)}, u32[]{:S(2)}) collective-permute-start(bf16[192,2048]{1,0:T(8,128)(2,1)S(1)} %collective-permute-done.19.refs_0_), channel_id=1, source_target_pairs={{8,16},{12,20},{16,8},{20,12},{9,17},{13,21},{17,9},{21,13},{10,18... | collective-permute-start | bytes 2359304 | tf_op jit(solution)/shard_map/ppermute | solution.py:274
  146.3 34.2 %collective-permute-start.29 = (bf16[192,2048]{1,0:T(8,128)(2,1)}, bf16[192,2048]{1,0:T(8,128)(2,1)S(1)}, u32[]{:S(2)}, u32[]{:S(2)}) collective-permute-start(bf16[192,2048]{1,0:T(8,128)(2,1)} %collective-permute-done.22), channel_id=1, source_target_pairs={{8,0},{12,4},{16,24},{20,28},{9,1},{13,5},{17,25},{21,29},{10,2},{... | collective-permute-start | bytes 2359304 | tf_op jit(solution)/shard_map/ppermute | solution.py:274
  159.9 20.6 %collective-permute-start.26 = (bf16[192,2048]{1,0:T(8,128)(2,1)S(1)}, bf16[192,2048]{1,0:T(8,128)(2,1)S(1)}, u32[]{:S(2)}, u32[]{:S(2)}) collective-permute-start(bf16[192,2048]{1,0:T(8,128)(2,1)S(1)} %broadcast_select_fusion.5.refs_0_), channel_id=1, source_target_pairs={{0,4},{4,0},{8,12},{12,8},{16,20},{20,16},{24,28},{28,24},{1,5},{5... | collective-permute-start | bytes 2359304 | tf_op jit(solution)/shard_map/ppermute | solution.py:276
  172.5 24.8 %collective-permute-start.21 = (bf16[192,2048]{1,0:T(8,128)(2,1)}, bf16[192,2048]{1,0:T(8,128)(2,1)S(1)}, u32[]{:S(2)}, u32[]{:S(2)}) collective-permute-start(bf16[192,2048]{1,0:T(8,128)(2,1)} %collective-permute-done.14), channel_id=1, source_target_pairs={{8,0},{12,4},{16,24},{20,28},{9,1},{13,5},{17,25},{21,29},{10,2},{... | collective-permute-start | bytes 2359304 | tf_op jit(solution)/shard_map/ppermute | solution.py:274
  174.1 23.4 %collective-permute-start.20 = (bf16[192,2048]{1,0:T(8,128)(2,1)S(1)}, bf16[192,2048]{1,0:T(8,128)(2,1)S(1)}, u32[]{:S(2)}, u32[]{:S(2)}) collective-permute-start(bf16[192,2048]{1,0:T(8,128)(2,1)S(1)} %broadcast_select_fusion.7.refs_0_), channel_id=1, source_target_pairs={{0,4},{4,0},{8,12},{12,8},{16,20},{20,16},{24,28},{28,24},{1,5},{5... | collective-permute-start | bytes 2359304 | tf_op jit(solution)/shard_map/ppermute | solution.py:276
  180.5 33.7 %collective-permute-start.32 = (bf16[192,2048]{1,0:T(8,128)(2,1)S(1)}, bf16[192,2048]{1,0:T(8,128)(2,1)S(1)}, u32[]{:S(2)}, u32[]{:S(2)}) collective-permute-start(bf16[192,2048]{1,0:T(8,128)(2,1)S(1)} %collective-permute-done.25), channel_id=1, source_target_pairs={{8,0},{12,4},{16,24},{20,28},{9,1},{13,5},{17,25},{21,29},{10,2},{... | collective-permute-start | bytes 2359304 | tf_op jit(solution)/shard_map/ppermute | solution.py:274
  181.9 32.3 %collective-permute-start.31 = (bf16[192,2048]{1,0:T(8,128)(2,1)S(1)}, bf16[192,2048]{1,0:T(8,128)(2,1)S(1)}, u32[]{:S(2)}, u32[]{:S(2)}) collective-permute-start(bf16[192,2048]{1,0:T(8,128)(2,1)S(1)} %broadcast_select_fusion.2.refs_0_), channel_id=1, source_target_pairs={{0,4},{4,0},{8,12},{12,8},{16,20},{20,16},{24,28},{28,24},{1,5},{5... | collective-permute-start | bytes 2359304 | tf_op jit(solution)/shard_map/ppermute | solution.py:276
  197.5 33.4 %collective-permute-start.28 = (bf16[192,2048]{1,0:T(8,128)(2,1)S(1)}, bf16[192,2048]{1,0:T(8,128)(2,1)S(1)}, u32[]{:S(2)}, u32[]{:S(2)}) collective-permute-start(bf16[192,2048]{1,0:T(8,128)(2,1)S(1)} %broadcast_select_fusion.3.refs_0_), channel_id=1, source_target_pairs={{0,4},{4,0},{8,12},{12,8},{16,20},{20,16},{24,28},{28,24},{1,5},{5... | collective-permute-start | bytes 2359304 | tf_op jit(solution)/shard_map/ppermute | solution.py:276
  198.7 32.4 %collective-permute-start.27 = (bf16[192,2048]{1,0:T(8,128)(2,1)S(1)}, bf16[192,2048]{1,0:T(8,128)(2,1)S(1)}, u32[]{:S(2)}, u32[]{:S(2)}) collective-permute-start(bf16[192,2048]{1,0:T(8,128)(2,1)S(1)} %collective-permute-done.15), channel_id=1, source_target_pairs={{8,0},{12,4},{16,24},{20,28},{9,1},{13,5},{17,25},{21,29},{10,2},{... | collective-permute-start | bytes 2359304 | tf_op jit(solution)/shard_map/ppermute | solution.py:274
  214.2 33.7 %collective-permute-start.36 = (bf16[192,2048]{1,0:T(8,128)(2,1)S(1)}, bf16[192,2048]{1,0:T(8,128)(2,1)S(1)}, u32[]{:S(2)}, u32[]{:S(2)}) collective-permute-start(bf16[192,2048]{1,0:T(8,128)(2,1)S(1)} %collective-permute-done.30), channel_id=1, source_target_pairs={{8,0},{12,4},{16,24},{20,28},{9,1},{13,5},{17,25},{21,29},{10,2},{... | collective-permute-start | bytes 2359304 | tf_op jit(solution)/shard_map/ppermute | solution.py:274
  215.6 32.4 %collective-permute-start.35 = (bf16[192,2048]{1,0:T(8,128)(2,1)S(1)}, bf16[192,2048]{1,0:T(8,128)(2,1)S(1)}, u32[]{:S(2)}, u32[]{:S(2)}) collective-permute-start(bf16[192,2048]{1,0:T(8,128)(2,1)S(1)} %broadcast_select_fusion.1.refs_0_), channel_id=1, source_target_pairs={{0,4},{4,0},{8,12},{12,8},{16,20},{20,16},{24,28},{28,24},{1,5},{5... | collective-permute-start | bytes 2359304 | tf_op jit(solution)/shard_map/ppermute | solution.py:276
  231.1 33.3 %collective-permute-start.34 = (bf16[192,2048]{1,0:T(8,128)(2,1)S(1)}, bf16[192,2048]{1,0:T(8,128)(2,1)S(1)}, u32[]{:S(2)}, u32[]{:S(2)}) collective-permute-start(bf16[192,2048]{1,0:T(8,128)(2,1)S(1)} %collective-permute-done.1.refs_0_), channel_id=1, source_target_pairs={{0,8},{4,12},{8,0},{12,4},{16,24},{20,28},{24,16},{28,20},{1,9},{5... | collective-permute-start | bytes 2359304 | tf_op jit(solution)/shard_map/ppermute | solution.py:274
  234.7 31.4 %collective-permute-start.33 = (bf16[192,2048]{1,0:T(8,128)(2,1)S(1)}, bf16[192,2048]{1,0:T(8,128)(2,1)S(1)}, u32[]{:S(2)}, u32[]{:S(2)}) collective-permute-start(bf16[192,2048]{1,0:T(8,128)(2,1)S(1)} %broadcast_select_fusion.4.refs_0_), channel_id=1, source_target_pairs={{0,4},{4,0},{8,12},{12,8},{16,20},{20,16},{24,28},{28,24},{1,5},{5... | collective-permute-start | bytes 2359304 | tf_op jit(solution)/shard_map/ppermute | solution.py:276
  248.0 24.0 %collective-permute-start.38 = (bf16[192,2048]{1,0:T(8,128)(2,1)S(1)}, bf16[192,2048]{1,0:T(8,128)(2,1)S(1)}, u32[]{:S(2)}, u32[]{:S(2)}) collective-permute-start(bf16[192,2048]{1,0:T(8,128)(2,1)S(1)} %broadcast_select_fusion.refs_0_), channel_id=1, source_target_pairs={{0,4},{4,0},{8,12},{12,8},{16,20},{20,16},{24,28},{28,24},{1,5},{5... | collective-permute-start | bytes 2359304 | tf_op jit(solution)/shard_map/ppermute | solution.py:276
  249.2 23.5 %collective-permute-start.37 = (bf16[192,2048]{1,0:T(8,128)(2,1)S(1)}, bf16[192,2048]{1,0:T(8,128)(2,1)S(1)}, u32[]{:S(2)}, u32[]{:S(2)}) collective-permute-start(bf16[192,2048]{1,0:T(8,128)(2,1)S(1)} %collective-permute-done.5.refs_0_), channel_id=1, source_target_pairs={{0,8},{4,12},{8,0},{12,4},{16,24},{20,28},{24,16},{28,20},{1,9},{5... | collective-permute-start | bytes 2359304 | tf_op jit(solution)/shard_map/ppermute | solution.py:274

commit v2 on v1

--- a/solution.py
+++ b/solution.py
@@ -11,6 +11,7 @@
 keep_rate = 0.7
 
 SPAN = 250.0
+SCALE_OF_CHUNK = (0, 1, 2, 1)
 
 
 KERNEL_VMEM = 14 * 2**20
@@ -35,49 +36,49 @@
     return jnp.concatenate([lanes] * (width // 128), axis=1)
 
 
-def coded(x):
-    size = jnp.abs(x)
-    m = jnp.max(size, axis=0, keepdims=True)
-    y = jnp.exp2(size * (SPAN / jnp.maximum(m, 1e-30)) - SPAN / 2)
-    return jnp.where(x < 0, -y, y).astype(jnp.bfloat16), m
-
-
-def encode_body(gain_ref, *refs, picks, earlier):
-    count = len(picks)
-    ins, outs = refs[: 2 * count], refs[2 * count + earlier :]
-    half_rows, width = ins[0].shape
+def scale_of(m):
+    return m.astype(jnp.bfloat16).astype(jnp.float32)
+
+
+def largest(x):
+    return jnp.max(jnp.abs(x), axis=0, keepdims=True)
+
+
+def coded(x, m):
+    y = jnp.exp2(jnp.abs(x) * (SPAN / jnp.maximum(scale_of(m), 1e-30)) - SPAN / 2)
+    return jnp.where(x < 0, -y, y).astype(jnp.bfloat16)
+
+
+def encode_rest_body(gain_ref, wu0, au0, wg, ag, wu1, au1, first_ref, up0, gate, up1, m_ref):
+    half_rows, width = wg.shape
     tall = tall_gain(gain_ref, width)
-    for i, half in enumerate(picks):
-        gain = tall[half * half_rows : (half + 1) * half_rows]
-        y, m = coded(gained(ins[2 * i], ins[2 * i + 1], gain))
-        outs[i][...] = y
-        outs[count][earlier + i] = m
-    if earlier:
-        outs[count][0] = refs[2 * count][0]
-
-
-def encode(chunks, gain, block, maxima=None):
-    half_rows, columns = chunks[0][0].shape[0] // 2, chunks[0][0].shape[1]
-    operands, in_specs, out_shape, out_specs = [gain], [pl.BlockSpec(gain.shape, lambda j: (0,))], [], []
-    earlier = 0 if maxima is None else 1
-    for w, avg, half in chunks:
-        operands += [stay_out(w), stay_out(avg)]
-        in_specs += [pl.BlockSpec((half_rows, block), lambda j, half=half: (half, j))] * 2
-        out_shape.append(jax.ShapeDtypeStruct((half_rows, columns), jnp.bfloat16))
-        out_specs.append(pl.BlockSpec((half_rows, block), lambda j: (0, j)))
-    if earlier:
-        operands.append(maxima)
-        in_specs.append(pl.BlockSpec((1, 1, block), lambda j: (0, 0, j)))
-    count = earlier + len(chunks)
-    return pl.pallas_call(
-        functools.partial(encode_body, picks=[half for _, _, half in chunks], earlier=earlier),
+    top, bottom = tall[:half_rows], tall[half_rows:]
+    upper, lower = gained(wu0, au0, top), gained(wu1, au1, bottom)
+    m = jnp.maximum(largest(upper), largest(lower))
+    up0[...] = coded(upper, m)
+    up1[...] = coded(lower, m)
+    m_ref[1] = m
+    x = gained(wg, ag, bottom)
+    m = largest(x)
+    gate[...] = coded(x, m)
+    m_ref[2] = m
+    m_ref[0] = first_ref[0]
+
+
+def encode_rest(w_gate, avg_gate, w_up, avg_up, gain, first_maxima, block):
+    half_rows, columns = w_gate.shape[0] // 2, w_gate.shape[1]
+    half = lambda h: [pl.BlockSpec((half_rows, block), lambda j: (h, j))] * 2
+    stacked = lambda n: pl.BlockSpec((n, 1, block), lambda j: (0, 0, j))
+    chunk = jax.ShapeDtypeStruct((half_rows, columns), jnp.bfloat16)
+    return pl.pallas_call(
+        encode_rest_body,
         grid=(columns // block,),
-        in_specs=in_specs,
-        out_specs=out_specs + [pl.BlockSpec((count, 1, block), lambda j: (0, 0, j))],
-        out_shape=out_shape + [jax.ShapeDtypeStruct((count, 1, columns), jnp.float32)],
-        compiler_params=pltpu.CompilerParams(vmem_limit_bytes=KERNEL_VMEM),
-        name="encode",
-    )(*operands)
+        in_specs=[pl.BlockSpec(gain.shape, lambda j: (0,)), *half(0), *half(1), *half(1), stacked(1)],
+        out_specs=[pl.BlockSpec((half_rows, block), lambda j: (0, j))] * 3 + [stacked(3)],
+        out_shape=[chunk, chunk, chunk, jax.ShapeDtypeStruct((3, 1, columns), jnp.float32)],
+        compiler_params=pltpu.CompilerParams(vmem_limit_bytes=KERNEL_VMEM),
+        name="encode_rest",
+    )(gain, *map(stay_out, (w_up, avg_up, w_gate, avg_gate, w_up, avg_up)), near_by(first_maxima))
 
 
 def encode_first_body(g_ref, w_ref, a_ref, y_ref, m_ref, gain_ref, ws, avgs, sems, *, half):
@@ -101,8 +102,9 @@
         for copy in pair:
             copy.wait()
         part = pl.ds(j * width, width)
-        y, m = coded(gained(ws.at[j], avgs.at[j], gain))
-        y_ref[:, part] = y
+        x = gained(ws.at[j], avgs.at[j], gain)
+        m = largest(x)
+        y_ref[:, part] = coded(x, m)
         m_ref[0, :, part] = m
 
 
@@ -156,30 +158,48 @@
     )(me, *map(stay_out, (w_gate, avg_gate, w_up, avg_up)), gain, factors)
 
 
-def ratios_body(*refs):
-    tables, (ratio_ref, factor_ref) = refs[:-2], refs[-2:]
-    order = [0, 2, 4, 6, 1, 3, 5, 7]
-    rows = [ref[i] for ref in tables for i in range(ref.shape[0])]
+def half_table_body(m0_ref, m1_ref, m2_ref, scale_ref, most_ref):
+    rows = [ref[i] for ref in (m0_ref, m1_ref, m2_ref) for i in range(ref.shape[0])]
+    for i, row in enumerate(rows):
+        scale_ref[i] = row.astype(jnp.bfloat16)
+    most_ref[0] = functools.reduce(jnp.maximum, rows[0::3] + rows[2::3])
+    most_ref[1] = functools.reduce(jnp.maximum, rows[1::3])
+
+
+def half_table(maxima):
+    columns = maxima[0].shape[-1]
+    return pl.pallas_call(
+        half_table_body,
+        out_shape=[
+            pltpu.VMEM((12, 1, columns), jnp.bfloat16),
+            pltpu.VMEM((2, 1, columns), jnp.float32),
+        ],
+        compiler_params=pltpu.CompilerParams(vmem_limit_bytes=KERNEL_VMEM),
+        name="half_table",
+    )(*map(near_by, maxima))
+
+
+def ratios_body(scale0_ref, scale1_ref, most0_ref, most1_ref, ratio_ref, factor_ref):
     for t in range(2):
-        mine = [rows[4 * place + c] for place in range(8) for c in (t, t + 2)]
-        factor = functools.reduce(jnp.maximum, mine)
+        factor = jnp.maximum(most0_ref[t], most1_ref[t])
         factor_ref[t : t + 1, :] = factor
-        for place, shard in enumerate(order):
-            for c in (t, t + 2):
-                ratio_ref[4 * shard + c] = rows[4 * place + c] / factor
-
-
-def ratios_of(tables):
-    columns = tables[0].shape[-1]
+        for side, scale_ref in enumerate((scale0_ref, scale1_ref)):
+            for place in range(4):
+                for k in (0, 2) if t == 0 else (1,):
+                    ratio_ref[3 * (2 * place + side) + k] = scale_ref[3 * place + k].astype(jnp.float32) / factor
+
+
+def ratios_of(scales, most):
+    columns = most[0].shape[-1]
     return pl.pallas_call(
         ratios_body,
         out_shape=[
-            pltpu.VMEM((32, 1, columns), jnp.float32),
+            pltpu.VMEM((24, 1, columns), jnp.float32),
             jax.ShapeDtypeStruct((2, columns), jnp.float32),
         ],
         compiler_params=pltpu.CompilerParams(vmem_limit_bytes=KERNEL_VMEM),
         name="ratios",
-    )(*map(near_by, tables))
+    )(*map(near_by, scales), *map(near_by, most))
 
 
 def decoded(y, ratio):
@@ -196,7 +216,7 @@
     copies = []
     for i, (shard_of, c) in enumerate(places):
         shard = shard_of(me)
-        ratio = r_ref[(shard ^ me) * 4 + c]
+        ratio = r_ref[(shard ^ me) * 3 + SCALE_OF_CHUNK[c]]
         start = (2 * shard + c // 2) * chunks[0].shape[0]
         for p in range(pieces):
             part = pl.ds(p * rows, rows)
@@ -265,6 +285,7 @@
 
 def local_plane(w_gate, avg_gate, w_up, avg_up, norm_gain):
     block = min(w_gate.shape[1], 1024)
+    width = lax.axis_size("width")
     index = lax.axis_index("rows")
     outer = (index < 2) | (index >= 6)
     me = jnp.reshape(index, (1,)).astype(jnp.int32)
@@ -279,9 +300,8 @@
     middle = lambda value: hop(value, [(1, 2), (2, 1)])
     skip = lambda value: hop(value, [(0, 2), (2, 0), (1, 3), (3, 1)])
 
-    first, maxima = encode_first(w_gate, avg_gate, norm_gain, 0, block // 4)
-    others = [(w_up, avg_up, 0), (w_gate, avg_gate, 1), (w_up, avg_up, 1)]
-    *rest, maxima = encode(others, norm_gain, block // 2, near_by(maxima))
+    first, first_maxima = encode_first(w_gate, avg_gate, norm_gain, 0, block // 4)
+    *rest, maxima = encode_rest(w_gate, avg_gate, w_up, avg_up, norm_gain, first_maxima, block // 2)
     own = [first, *rest]
 
     X, B, M, O, V, F = {}, {}, {}, {}, {}, {}
@@ -313,6 +333,21 @@
             waiting.append((V[j], near_of if j < 4 else far_of, j % 4))
         return got
 
+    def send_first():
+        odd = lax.axis_index("width") % 2 == 1
+        cores = [(row, column) for row in range(8) for column in range(width)]
+        flat = lambda row, column: row * width + column
+        swap = lambda turn: lax.ppermute(
+            first,
+            ("rows", "width"),
+            [(flat(r, c), flat(r ^ (1 if (c + turn) % 2 == 0 else 2), c)) for r, c in cores],
+        )
+        one = swap(0)
+        two = swap(1)
+        M[0] = middle(first)
+        X[0] = jnp.where(odd, two, one)
+        B[0] = jnp.where(odd, one, two)
+
     def send(k, *ties):
         tie = lambda value: after(value, *ties) if ties else value
         if k < 4:
@@ -340,7 +375,7 @@
             done.append(token)
         return done
 
-    send(0)
+    send_first()
     tables.append(buddies(maxima))
     send(1)
     for k in range(14):
@@ -350,10 +385,12 @@
             tables.append(skip(after(jnp.concatenate(tables, axis=0), *got)))
         if k == 1:
             got.append(tables[2])
-            tables.append(across(after(jnp.concatenate(tables, axis=0), *got)))
+            scales, most = half_table(tables)
+            far_scales = across(after(scales, *got))
+            far_most = across(after(most, *got))
         if k == 2:
-            got.append(tables[3])
-            ratios, factors = ratios_of(tables)
+            got += [far_scales, far_most]
+            ratios, factors = ratios_of((scales, far_scales), (most, far_most))
         if k + 2 < 14:
             send(k + 2, *got, *tokens)
         if k == 2:

time: 276 us -> 280 us (1.014)
  starting transfers between devices: 49.7 us -> 57.8 us
  waiting for transfers between devices: 152 us -> 145 us
    ppermute x24 -> x23, waiting for transfers between devices: 96.9 us -> 89.7 us  [hop(): return lax.ppermute(value, 'rows', both)]
    ppermute x0 -> x2, waiting for transfers between devices: none -> 4.93 us  [send_first(): lax.ppermute(first, ('rows', 'width'), [(flat(r, c), flat(r ^ (1 if (c +...]
    ppermute x0 -> x2, starting transfers between devices: none -> 4.61 us  [send_first(): lax.ppermute(first, ('rows', 'width'), [(flat(r, c), flat(r ^ (1 if (c +...]
    ppermute x15, waiting for transfers between devices: 55.1 us -> 50.6 us  [local_plane(): lax.ppermute(value, 'rows', [(i, i ^ 1) for i in range(8)])]
    ppermute x24 -> x23, starting transfers between devices: 32.2 us -> 34 us  [hop(): return lax.ppermute(value, 'rows', both)]
    pallas_call x2 -> x3, Pallas kernels: 6.3 us -> 6.33 us  [the longest x1 6.22 us: encode_rest(): pl.pallas_call(encode_rest_body, grid=(columns // block,), in_specs=[pl.B...]
  transfers between devices with their start and end apart: 39 -> 40, of which waited for: 18 -> 20; matrix products, arithmetic and copies ran while one was open for 1% -> 1% of each run, Pallas kernels for 23% -> 22%
where the time goes in v2:
time: 280 us; the launch traced here: 279 us
  waiting for transfers between devices  145 us (52%)
  Pallas kernels  67 us (24%)
  starting transfers between devices  57.8 us (21%)
  local copies, waits for them, and re-layouts  3.96 us (1%)
  other arithmetic  3.39 us (1%)
    ppermute x23, waiting for transfers between devices, hop(): return lax.ppermute(value, 'rows', both)  89.7 us
    pallas_call x27, Pallas kernels, decode(): pl.pallas_call(functools.partial(decode_body, places=places, pieces=piece...  51.3 us
    ppermute x15, waiting for transfers between devices, local_plane(): lax.ppermute(value, 'rows', [(i, i ^ 1) for i in range(8)])  50.6 us
    ppermute x23, starting transfers between devices, hop(): return lax.ppermute(value, 'rows', both)  34 us
    ppermute x15, starting transfers between devices, local_plane(): lax.ppermute(value, 'rows', [(i, i ^ 1) for i in range(8)])  19.2 us
    pallas_call x1, Pallas kernels, own_share(): pl.pallas_call(own_body, grid_spec=pltpu.PrefetchScalarGridSpec(num_scala...  7 us
    pallas_call x1, Pallas kernels, encode_rest(): pl.pallas_call(encode_rest_body, grid=(columns // block,), in_specs=[pl.B...  6.22 us
  transfers between devices with their start and end apart: 40, of which 20 were waited for; matrix products, arithmetic and copies ran while one was open for 1% of the time, Pallas kernels for 22%

profile of v2, /device:TPU:0, one launch (start us, length us, event | category | flops | bytes accessed | tf_op | source)
XLA Modules:
  0.0 278.7 jit_solution(11721300728616696026)
XLA Ops:
  0.6 2.3 encode_first.1
  3.0 3.1 %collective-permute-start.1 = (bf16[192,2048]{1,0:T(8,128)(2,1)S(1)}, bf16[192,2048]{1,0:T(8,128)(2,1)}, u32[]{:S(2)}, u32[]{:S(2)}) collective-permute-start(bf16[192,2048]{1,0:T(8,128)(2,1)S(1)} %get-tuple-element.97), channel_id=1, source_target_pairs={{0,8},{1,5},{2,10},{3,7},{4,12},{5,1},{6,14},{7,3},{8,0},{9,13},{1... | collective-permute-start | bytes 2359304 | tf_op jit(solution)/shard_map/ppermute | solution.py:340
  7.6 1.5 collective-permute-start.3
  9.8 6.2 %encode_rest.1 = (bf16[192,2048]{1,0:T(8,128)(2,1)}, bf16[192,2048]{1,0:T(8,128)(2,1)}, bf16[192,2048]{1,0:T(8,128)(2,1)S(1)}, f32[3,1,2048]{2,1,0:T(1,128)S(1)}) custom-call(f32[384]{0:T(512)S(1)} %copy-done.4, f32[384,2048]{1,0:T(8,128)} %wu_ref.1, f32[384,2048]{1,0:T(8,128)} %au_ref.1, f32[384,2048]{1,0:T(8,128)} %wg_ref.1, f32[384,2048]{1,0:T(8,128)} %ag_ref.1, ...), custom_call_target="tpu_custom_call" | custom-call | tf_op jit(solution)/shard_map/encode_rest/pallas_call | solution.py:73
  17.4 3.5 %collective-permute-start.6 = (bf16[192,2048]{1,0:T(8,128)(2,1)}, bf16[192,2048]{1,0:T(8,128)(2,1)}, u32[]{:S(2)}, u32[]{:S(2)}) collective-permute-start(bf16[192,2048]{1,0:T(8,128)(2,1)} %get-tuple-element.100), channel_id=1, source_target_pairs={{0,8},{4,12},{8,0},{12,4},{16,24},{20,28},{24,16},{28,20},{1,9},{5... | collective-permute-start | bytes 2359304 | tf_op jit(solution)/shard_map/ppermute | solution.py:295
  21.0 3.1 %collective-permute-done.1 = bf16[192,2048]{1,0:T(8,128)(2,1)} collective-permute-done((bf16[192,2048]{1,0:T(8,128)(2,1)S(1)}, bf16[192,2048]{1,0:T(8,128)(2,1)}, u32[]{:S(2)}, u32[]{:S(2)}) %collective-permute-start.1) | collective-permute-done | bytes 786464 | tf_op jit(solution)/shard_map/ppermute | solution.py:340
  24.8 1.8 collective-permute-done.2
  26.6 3.5 %collective-permute-start = (f32[3,1,2048]{2,1,0:T(1,128)S(1)}, f32[3,1,2048]{2,1,0:T(1,128)S(1)}, u32[]{:S(2)}, u32[]{:S(2)}) collective-permute-start(f32[3,1,2048]{2,1,0:T(1,128)S(1)} %get-tuple-element.96.m0_ref), channel_id=1, source_target_pairs={{0,8},{4,12},{8,0},{12,4},{16,24},{20,28},{24,16},{28,20},{1,9},{5... | collective-permute-start | bytes 73736 | tf_op jit(solution)/shard_map/ppermute | solution.py:295
  31.5 9.8 %collective-permute-done.m1_ref = f32[3,1,2048]{2,1,0:T(1,128)S(1)} collective-permute-done((f32[3,1,2048]{2,1,0:T(1,128)S(1)}, f32[3,1,2048]{2,1,0:T(1,128)S(1)}, u32[]{:S(2)}, u32[]{:S(2)}) %collective-permute-start) | collective-permute-done | bytes 24608 | tf_op jit(solution)/shard_map/ppermute | solution.py:295
  42.7 1.7 collective-permute-start.10
  45.3 3.9 %collective-permute-start.4 = (f32[6,1,2048]{2,1,0:T(1,128)S(1)}, f32[6,1,2048]{2,1,0:T(1,128)S(1)}, u32[]{:S(2)}, u32[]{:S(2)}) collective-permute-start(f32[6,1,2048]{2,1,0:T(1,128)S(1)} %pad_maximum_fusion), channel_id=1, source_target_pairs={{0,16},{4,20},{16,0},{20,4},{8,24},{12,28},{24,8},{28,12},{1,17},{... | collective-permute-start | bytes 147464 | tf_op jit(solution)/shard_map/ppermute | solution.py:295
  49.1 19.0 %collective-permute-done.4.m2_ref = f32[6,1,2048]{2,1,0:T(1,128)S(1)} collective-permute-done((f32[6,1,2048]{2,1,0:T(1,128)S(1)}, f32[6,1,2048]{2,1,0:T(1,128)S(1)}, u32[]{:S(2)}, u32[]{:S(2)}) %collective-permute-start.4) | collective-permute-done | bytes 49184 | tf_op jit(solution)/shard_map/ppermute | solution.py:295
  68.1 1.7 collective-permute-start.19
  70.3 16.5 %collective-permute-done.9.most1_ref = f32[2,1,2048]{2,1,0:T(1,128)S(1)} collective-permute-done((f32[2,1,2048]{2,1,0:T(1,128)S(1)}, f32[2,1,2048]{2,1,0:T(1,128)S(1)}, u32[]{:S(2)}, u32[]{:S(2)}) %collective-permute-start.9) | collective-permute-done | bytes 16416 | tf_op jit(solution)/shard_map/ppermute | solution.py:297
  86.8 1.7 collective-permute-start.8
  88.6 2.9 %collective-permute-done.8.scale1_ref = bf16[12,1,2048]{2,1,0:T(2,128)(2,1)S(1)} collective-permute-done((bf16[12,1,2048]{2,1,0:T(2,128)(2,1)S(1)}, bf16[12,1,2048]{2,1,0:T(2,128)(2,1)S(1)}, u32[]{:S(2)}, u32[]{:S(2)}) %collective-permute-start.8) | collective-permute-done | bytes 49184 | tf_op jit(solution)/shard_map/ppermute | solution.py:297
  92.3 1.5 collective-permute-start.23
  95.2 1.8 collective-permute-start.13
  97.9 1.6 collective-permute-start.15
  99.5 7.0 %own_share.1 = (bf16[3072,2048]{1,0:T(8,128)(2,1)}, bf16[3072,2048]{1,0:T(8,128)(2,1)}, f32[8,128]{1,0:T(8,128)}) custom-call(s32[1]{0:T(128)} %bitcast.me_ref, f32[384,2048]{1,0:T(8,128)} %wg_ref.1, f32[384,2048]{1,0:T(8,128)} %ag_ref.1, f32[384,2048]{1,0:T(8,128)} %wu_ref.1, f32[384,2048]{1,0:T(8,128)} %au_ref.1, f32[384]{0:T(512)S(1)} %copy-done.5, ...), custom_call_target="tpu_custom_call" | custom-call | tf_op jit(solution)/shard_map/own_share/pallas_call | solution.py:143
  106.5 5.6 %collective-permute-done.20.refs_0_ = bf16[192,2048]{1,0:T(8,128)(2,1)} collective-permute-done((bf16[192,2048]{1,0:T(8,128)(2,1)}, bf16[192,2048]{1,0:T(8,128)(2,1)}, u32[]{:S(2)}, u32[]{:S(2)}) %collective-permute-start.20) | collective-permute-done | bytes 786464 | tf_op jit(solution)/shard_map/ppermute | solution.py:295
  114.2 14.8 %collective-permute-done.14 = bf16[192,2048]{1,0:T(8,128)(2,1)} collective-permute-done((bf16[192,2048]{1,0:T(8,128)(2,1)}, bf16[192,2048]{1,0:T(8,128)(2,1)}, u32[]{:S(2)}, u32[]{:S(2)}) %collective-permute-start.14) | collective-permute-done | bytes 786464 | tf_op jit(solution)/shard_map/ppermute | solution.py:295
  129.0 1.7 collective-permute-start.25
  130.8 1.8 decode.27
  132.5 1.8 decode.28
  134.3 1.8 decode.29
  137.7 2.9 %decode.30 = (bf16[3072,2048]{1,0:T(8,128)(2,1)}, f32[8,128]{1,0:T(8,128)}) custom-call(s32[1]{0:T(128)} %bitcast.me_ref, f32[24,1,2048]{2,1,0:T(1,128)S(1)} %get-tuple-element.104.r_ref, bf16[192,2048]{1,0:T(8,128)(2,1)} %collective-permute-done.6.refs_0_, bf16[3072,2048]{1,0:T(8,128)(2,1)} %get-tuple-element.122.refs_1_), custom_call_target="tpu_custom_call", output_to_operand_aliasing={{0}: (3, {})} | custom-call | tf_op jit(solution)/shard_map/decode/pallas_call | solution.py:236
  140.6 1.8 decode.33
  142.4 1.8 decode.34
  146.2 2.5 collective-permute-done.25.refs_0_
  150.7 13.1 %collective-permute-done.18.refs_0_ = bf16[192,2048]{1,0:T(8,128)(2,1)S(1)} collective-permute-done((bf16[192,2048]{1,0:T(8,128)(2,1)S(1)}, bf16[192,2048]{1,0:T(8,128)(2,1)S(1)}, u32[]{:S(2)}, u32[]{:S(2)}) %collective-permute-start.18) | collective-permute-done | bytes 786464 | tf_op jit(solution)/shard_map/ppermute | solution.py:297
  163.8 1.7 collective-permute-start.27
  165.6 1.8 decode.31
  167.3 2.9 %decode.32 = (bf16[3072,2048]{1,0:T(8,128)(2,1)}, f32[8,128]{1,0:T(8,128)}) custom-call(s32[1]{0:T(128)} %bitcast.me_ref, f32[24,1,2048]{2,1,0:T(1,128)S(1)} %get-tuple-element.104.r_ref, bf16[192,2048]{1,0:T(8,128)(2,1)} %collective-permute-done.20.refs_0_, bf16[3072,2048]{1,0:T(8,128)(2,1)} %get-tuple-element.125.refs_1_), custom_call_target="tpu_custom_call", output_to_operand_aliasing={{0}: (3, {})} | custom-call | tf_op jit(solution)/shard_map/decode/pallas_call | solution.py:236
  170.2 2.9 %decode.35 = (bf16[3072,2048]{1,0:T(8,128)(2,1)}, f32[8,128]{1,0:T(8,128)}) custom-call(s32[1]{0:T(128)} %bitcast.me_ref, f32[24,1,2048]{2,1,0:T(1,128)S(1)} %get-tuple-element.104.r_ref, bf16[192,2048]{1,0:T(8,128)(2,1)} %collective-permute-done.13.refs_0_, bf16[3072,2048]{1,0:T(8,128)(2,1)} %get-tuple-element.129.refs_1_), custom_call_target="tpu_custom_call", output_to_operand_aliasing={{0}: (3, {})} | custom-call | tf_op jit(solution)/shard_map/decode/pallas_call | solution.py:236
  173.1 1.8 decode.36
  174.9 1.8 decode.39
  176.6 1.8 decode.40
  180.4 1.8 decode.37
  185.6 1.8 collective-permute-start.32
  187.4 1.8 decode.38
  189.2 1.8 decode.41
  191.0 10.0 %collective-permute-done.22 = bf16[192,2048]{1,0:T(8,128)(2,1)S(1)} collective-permute-done((bf16[192,2048]{1,0:T(8,128)(2,1)}, bf16[192,2048]{1,0:T(8,128)(2,1)S(1)}, u32[]{:S(2)}, u32[]{:S(2)}) %collective-permute-start.22) | collective-permute-done | bytes 786464 | tf_op jit(solution)/shard_map/ppermute | solution.py:295
  201.1 1.7 collective-permute-start.29
  204.1 1.8 decode.42
  205.9 1.8 decode.45
  207.6 1.8 decode.46
  209.4 8.4 %collective-permute-done.33 = bf16[192,2048]{1,0:T(8,128)(2,1)S(1)} collective-permute-done((bf16[192,2048]{1,0:T(8,128)(2,1)S(1)}, bf16[192,2048]{1,0:T(8,128)(2,1)S(1)}, u32[]{:S(2)}, u32[]{:S(2)}) %collective-permute-start.33) | collective-permute-done | bytes 786464 | tf_op jit(solution)/shard_map/ppermute | solution.py:295
  219.3 1.8 collective-permute-start.36
  221.1 1.8 decode.43
  222.9 1.8 decode.44
  224.6 10.1 %collective-permute-done.29.refs_0_ = bf16[192,2048]{1,0:T(8,128)(2,1)S(1)} collective-permute-done((bf16[192,2048]{1,0:T(8,128)(2,1)S(1)}, bf16[192,2048]{1,0:T(8,128)(2,1)S(1)}, u32[]{:S(2)}, u32[]{:S(2)}) %collective-permute-start.29) | collective-permute-done | bytes 786464 | tf_op jit(solution)/shard_map/ppermute | solution.py:297
  234.8 2.1 collective-permute-start.35
  236.9 1.8 decode.47
  238.7 1.8 decode.48
  240.9 10.7 %collective-permute-done.37 = bf16[192,2048]{1,0:T(8,128)(2,1)S(1)} collective-permute-done((bf16[192,2048]{1,0:T(8,128)(2,1)S(1)}, bf16[192,2048]{1,0:T(8,128)(2,1)S(1)}, u32[]{:S(2)}, u32[]{:S(2)}) %collective-permute-start.37) | collective-permute-done | bytes 786464 | tf_op jit(solution)/shard_map/ppermute | solution.py:295
  251.6 1.7 collective-permute-start.39
  254.6 1.8 decode.51
  256.4 1.8 decode.52
  258.2 9.7 %collective-permute-done.35.refs_0_ = bf16[192,2048]{1,0:T(8,128)(2,1)S(1)} collective-permute-done((bf16[192,2048]{1,0:T(8,128)(2,1)S(1)}, bf16[192,2048]{1,0:T(8,128)(2,1)S(1)}, u32[]{:S(2)}, u32[]{:S(2)}) %collective-permute-start.35) | collective-permute-done | bytes 786464 | tf_op jit(solution)/shard_map/ppermute | solution.py:295
  267.9 1.8 decode.49
  269.7 1.8 decode.50
  271.4 4.4 %collective-permute-done.39.refs_1_ = bf16[192,2048]{1,0:T(8,128)(2,1)S(1)} collective-permute-done((bf16[192,2048]{1,0:T(8,128)(2,1)S(1)}, bf16[192,2048]{1,0:T(8,128)(2,1)S(1)}, u32[]{:S(2)}, u32[]{:S(2)}) %collective-permute-start.39) | collective-permute-done | bytes 786464 | tf_op jit(solution)/shard_map/ppermute | solution.py:297
  276.3 2.2 decode.53
  (81 shorter events, 29.7 us)
Async XLA Ops:
  2.9 96.6 %copy-start.5 = (f32[384]{0:T(512)S(1)}, f32[384]{0:T(512)}, u32[]{:S(2)}) copy-start(f32[384]{0:T(512)} %g_ref.3) | copy-start | bytes 4612
  3.0 21.1 %collective-permute-start.1 = (bf16[192,2048]{1,0:T(8,128)(2,1)S(1)}, bf16[192,2048]{1,0:T(8,128)(2,1)}, u32[]{:S(2)}, u32[]{:S(2)}) collective-permute-start(bf16[192,2048]{1,0:T(8,128)(2,1)S(1)} %get-tuple-element.97), channel_id=1, source_target_pairs={{0,8},{1,5},{2,10},{3,7},{4,12},{5,1},{6,14},{7,3},{8,0},{9,13},{1... | collective-permute-start | bytes 2359304 | tf_op jit(solution)/shard_map/ppermute | solution.py:340
  6.1 20.5 %collective-permute-start.2 = (bf16[192,2048]{1,0:T(8,128)(2,1)S(1)}, bf16[192,2048]{1,0:T(8,128)(2,1)}, u32[]{:S(2)}, u32[]{:S(2)}) collective-permute-start(bf16[192,2048]{1,0:T(8,128)(2,1)S(1)} %get-tuple-element.97), channel_id=1, source_target_pairs={{0,4},{1,9},{2,6},{3,11},{4,0},{5,13},{6,2},{7,15},{8,12},{9,1},{1... | collective-permute-start | bytes 2359304 | tf_op jit(solution)/shard_map/ppermute | solution.py:340
  7.6 33.8 %collective-permute-start.3 = (bf16[192,2048]{1,0:T(8,128)(2,1)S(1)}, bf16[192,2048]{1,0:T(8,128)(2,1)}, u32[]{:S(2)}, u32[]{:S(2)}) collective-permute-start(bf16[192,2048]{1,0:T(8,128)(2,1)S(1)} %get-tuple-element.97), channel_id=1, source_target_pairs={{8,16},{12,20},{16,8},{20,12},{9,17},{13,21},{17,9},{21,13},{10,18... | collective-permute-start | bytes 2359304 | tf_op jit(solution)/shard_map/ppermute | solution.py:295
  9.1 0.7 copy-start.4
  16.0 0.9 copy-start.6
  16.9 27.6 %collective-permute-start.5 = (bf16[192,2048]{1,0:T(8,128)(2,1)}, bf16[192,2048]{1,0:T(8,128)(2,1)S(1)}, u32[]{:S(2)}, u32[]{:S(2)}) collective-permute-start(bf16[192,2048]{1,0:T(8,128)(2,1)} %get-tuple-element.100), channel_id=1, source_target_pairs={{0,4},{4,0},{8,12},{12,8},{16,20},{20,16},{24,28},{28,24},{1,5},{5... | collective-permute-start | bytes 2359304 | tf_op jit(solution)/shard_map/ppermute | solution.py:297
  17.4 27.8 %collective-permute-start.6 = (bf16[192,2048]{1,0:T(8,128)(2,1)}, bf16[192,2048]{1,0:T(8,128)(2,1)}, u32[]{:S(2)}, u32[]{:S(2)}) collective-permute-start(bf16[192,2048]{1,0:T(8,128)(2,1)} %get-tuple-element.100), channel_id=1, source_target_pairs={{0,8},{4,12},{8,0},{12,4},{16,24},{20,28},{24,16},{28,20},{1,9},{5... | collective-permute-start | bytes 2359304 | tf_op jit(solution)/shard_map/ppermute | solution.py:295
  24.1 25.1 %collective-permute-start.7 = (bf16[192,2048]{1,0:T(8,128)(2,1)}, bf16[192,2048]{1,0:T(8,128)(2,1)S(1)}, u32[]{:S(2)}, u32[]{:S(2)}) collective-permute-start(bf16[192,2048]{1,0:T(8,128)(2,1)} %get-tuple-element.100), channel_id=1, source_target_pairs={{8,16},{12,20},{16,8},{20,12},{9,17},{13,21},{17,9},{21,13},{10,18... | collective-permute-start | bytes 2359304 | tf_op jit(solution)/shard_map/ppermute | solution.py:295
  26.6 14.7 %collective-permute-start = (f32[3,1,2048]{2,1,0:T(1,128)S(1)}, f32[3,1,2048]{2,1,0:T(1,128)S(1)}, u32[]{:S(2)}, u32[]{:S(2)}) collective-permute-start(f32[3,1,2048]{2,1,0:T(1,128)S(1)} %get-tuple-element.96.m0_ref), channel_id=1, source_target_pairs={{0,8},{4,12},{8,0},{12,4},{16,24},{20,28},{24,16},{28,20},{1,9},{5... | collective-permute-start | bytes 73736 | tf_op jit(solution)/shard_map/ppermute | solution.py:295
  41.3 50.1 %collective-permute-start.11 = (bf16[192,2048]{1,0:T(8,128)(2,1)}, bf16[192,2048]{1,0:T(8,128)(2,1)S(1)}, u32[]{:S(2)}, u32[]{:S(2)}) collective-permute-start(bf16[192,2048]{1,0:T(8,128)(2,1)} %get-tuple-element.106), channel_id=1, source_target_pairs={{0,4},{4,0},{8,12},{12,8},{16,20},{20,16},{24,28},{28,24},{1,5},{5... | collective-permute-start | bytes 2359304 | tf_op jit(solution)/shard_map/ppermute | solution.py:297
  42.7 51.1 %collective-permute-start.10 = (bf16[192,2048]{1,0:T(8,128)(2,1)}, bf16[192,2048]{1,0:T(8,128)(2,1)S(1)}, u32[]{:S(2)}, u32[]{:S(2)}) collective-permute-start(bf16[192,2048]{1,0:T(8,128)(2,1)} %get-tuple-element.106), channel_id=1, source_target_pairs={{0,8},{4,12},{8,0},{12,4},{16,24},{20,28},{24,16},{28,20},{1,9},{5... | collective-permute-start | bytes 2359304 | tf_op jit(solution)/shard_map/ppermute | solution.py:295
  44.5 49.4 %collective-permute-start.12 = (bf16[192,2048]{1,0:T(8,128)(2,1)}, bf16[192,2048]{1,0:T(8,128)(2,1)S(1)}, u32[]{:S(2)}, u32[]{:S(2)}) collective-permute-start(bf16[192,2048]{1,0:T(8,128)(2,1)} %get-tuple-element.106), channel_id=1, source_target_pairs={{8,16},{12,20},{16,8},{20,12},{9,17},{13,21},{17,9},{21,13},{10,18... | collective-permute-start | bytes 2359304 | tf_op jit(solution)/shard_map/ppermute | solution.py:295
  45.3 22.9 %collective-permute-start.4 = (f32[6,1,2048]{2,1,0:T(1,128)S(1)}, f32[6,1,2048]{2,1,0:T(1,128)S(1)}, u32[]{:S(2)}, u32[]{:S(2)}) collective-permute-start(f32[6,1,2048]{2,1,0:T(1,128)S(1)} %pad_maximum_fusion), channel_id=1, source_target_pairs={{0,16},{4,20},{16,0},{20,4},{8,24},{12,28},{24,8},{28,12},{1,17},{... | collective-permute-start | bytes 147464 | tf_op jit(solution)/shard_map/ppermute | solution.py:295
  49.1 47.9 %copy-start.9 = (bf16[192,2048]{1,0:T(8,128)(2,1)}, bf16[192,2048]{1,0:T(8,128)(2,1)S(1)}, u32[]{:S(2)}) copy-start(bf16[192,2048]{1,0:T(8,128)(2,1)S(1)} %collective-permute-done.7) | copy-start | bytes 2359300
  68.1 28.9 %collective-permute-start.19 = (bf16[192,2048]{1,0:T(8,128)(2,1)}, bf16[192,2048]{1,0:T(8,128)(2,1)S(1)}, u32[]{:S(2)}, u32[]{:S(2)}) collective-permute-start(bf16[192,2048]{1,0:T(8,128)(2,1)} %copy-done.6), channel_id=1, source_target_pairs={{0,4},{4,0},{8,12},{12,8},{16,20},{20,16},{24,28},{28,24},{1,5},{5... | collective-permute-start | bytes 2359304 | tf_op jit(solution)/shard_map/ppermute | solution.py:297
  69.9 16.9 %collective-permute-start.9 = (f32[2,1,2048]{2,1,0:T(1,128)S(1)}, f32[2,1,2048]{2,1,0:T(1,128)S(1)}, u32[]{:S(2)}, u32[]{:S(2)}) collective-permute-start(f32[2,1,2048]{2,1,0:T(1,128)S(1)} %get-tuple-element.103.most0_ref), channel_id=1, source_target_pairs={{0,4},{4,0},{8,12},{12,8},{16,20},{20,16},{24,28},{28,24},{1,5},{5... | collective-permute-start | bytes 49160 | tf_op jit(solution)/shard_map/ppermute | solution.py:297
  86.8 4.6 %collective-permute-start.8 = (bf16[12,1,2048]{2,1,0:T(2,128)(2,1)S(1)}, bf16[12,1,2048]{2,1,0:T(2,128)(2,1)S(1)}, u32[]{:S(2)}, u32[]{:S(2)}) collective-permute-start(bf16[12,1,2048]{2,1,0:T(2,128)(2,1)S(1)} %get-tuple-element.101.scale0_ref), channel_id=1, source_target_pairs={{0,4},{4,0},{8,12},{12,8},{16,20},{20,16},{24,28},{28,24},{1,5},{5... | collective-permute-start | bytes 147464 | tf_op jit(solution)/shard_map/ppermute | solution.py:297
  91.4 20.7 %collective-permute-start.20 = (bf16[192,2048]{1,0:T(8,128)(2,1)}, bf16[192,2048]{1,0:T(8,128)(2,1)}, u32[]{:S(2)}, u32[]{:S(2)}) collective-permute-start(bf16[192,2048]{1,0:T(8,128)(2,1)} %copy-done.6), channel_id=1, source_target_pairs={{0,8},{4,12},{8,0},{12,4},{16,24},{20,28},{24,16},{28,20},{1,9},{5... | collective-permute-start | bytes 2359304 | tf_op jit(solution)/shard_map/ppermute | solution.py:295
  91.5 0.9 copy-start.2
  92.3 19.8 %collective-permute-start.23 = (bf16[192,2048]{1,0:T(8,128)(2,1)}, bf16[192,2048]{1,0:T(8,128)(2,1)}, u32[]{:S(2)}, u32[]{:S(2)}) collective-permute-start(bf16[192,2048]{1,0:T(8,128)(2,1)} %copy-done.6), channel_id=1, source_target_pairs={{8,16},{12,20},{16,8},{20,12},{9,17},{13,21},{17,9},{21,13},{10,18... | collective-permute-start | bytes 2359304 | tf_op jit(solution)/shard_map/ppermute | solution.py:295
  93.9 3.1 %copy-start.7 = (bf16[192,2048]{1,0:T(8,128)(2,1)}, bf16[192,2048]{1,0:T(8,128)(2,1)S(1)}, u32[]{:S(2)}) copy-start(bf16[192,2048]{1,0:T(8,128)(2,1)S(1)} %collective-permute-done.12) | copy-start | bytes 2359300
  93.9 35.1 %collective-permute-start.14 = (bf16[192,2048]{1,0:T(8,128)(2,1)}, bf16[192,2048]{1,0:T(8,128)(2,1)}, u32[]{:S(2)}, u32[]{:S(2)}) collective-permute-start(bf16[192,2048]{1,0:T(8,128)(2,1)} %collective-permute-done.3), channel_id=1, source_target_pairs={{8,0},{12,4},{16,24},{20,28},{9,1},{13,5},{17,25},{21,29},{10,2},{... | collective-permute-start | bytes 2359304 | tf_op jit(solution)/shard_map/ppermute | solution.py:295
  95.2 42.1 %collective-permute-start.13 = (bf16[192,2048]{1,0:T(8,128)(2,1)S(1)}, bf16[192,2048]{1,0:T(8,128)(2,1)}, u32[]{:S(2)}, u32[]{:S(2)}) collective-permute-start(bf16[192,2048]{1,0:T(8,128)(2,1)S(1)} %collective-permute-done.10.refs_0_), channel_id=1, source_target_pairs={{0,4},{4,0},{8,12},{12,8},{16,20},{20,16},{24,28},{28,24},{1,5},{5... | collective-permute-start | bytes 2359304 | tf_op jit(solution)/shard_map/ppermute | solution.py:297
  97.0 0.9 copy-start
  97.9 39.4 %collective-permute-start.15 = (bf16[192,2048]{1,0:T(8,128)(2,1)S(1)}, bf16[192,2048]{1,0:T(8,128)(2,1)}, u32[]{:S(2)}, u32[]{:S(2)}) collective-permute-start(bf16[192,2048]{1,0:T(8,128)(2,1)S(1)} %get-tuple-element.109.refs_0_), channel_id=1, source_target_pairs={{8,16},{12,20},{16,8},{20,12},{9,17},{13,21},{17,9},{21,13},{10,18... | collective-permute-start | bytes 2359304 | tf_op jit(solution)/shard_map/ppermute | solution.py:295
  99.5 12.7 %copy-start.10 = (bf16[192,2048]{1,0:T(8,128)(2,1)S(1)}, bf16[192,2048]{1,0:T(8,128)(2,1)}, u32[]{:S(2)}) copy-start(bf16[192,2048]{1,0:T(8,128)(2,1)} %copy-done.9) | copy-start | bytes 2359300
  112.2 33.3 %collective-permute-start.24 = (bf16[192,2048]{1,0:T(8,128)(2,1)S(1)}, bf16[192,2048]{1,0:T(8,128)(2,1)S(1)}, u32[]{:S(2)}, u32[]{:S(2)}) collective-permute-start(bf16[192,2048]{1,0:T(8,128)(2,1)S(1)} %copy-done.10), channel_id=1, source_target_pairs={{8,0},{12,4},{16,24},{20,28},{9,1},{13,5},{17,25},{21,29},{10,2},{... | collective-permute-start | bytes 2359304 | tf_op jit(solution)/shard_map/ppermute | solution.py:295
  113.5 32.7 %collective-permute-start.26 = (bf16[192,2048]{1,0:T(8,128)(2,1)}, bf16[192,2048]{1,0:T(8,128)(2,1)S(1)}, u32[]{:S(2)}, u32[]{:S(2)}) collective-permute-start(bf16[192,2048]{1,0:T(8,128)(2,1)} %collective-permute-done.6.refs_0_), channel_id=1, source_target_pairs={{8,16},{12,20},{16,8},{20,12},{9,17},{13,21},{17,9},{21,13},{10,18... | collective-permute-start | bytes 2359304 | tf_op jit(solution)/shard_map/ppermute | solution.py:295
  129.0 19.6 %collective-permute-start.25 = (bf16[192,2048]{1,0:T(8,128)(2,1)}, bf16[192,2048]{1,0:T(8,128)(2,1)S(1)}, u32[]{:S(2)}, u32[]{:S(2)}) collective-permute-start(bf16[192,2048]{1,0:T(8,128)(2,1)} %collective-permute-done.20.refs_0_), channel_id=1, source_target_pairs={{0,4},{4,0},{8,12},{12,8},{16,20},{20,16},{24,28},{28,24},{1,5},{5... | collective-permute-start | bytes 2359304 | tf_op jit(solution)/shard_map/ppermute | solution.py:297
  134.3 6.3 %copy-start.3 = (bf16[192,2048]{1,0:T(8,128)(2,1)S(1)}, bf16[192,2048]{1,0:T(8,128)(2,1)}, u32[]{:S(2)}) copy-start(bf16[192,2048]{1,0:T(8,128)(2,1)} %copy-done.2) | copy-start | bytes 2359300
  137.3 26.5 %collective-permute-start.18 = (bf16[192,2048]{1,0:T(8,128)(2,1)S(1)}, bf16[192,2048]{1,0:T(8,128)(2,1)S(1)}, u32[]{:S(2)}, u32[]{:S(2)}) collective-permute-start(bf16[192,2048]{1,0:T(8,128)(2,1)S(1)} %broadcast_select_fusion.6.refs_0_), channel_id=1, source_target_pairs={{0,4},{4,0},{8,12},{12,8},{16,20},{20,16},{24,28},{28,24},{1,5},{5... | collective-permute-start | bytes 2359304 | tf_op jit(solution)/shard_map/ppermute | solution.py:297
  140.6 3.6 %copy-start.8 = (bf16[192,2048]{1,0:T(8,128)(2,1)S(1)}, bf16[192,2048]{1,0:T(8,128)(2,1)}, u32[]{:S(2)}) copy-start(bf16[192,2048]{1,0:T(8,128)(2,1)} %copy-done.7) | copy-start | bytes 2359300
  140.6 24.9 %copy-start.1 = (bf16[192,2048]{1,0:T(8,128)(2,1)S(1)}, bf16[192,2048]{1,0:T(8,128)(2,1)}, u32[]{:S(2)}) copy-start(bf16[192,2048]{1,0:T(8,128)(2,1)} %copy-done) | copy-start | bytes 2359300
  144.2 34.3 %collective-permute-start.17 = (bf16[192,2048]{1,0:T(8,128)(2,1)S(1)}, bf16[192,2048]{1,0:T(8,128)(2,1)S(1)}, u32[]{:S(2)}, u32[]{:S(2)}) collective-permute-start(bf16[192,2048]{1,0:T(8,128)(2,1)S(1)} %copy-done.8), channel_id=1, source_target_pairs={{8,0},{12,4},{16,24},{20,28},{9,1},{13,5},{17,25},{21,29},{10,2},{... | collective-permute-start | bytes 2359304 | tf_op jit(solution)/shard_map/ppermute | solution.py:295
  145.5 33.0 %collective-permute-start.16 = (bf16[192,2048]{1,0:T(8,128)(2,1)S(1)}, bf16[192,2048]{1,0:T(8,128)(2,1)S(1)}, u32[]{:S(2)}, u32[]{:S(2)}) collective-permute-start(bf16[192,2048]{1,0:T(8,128)(2,1)S(1)} %collective-permute-done.10.refs_0_), channel_id=1, source_target_pairs={{8,16},{12,20},{16,8},{20,12},{9,17},{13,21},{17,9},{21,13},{10,18... | collective-permute-start | bytes 2359304 | tf_op jit(solution)/shard_map/ppermute | solution.py:295
  148.6 33.5 %collective-permute-start.31 = (bf16[192,2048]{1,0:T(8,128)(2,1)}, bf16[192,2048]{1,0:T(8,128)(2,1)S(1)}, u32[]{:S(2)}, u32[]{:S(2)}) collective-permute-start(bf16[192,2048]{1,0:T(8,128)(2,1)} %collective-permute-done.20.refs_0_), channel_id=1, source_target_pairs={{8,16},{12,20},{16,8},{20,12},{9,17},{13,21},{17,9},{21,13},{10,18... | collective-permute-start | bytes 2359304 | tf_op jit(solution)/shard_map/ppermute | solution.py:295
  149.4 34.0 %collective-permute-start.30 = (bf16[192,2048]{1,0:T(8,128)(2,1)}, bf16[192,2048]{1,0:T(8,128)(2,1)S(1)}, u32[]{:S(2)}, u32[]{:S(2)}) collective-permute-start(bf16[192,2048]{1,0:T(8,128)(2,1)} %collective-permute-done.23), channel_id=1, source_target_pairs={{8,0},{12,4},{16,24},{20,28},{9,1},{13,5},{17,25},{21,29},{10,2},{... | collective-permute-start | bytes 2359304 | tf_op jit(solution)/shard_map/ppermute | solution.py:295
  163.8 20.4 %collective-permute-start.27 = (bf16[192,2048]{1,0:T(8,128)(2,1)S(1)}, bf16[192,2048]{1,0:T(8,128)(2,1)S(1)}, u32[]{:S(2)}, u32[]{:S(2)}) collective-permute-start(bf16[192,2048]{1,0:T(8,128)(2,1)S(1)} %broadcast_select_fusion.5.refs_0_), channel_id=1, source_target_pairs={{0,4},{4,0},{8,12},{12,8},{16,20},{20,16},{24,28},{28,24},{1,5},{5... | collective-permute-start | bytes 2359304 | tf_op jit(solution)/shard_map/ppermute | solution.py:297
  178.4 22.5 %collective-permute-start.22 = (bf16[192,2048]{1,0:T(8,128)(2,1)}, bf16[192,2048]{1,0:T(8,128)(2,1)S(1)}, u32[]{:S(2)}, u32[]{:S(2)}) collective-permute-start(bf16[192,2048]{1,0:T(8,128)(2,1)} %collective-permute-done.15), channel_id=1, source_target_pairs={{8,0},{12,4},{16,24},{20,28},{9,1},{13,5},{17,25},{21,29},{10,2},{... | collective-permute-start | bytes 2359304 | tf_op jit(solution)/shard_map/ppermute | solution.py:295
  180.0 21.1 %collective-permute-start.21 = (bf16[192,2048]{1,0:T(8,128)(2,1)S(1)}, bf16[192,2048]{1,0:T(8,128)(2,1)S(1)}, u32[]{:S(2)}, u32[]{:S(2)}) collective-permute-start(bf16[192,2048]{1,0:T(8,128)(2,1)S(1)} %broadcast_select_fusion.7.refs_0_), channel_id=1, source_target_pairs={{0,4},{4,0},{8,12},{12,8},{16,20},{20,16},{24,28},{28,24},{1,5},{5... | collective-permute-start | bytes 2359304 | tf_op jit(solution)/shard_map/ppermute | solution.py:297
  184.2 33.6 %collective-permute-start.33 = (bf16[192,2048]{1,0:T(8,128)(2,1)S(1)}, bf16[192,2048]{1,0:T(8,128)(2,1)S(1)}, u32[]{:S(2)}, u32[]{:S(2)}) collective-permute-start(bf16[192,2048]{1,0:T(8,128)(2,1)S(1)} %collective-permute-done.26), channel_id=1, source_target_pairs={{8,0},{12,4},{16,24},{20,28},{9,1},{13,5},{17,25},{21,29},{10,2},{... | collective-permute-start | bytes 2359304 | tf_op jit(solution)/shard_map/ppermute | solution.py:295
  185.6 32.3 %collective-permute-start.32 = (bf16[192,2048]{1,0:T(8,128)(2,1)S(1)}, bf16[192,2048]{1,0:T(8,128)(2,1)S(1)}, u32[]{:S(2)}, u32[]{:S(2)}) collective-permute-start(bf16[192,2048]{1,0:T(8,128)(2,1)S(1)} %broadcast_select_fusion.2.refs_0_), channel_id=1, source_target_pairs={{0,4},{4,0},{8,12},{12,8},{16,20},{20,16},{24,28},{28,24},{1,5},{5... | collective-permute-start | bytes 2359304 | tf_op jit(solution)/shard_map/ppermute | solution.py:297
  201.1 33.7 %collective-permute-start.29 = (bf16[192,2048]{1,0:T(8,128)(2,1)S(1)}, bf16[192,2048]{1,0:T(8,128)(2,1)S(1)}, u32[]{:S(2)}, u32[]{:S(2)}) collective-permute-start(bf16[192,2048]{1,0:T(8,128)(2,1)S(1)} %broadcast_select_fusion.3.refs_0_), channel_id=1, source_target_pairs={{0,4},{4,0},{8,12},{12,8},{16,20},{20,16},{24,28},{28,24},{1,5},{5... | collective-permute-start | bytes 2359304 | tf_op jit(solution)/shard_map/ppermute | solution.py:297
  202.8 32.0 %collective-permute-start.28 = (bf16[192,2048]{1,0:T(8,128)(2,1)S(1)}, bf16[192,2048]{1,0:T(8,128)(2,1)S(1)}, u32[]{:S(2)}, u32[]{:S(2)}) collective-permute-start(bf16[192,2048]{1,0:T(8,128)(2,1)S(1)} %collective-permute-done.16), channel_id=1, source_target_pairs={{8,0},{12,4},{16,24},{20,28},{9,1},{13,5},{17,25},{21,29},{10,2},{... | collective-permute-start | bytes 2359304 | tf_op jit(solution)/shard_map/ppermute | solution.py:295
  217.9 33.6 %collective-permute-start.37 = (bf16[192,2048]{1,0:T(8,128)(2,1)S(1)}, bf16[192,2048]{1,0:T(8,128)(2,1)S(1)}, u32[]{:S(2)}, u32[]{:S(2)}) collective-permute-start(bf16[192,2048]{1,0:T(8,128)(2,1)S(1)} %collective-permute-done.31), channel_id=1, source_target_pairs={{8,0},{12,4},{16,24},{20,28},{9,1},{13,5},{17,25},{21,29},{10,2},{... | collective-permute-start | bytes 2359304 | tf_op jit(solution)/shard_map/ppermute | solution.py:295
  219.3 32.3 %collective-permute-start.36 = (bf16[192,2048]{1,0:T(8,128)(2,1)S(1)}, bf16[192,2048]{1,0:T(8,128)(2,1)S(1)}, u32[]{:S(2)}, u32[]{:S(2)}) collective-permute-start(bf16[192,2048]{1,0:T(8,128)(2,1)S(1)} %broadcast_select_fusion.1.refs_0_), channel_id=1, source_target_pairs={{0,4},{4,0},{8,12},{12,8},{16,20},{20,16},{24,28},{28,24},{1,5},{5... | collective-permute-start | bytes 2359304 | tf_op jit(solution)/shard_map/ppermute | solution.py:297
  234.8 33.1 %collective-permute-start.35 = (bf16[192,2048]{1,0:T(8,128)(2,1)S(1)}, bf16[192,2048]{1,0:T(8,128)(2,1)S(1)}, u32[]{:S(2)}, u32[]{:S(2)}) collective-permute-start(bf16[192,2048]{1,0:T(8,128)(2,1)S(1)} %get-tuple-element.165.refs_0_), channel_id=1, source_target_pairs={{0,8},{4,12},{8,0},{12,4},{16,24},{20,28},{24,16},{28,20},{1,9},{5... | collective-permute-start | bytes 2359304 | tf_op jit(solution)/shard_map/ppermute | solution.py:295
  240.5 29.1 %collective-permute-start.34 = (bf16[192,2048]{1,0:T(8,128)(2,1)S(1)}, bf16[192,2048]{1,0:T(8,128)(2,1)S(1)}, u32[]{:S(2)}, u32[]{:S(2)}) collective-permute-start(bf16[192,2048]{1,0:T(8,128)(2,1)S(1)} %broadcast_select_fusion.4.refs_0_), channel_id=1, source_target_pairs={{0,4},{4,0},{8,12},{12,8},{16,20},{20,16},{24,28},{28,24},{1,5},{5... | collective-permute-start | bytes 2359304 | tf_op jit(solution)/shard_map/ppermute | solution.py:297
  251.6 24.2 %collective-permute-start.39 = (bf16[192,2048]{1,0:T(8,128)(2,1)S(1)}, bf16[192,2048]{1,0:T(8,128)(2,1)S(1)}, u32[]{:S(2)}, u32[]{:S(2)}) collective-permute-start(bf16[192,2048]{1,0:T(8,128)(2,1)S(1)} %broadcast_select_fusion.refs_0_), channel_id=1, source_target_pairs={{0,4},{4,0},{8,12},{12,8},{16,20},{20,16},{24,28},{28,24},{1,5},{5... | collective-permute-start | bytes 2359304 | tf_op jit(solution)/shard_map/ppermute | solution.py:297
  253.4 22.9 %collective-permute-start.38 = (bf16[192,2048]{1,0:T(8,128)(2,1)S(1)}, bf16[192,2048]{1,0:T(8,128)(2,1)S(1)}, u32[]{:S(2)}, u32[]{:S(2)}) collective-permute-start(bf16[192,2048]{1,0:T(8,128)(2,1)S(1)} %collective-permute-done.5.refs_0_), channel_id=1, source_target_pairs={{0,8},{4,12},{8,0},{12,4},{16,24},{20,28},{24,16},{28,20},{1,9},{5... | collective-permute-start | bytes 2359304 | tf_op jit(solution)/shard_map/ppermute | solution.py:295

commit v3 on v2

--- a/solution.py
+++ b/solution.py
@@ -127,41 +127,10 @@
     )(stay_out(gain), stay_out(w), stay_out(avg))
 
 
-def own_body(me_ref, wg_ref, ag_ref, wu_ref, au_ref, g_ref, f_ref, og_ref, ou_ref, token_ref):
-    del me_ref
-    gain = tall_gain(g_ref, wg_ref.shape[1])
-    og_ref[...] = (gained(wg_ref, ag_ref, gain) / f_ref[0:1, :]).astype(jnp.bfloat16)
-    ou_ref[...] = (gained(wu_ref, au_ref, gain) / f_ref[1:2, :]).astype(jnp.bfloat16)
-    token_ref[...] = jnp.zeros_like(token_ref)
-
-
-def own_share(me, shards, w_gate, avg_gate, w_up, avg_up, gain, factors, block):
-    rows, columns = w_gate.shape
-    tile = pl.BlockSpec((rows, block), lambda j, me: (0, j))
-    landed = pl.BlockSpec((rows, block), lambda j, me: (me[0], j))
-    out = jax.ShapeDtypeStruct((rows * shards, columns), jnp.bfloat16)
-    return pl.pallas_call(
-        own_body,
-        grid_spec=pltpu.PrefetchScalarGridSpec(
-            num_scalar_prefetch=1,
-            grid=(columns // block,),
-            in_specs=[tile] * 4
-            + [
-                pl.BlockSpec(gain.shape, lambda j, me: (0,)),
-                pl.BlockSpec((2, block), lambda j, me: (0, j)),
-            ],
-            out_specs=[landed, landed, pl.BlockSpec((8, 128), lambda j, me: (0, 0))],
-        ),
-        out_shape=[out, out, jax.ShapeDtypeStruct((8, 128), jnp.float32)],
-        compiler_params=pltpu.CompilerParams(vmem_limit_bytes=KERNEL_VMEM),
-        name="own_share",
-    )(me, *map(stay_out, (w_gate, avg_gate, w_up, avg_up)), gain, factors)
-
-
 def half_table_body(m0_ref, m1_ref, m2_ref, scale_ref, most_ref):
     rows = [ref[i] for ref in (m0_ref, m1_ref, m2_ref) for i in range(ref.shape[0])]
-    for i, row in enumerate(rows):
-        scale_ref[i] = row.astype(jnp.bfloat16)
+    rest = [jnp.zeros_like(rows[0])] * (scale_ref.shape[0] - len(rows))
+    scale_ref[...] = jnp.concatenate(rows + rest, axis=0).astype(jnp.bfloat16)
     most_ref[0] = functools.reduce(jnp.maximum, rows[0::3] + rows[2::3])
     most_ref[1] = functools.reduce(jnp.maximum, rows[1::3])
 
@@ -171,7 +140,7 @@
     return pl.pallas_call(
         half_table_body,
         out_shape=[
-            pltpu.VMEM((12, 1, columns), jnp.bfloat16),
+            pltpu.VMEM((16, columns), jnp.bfloat16),
             pltpu.VMEM((2, 1, columns), jnp.float32),
         ],
         compiler_params=pltpu.CompilerParams(vmem_limit_bytes=KERNEL_VMEM),
@@ -184,9 +153,10 @@
         factor = jnp.maximum(most0_ref[t], most1_ref[t])
         factor_ref[t : t + 1, :] = factor
         for side, scale_ref in enumerate((scale0_ref, scale1_ref)):
+            scales = scale_ref[...].astype(jnp.float32)
             for place in range(4):
-                for k in (0, 2) if t == 0 else (1,):
-                    ratio_ref[3 * (2 * place + side) + k] = scale_ref[3 * place + k].astype(jnp.float32) / factor
+                for k in (3 * place, 3 * place + 2) if t == 0 else (3 * place + 1,):
+                    ratio_ref[3 * place + 3 * side + k] = scales[k : k + 1] / factor
 
 
 def ratios_of(scales, most):
@@ -210,7 +180,7 @@
 
 def decode_body(me_ref, r_ref, *refs, places, pieces):
     count = len(places)
-    chunks, (out_ref, token_ref, buffer, sems) = refs[:count], refs[count + 1 :]
+    chunks, (out_ref, token_ref, buffer, sems) = refs[:count], refs[-4:]
     rows = chunks[0].shape[0] // pieces
     me = me_ref[0]
     copies = []
@@ -233,9 +203,10 @@
 def decode(whole, chunks, ratios, me, places, pieces=4):
     here = pl.BlockSpec(memory_space=pltpu.VMEM)
     there = pl.BlockSpec(memory_space=pl.ANY)
+    begun = not isinstance(whole, jax.ShapeDtypeStruct)
     return pl.pallas_call(
         functools.partial(decode_body, places=places, pieces=pieces),
-        in_specs=[pl.BlockSpec(memory_space=pltpu.SMEM), here] + [here] * len(chunks) + [there],
+        in_specs=[pl.BlockSpec(memory_space=pltpu.SMEM), here] + [here] * len(chunks) + [there] * begun,
         out_specs=[there, here],
         out_shape=[
             jax.ShapeDtypeStruct(whole.shape, whole.dtype),
@@ -245,16 +216,20 @@
             pltpu.VMEM((len(chunks), *chunks[0].shape), whole.dtype),
             pltpu.SemaphoreType.DMA((len(chunks), pieces)),
         ],
-        input_output_aliases={2 + len(chunks): 0},
+        input_output_aliases={2 + len(chunks): 0} if begun else {},
         compiler_params=pltpu.CompilerParams(vmem_limit_bytes=KERNEL_VMEM),
         name="decode",
-    )(me, near_by(ratios), *map(near_by, chunks), whole)
+    )(me, near_by(ratios), *map(near_by, chunks), *[whole] * begun)
 
 
 def after(value, *tokens):
     return lax.optimization_barrier((value, *tokens))[0]
 
 
+def own_of(me):
+    return me
+
+
 def across_of(me):
     return me ^ 1
 
@@ -284,7 +259,8 @@
 
 
 def local_plane(w_gate, avg_gate, w_up, avg_up, norm_gain):
-    block = min(w_gate.shape[1], 1024)
+    rows, columns = w_gate.shape
+    block = min(columns, 1024)
     width = lax.axis_size("width")
     index = lax.axis_index("rows")
     outer = (index < 2) | (index >= 6)
@@ -394,8 +370,9 @@
         if k + 2 < 14:
             send(k + 2, *got, *tokens)
         if k == 2:
-            *wholes, token = own_share(me, 8, w_gate, avg_gate, w_up, avg_up, norm_gain, factors, block // 2)
-            tokens = [token]
+            out = jax.ShapeDtypeStruct((8 * rows, columns), jnp.bfloat16)
+            wholes, tokens = zip(*[decode(out, own[t::2], ratios, me, [(own_of, t), (own_of, t + 2)]) for t in (0, 1)])
+            wholes = list(wholes)
         if k >= 3:
             tokens = settle(3 if k < 13 else len(waiting) - 2)
     chunks, shards_of, cs = zip(*waiting)

time: 280 us -> 264 us (0.943)
  waiting for transfers between devices: 145 us -> 123 us
  local copies, waits for them, and re-layouts: 3.96 us -> 6.93 us
    ppermute x23, waiting for transfers between devices: 89.7 us -> 77 us  [hop(): return lax.ppermute(value, 'rows', both)]
    pallas_call x27 -> x29, Pallas kernels: 51.3 us -> 60.3 us  [decode(): pl.pallas_call(functools.partial(decode_body, places=places, pieces=piece...]
    pallas_call x2 -> x1, Pallas kernels: 7.06 us -> 0.05 us  [half_table(): pl.pallas_call(half_table_body, out_shape=[pltpu.VMEM((16, columns), jnp....]
    ppermute x15, waiting for transfers between devices: 50.6 us -> 44.5 us  [local_plane(): lax.ppermute(value, 'rows', [(i, i ^ 1) for i in range(8)])]
    ppermute x2, waiting for transfers between devices: 4.93 us -> 1.41 us  [send_first(): lax.ppermute(first, ('rows', 'width'), [(flat(r, c), flat(r ^ (1 if (c +...]
    ppermute x23, starting transfers between devices: 34 us -> 37.2 us  [hop(): return lax.ppermute(value, 'rows', both)]
    unnamed x22 -> x26, local copies, waits for them, and re-layouts: 3.35 us -> 6.31 us
  transfers between devices with their start and end apart: 40 -> 40, of which waited for: 20 -> 18; matrix products, arithmetic and copies ran while one was open for 1% -> 2% of each run, Pallas kernels for 22% -> 24%
where the time goes in v3:
time: 264 us; the launch traced here: 263 us
  waiting for transfers between devices  123 us (47%)
  Pallas kernels  69 us (26%)
  starting transfers between devices  58.7 us (22%)
  local copies, waits for them, and re-layouts  6.93 us (3%)
  other arithmetic  4.48 us (2%)
    ppermute x23, waiting for transfers between devices, hop(): return lax.ppermute(value, 'rows', both)  77 us
    pallas_call x29, Pallas kernels, decode(): pl.pallas_call(functools.partial(decode_body, places=places, pieces=piece...  60.3 us
    ppermute x15, waiting for transfers between devices, local_plane(): lax.ppermute(value, 'rows', [(i, i ^ 1) for i in range(8)])  44.5 us
    ppermute x23, starting transfers between devices, hop(): return lax.ppermute(value, 'rows', both)  37.2 us
    ppermute x15, starting transfers between devices, local_plane(): lax.ppermute(value, 'rows', [(i, i ^ 1) for i in range(8)])  16.9 us
    unnamed x26, local copies, waits for them, and re-layouts  6.31 us
    pallas_call x1, Pallas kernels, encode_rest(): pl.pallas_call(encode_rest_body, grid=(columns // block,), in_specs=[pl.B...  6.18 us
  transfers between devices with their start and end apart: 40, of which 18 were waited for; matrix products, arithmetic and copies ran while one was open for 2% of the time, Pallas kernels for 24%

profile of v3, /device:TPU:0, one launch (start us, length us, event | category | flops | bytes accessed | tf_op | source)
XLA Modules:
  0.0 263.4 jit_solution(8781575104507066922)
XLA Ops:
  0.6 2.3 encode_first.1
  2.9 3.0 %collective-permute-start.2 = (bf16[192,2048]{1,0:T(8,128)(2,1)S(1)}, bf16[192,2048]{1,0:T(8,128)(2,1)S(1)}, u32[]{:S(2)}, u32[]{:S(2)}) collective-permute-start(bf16[192,2048]{1,0:T(8,128)(2,1)S(1)} %get-tuple-element.98.refs_0_), channel_id=1, source_target_pairs={{0,4},{1,9},{2,6},{3,11},{4,0},{5,13},{6,2},{7,15},{8,12},{9,1},{1... | collective-permute-start | bytes 2359304 | tf_op jit(solution)/shard_map/ppermute | solution.py:316
  6.0 1.6 collective-permute-start.1
  7.5 1.5 collective-permute-start.3
  9.8 6.2 %encode_rest.1 = (bf16[192,2048]{1,0:T(8,128)(2,1)}, bf16[192,2048]{1,0:T(8,128)(2,1)S(1)}, bf16[192,2048]{1,0:T(8,128)(2,1)S(1)}, f32[3,1,2048]{2,1,0:T(1,128)S(1)}) custom-call(f32[384]{0:T(512)S(1)} %copy-done.6, f32[384,2048]{1,0:T(8,128)} %wu1.1, f32[384,2048]{1,0:T(8,128)} %au1.1, f32[384,2048]{1,0:T(8,128)} %wg.1, f32[384,2048]{1,0:T(8,128)} %ag.1, ...), custom_call_target="tpu_custom_call" | custom-call | tf_op jit(solution)/shard_map/encode_rest/pallas_call | solution.py:73
  16.8 1.5 collective-permute-start.7
  18.4 4.0 %collective-permute-start.6 = (bf16[192,2048]{1,0:T(8,128)(2,1)}, bf16[192,2048]{1,0:T(8,128)(2,1)}, u32[]{:S(2)}, u32[]{:S(2)}) collective-permute-start(bf16[192,2048]{1,0:T(8,128)(2,1)} %get-tuple-element.101.refs_0_), channel_id=1, source_target_pairs={{0,8},{4,12},{8,0},{12,4},{16,24},{20,28},{24,16},{28,20},{1,9},{5... | collective-permute-start | bytes 2359304 | tf_op jit(solution)/shard_map/ppermute | solution.py:271
  22.3 1.4 collective-permute-done.2
  23.7 2.5 collective-permute-start.5
  27.9 1.5 broadcast_select_fusion.8
  29.4 11.6 %collective-permute-done.m1_ref = f32[3,1,2048]{2,1,0:T(1,128)S(1)} collective-permute-done((f32[3,1,2048]{2,1,0:T(1,128)S(1)}, f32[3,1,2048]{2,1,0:T(1,128)S(1)}, u32[]{:S(2)}, u32[]{:S(2)}) %collective-permute-start) | collective-permute-done | bytes 24608 | tf_op jit(solution)/shard_map/ppermute | solution.py:271
  41.7 1.7 collective-permute-start.11
  43.4 4.3 %collective-permute-start.10 = (bf16[192,2048]{1,0:T(8,128)(2,1)}, bf16[192,2048]{1,0:T(8,128)(2,1)}, u32[]{:S(2)}, u32[]{:S(2)}) collective-permute-start(bf16[192,2048]{1,0:T(8,128)(2,1)} %copy-done), channel_id=1, source_target_pairs={{0,8},{4,12},{8,0},{12,4},{16,24},{20,28},{24,16},{28,20},{1,9},{5... | collective-permute-start | bytes 2359304 | tf_op jit(solution)/shard_map/ppermute | solution.py:271
  48.9 15.5 %collective-permute-done.4.m2_ref = f32[6,1,2048]{2,1,0:T(1,128)S(1)} collective-permute-done((f32[6,1,2048]{2,1,0:T(1,128)S(1)}, f32[6,1,2048]{2,1,0:T(1,128)S(1)}, u32[]{:S(2)}, u32[]{:S(2)}) %collective-permute-start.4) | collective-permute-done | bytes 49184 | tf_op jit(solution)/shard_map/ppermute | solution.py:271
  66.3 2.7 %collective-permute-done.9.most1_ref = f32[2,1,2048]{2,1,0:T(1,128)S(1)} collective-permute-done((f32[2,1,2048]{2,1,0:T(1,128)S(1)}, f32[2,1,2048]{2,1,0:T(1,128)S(1)}, u32[]{:S(2)}, u32[]{:S(2)}) %collective-permute-start.9) | collective-permute-done | bytes 16416 | tf_op jit(solution)/shard_map/ppermute | solution.py:273
  70.0 3.2 %collective-permute-done.8.scale1_ref = bf16[16,2048]{1,0:T(8,128)(2,1)S(1)} collective-permute-done((bf16[16,2048]{1,0:T(8,128)(2,1)S(1)}, bf16[16,2048]{1,0:T(8,128)(2,1)S(1)}, u32[]{:S(2)}, u32[]{:S(2)}) %collective-permute-start.8) | collective-permute-done | bytes 65568 | tf_op jit(solution)/shard_map/ppermute | solution.py:273
  73.2 5.4 %collective-permute-start.20 = (bf16[192,2048]{1,0:T(8,128)(2,1)S(1)}, bf16[192,2048]{1,0:T(8,128)(2,1)}, u32[]{:S(2)}, u32[]{:S(2)}) collective-permute-start(bf16[192,2048]{1,0:T(8,128)(2,1)S(1)} %get-tuple-element.121.refs_1_), channel_id=1, source_target_pairs={{0,8},{4,12},{8,0},{12,4},{16,24},{20,28},{24,16},{28,20},{1,9},{5... | collective-permute-start | bytes 2359304 | tf_op jit(solution)/shard_map/ppermute | solution.py:271
  83.8 1.6 collective-permute-start.15
  86.6 2.2 decode.29
  88.8 3.4 %decode.32 = (bf16[3072,2048]{1,0:T(8,128)(2,1)}, f32[8,128]{1,0:T(8,128)}) custom-call(s32[1]{0:T(128)} %bitcast.me_ref, f32[24,1,2048]{2,1,0:T(1,128)S(1)} %get-tuple-element.105.r_ref, bf16[192,2048]{1,0:T(8,128)(2,1)} %get-tuple-element.101.refs_0_, bf16[192,2048]{1,0:T(8,128)(2,1)S(1)} %get-tuple-element.121.refs_1_), custom_call_target="tpu_custom_call" | custom-call | tf_op jit(solution)/shard_map/decode/pallas_call | solution.py:207
  92.2 4.9 %collective-permute-done.20.refs_0_ = bf16[192,2048]{1,0:T(8,128)(2,1)} collective-permute-done((bf16[192,2048]{1,0:T(8,128)(2,1)S(1)}, bf16[192,2048]{1,0:T(8,128)(2,1)}, u32[]{:S(2)}, u32[]{:S(2)}) %collective-permute-start.20) | collective-permute-done | bytes 786464 | tf_op jit(solution)/shard_map/ppermute | solution.py:271
  97.2 2.0 collective-permute-done.19.refs_0_
  99.2 1.3 collective-permute-start.24
  101.5 14.5 %collective-permute-done.13.refs_0_ = bf16[192,2048]{1,0:T(8,128)(2,1)} collective-permute-done((bf16[192,2048]{1,0:T(8,128)(2,1)}, bf16[192,2048]{1,0:T(8,128)(2,1)}, u32[]{:S(2)}, u32[]{:S(2)}) %collective-permute-start.13) | collective-permute-done | bytes 786464 | tf_op jit(solution)/shard_map/ppermute | solution.py:273
  116.0 1.6 collective-permute-start.26
  117.6 1.8 decode.30
  119.4 1.8 decode.31
  121.2 1.8 decode.33
  122.9 2.9 %decode.34 = (bf16[3072,2048]{1,0:T(8,128)(2,1)}, f32[8,128]{1,0:T(8,128)}) custom-call(s32[1]{0:T(128)} %bitcast.me_ref, f32[24,1,2048]{2,1,0:T(1,128)S(1)} %get-tuple-element.105.r_ref, bf16[192,2048]{1,0:T(8,128)(2,1)} %collective-permute-done.6.refs_0_, bf16[3072,2048]{1,0:T(8,128)(2,1)} %get-tuple-element.122.refs_1_), custom_call_target="tpu_custom_call", output_to_operand_aliasing={{0}: (3, {})} | custom-call | tf_op jit(solution)/shard_map/decode/pallas_call | solution.py:207
  125.9 1.8 decode.37
  127.6 2.9 %decode.38 = (bf16[3072,2048]{1,0:T(8,128)(2,1)}, f32[8,128]{1,0:T(8,128)}) custom-call(s32[1]{0:T(128)} %bitcast.me_ref, f32[24,1,2048]{2,1,0:T(1,128)S(1)} %get-tuple-element.105.r_ref, bf16[192,2048]{1,0:T(8,128)(2,1)} %collective-permute-done.10.refs_0_, bf16[3072,2048]{1,0:T(8,128)(2,1)} %get-tuple-element.128.refs_1_), custom_call_target="tpu_custom_call", output_to_operand_aliasing={{0}: (3, {})} | custom-call | tf_op jit(solution)/shard_map/decode/pallas_call | solution.py:207
  132.5 1.3 collective-permute-start.17
  139.4 2.9 %decode.35 = (bf16[3072,2048]{1,0:T(8,128)(2,1)}, f32[8,128]{1,0:T(8,128)}) custom-call(s32[1]{0:T(128)} %bitcast.me_ref, f32[24,1,2048]{2,1,0:T(1,128)S(1)} %get-tuple-element.105.r_ref, bf16[192,2048]{1,0:T(8,128)(2,1)} %collective-permute-done.19.refs_0_, bf16[3072,2048]{1,0:T(8,128)(2,1)} %get-tuple-element.123.refs_1_), custom_call_target="tpu_custom_call", output_to_operand_aliasing={{0}: (3, {})} | custom-call | tf_op jit(solution)/shard_map/decode/pallas_call | solution.py:207
  142.3 2.9 %decode.36 = (bf16[3072,2048]{1,0:T(8,128)(2,1)}, f32[8,128]{1,0:T(8,128)}) custom-call(s32[1]{0:T(128)} %bitcast.me_ref, f32[24,1,2048]{2,1,0:T(1,128)S(1)} %get-tuple-element.105.r_ref, bf16[192,2048]{1,0:T(8,128)(2,1)} %collective-permute-done.20.refs_0_, bf16[3072,2048]{1,0:T(8,128)(2,1)} %get-tuple-element.125.refs_1_), custom_call_target="tpu_custom_call", output_to_operand_aliasing={{0}: (3, {})} | custom-call | tf_op jit(solution)/shard_map/decode/pallas_call | solution.py:207
  145.2 2.9 %decode.39 = (bf16[3072,2048]{1,0:T(8,128)(2,1)}, f32[8,128]{1,0:T(8,128)}) custom-call(s32[1]{0:T(128)} %bitcast.me_ref, f32[24,1,2048]{2,1,0:T(1,128)S(1)} %get-tuple-element.105.r_ref, bf16[192,2048]{1,0:T(8,128)(2,1)} %collective-permute-done.13.refs_0_, bf16[3072,2048]{1,0:T(8,128)(2,1)} %get-tuple-element.129.refs_1_), custom_call_target="tpu_custom_call", output_to_operand_aliasing={{0}: (3, {})} | custom-call | tf_op jit(solution)/shard_map/decode/pallas_call | solution.py:207
  148.1 1.8 decode.40
  149.9 2.9 %decode.43 = (bf16[3072,2048]{1,0:T(8,128)(2,1)}, f32[8,128]{1,0:T(8,128)}) custom-call(s32[1]{0:T(128)} %bitcast.me_ref, f32[24,1,2048]{2,1,0:T(1,128)S(1)} %get-tuple-element.105.r_ref, bf16[192,2048]{1,0:T(8,128)(2,1)} %collective-permute-done.25.refs_0_, bf16[3072,2048]{1,0:T(8,128)(2,1)} %get-tuple-element.147.refs_1_), custom_call_target="tpu_custom_call", output_to_operand_aliasing={{0}: (3, {})} | custom-call | tf_op jit(solution)/shard_map/decode/pallas_call | solution.py:207
  152.8 1.8 decode.44
  154.6 1.3 collective-permute-start.22
  157.0 1.8 decode.41
  158.8 12.4 %collective-permute-done.27.refs_0_ = bf16[192,2048]{1,0:T(8,128)(2,1)S(1)} collective-permute-done((bf16[192,2048]{1,0:T(8,128)(2,1)S(1)}, bf16[192,2048]{1,0:T(8,128)(2,1)S(1)}, u32[]{:S(2)}, u32[]{:S(2)}) %collective-permute-start.27) | collective-permute-done | bytes 786464 | tf_op jit(solution)/shard_map/ppermute | solution.py:273
  173.6 1.8 decode.42
  175.4 1.8 decode.45
  177.1 10.7 %collective-permute-done.22 = bf16[192,2048]{1,0:T(8,128)(2,1)S(1)} collective-permute-done((bf16[192,2048]{1,0:T(8,128)(2,1)}, bf16[192,2048]{1,0:T(8,128)(2,1)S(1)}, u32[]{:S(2)}, u32[]{:S(2)}) %collective-permute-start.22) | collective-permute-done | bytes 786464 | tf_op jit(solution)/shard_map/ppermute | solution.py:271
  188.0 1.3 collective-permute-start.28
  190.4 1.8 decode.46
  192.1 1.8 decode.49
  193.9 1.8 decode.50
  195.7 9.2 %collective-permute-done.32.refs_0_ = bf16[192,2048]{1,0:T(8,128)(2,1)S(1)} collective-permute-done((bf16[192,2048]{1,0:T(8,128)(2,1)S(1)}, bf16[192,2048]{1,0:T(8,128)(2,1)S(1)}, u32[]{:S(2)}, u32[]{:S(2)}) %collective-permute-start.32) | collective-permute-done | bytes 786464 | tf_op jit(solution)/shard_map/ppermute | solution.py:273
  204.9 1.5 collective-permute-start.37
  206.5 1.8 decode.47
  208.2 1.8 decode.48
  211.1 10.5 %collective-permute-done.28 = bf16[192,2048]{1,0:T(8,128)(2,1)S(1)} collective-permute-done((bf16[192,2048]{1,0:T(8,128)(2,1)S(1)}, bf16[192,2048]{1,0:T(8,128)(2,1)S(1)}, u32[]{:S(2)}, u32[]{:S(2)}) %collective-permute-start.28) | collective-permute-done | bytes 786464 | tf_op jit(solution)/shard_map/ppermute | solution.py:271
  221.7 1.8 decode.51
  223.6 1.8 decode.52
  227.3 11.0 %collective-permute-done.37 = bf16[192,2048]{1,0:T(8,128)(2,1)S(1)} collective-permute-done((bf16[192,2048]{1,0:T(8,128)(2,1)S(1)}, bf16[192,2048]{1,0:T(8,128)(2,1)S(1)}, u32[]{:S(2)}, u32[]{:S(2)}) %collective-permute-start.37) | collective-permute-done | bytes 786464 | tf_op jit(solution)/shard_map/ppermute | solution.py:271
  238.6 1.9 collective-permute-start.38
  241.1 1.8 decode.55
  242.9 1.8 decode.56
  244.7 7.9 %collective-permute-done.35.refs_0_ = bf16[192,2048]{1,0:T(8,128)(2,1)S(1)} collective-permute-done((bf16[192,2048]{1,0:T(8,128)(2,1)S(1)}, bf16[192,2048]{1,0:T(8,128)(2,1)S(1)}, u32[]{:S(2)}, u32[]{:S(2)}) %collective-permute-start.35) | collective-permute-done | bytes 786464 | tf_op jit(solution)/shard_map/ppermute | solution.py:271
  252.5 1.8 decode.53
  254.3 1.8 decode.54
  256.1 4.9 %collective-permute-done.38.refs_0_ = bf16[192,2048]{1,0:T(8,128)(2,1)S(1)} collective-permute-done((bf16[192,2048]{1,0:T(8,128)(2,1)S(1)}, bf16[192,2048]{1,0:T(8,128)(2,1)S(1)}, u32[]{:S(2)}, u32[]{:S(2)}) %collective-permute-start.38) | collective-permute-done | bytes 786464 | tf_op jit(solution)/shard_map/ppermute | solution.py:271
  261.0 2.2 decode.57
  (86 shorter events, 32.0 us)
Async XLA Ops:
  2.9 20.8 %collective-permute-start.2 = (bf16[192,2048]{1,0:T(8,128)(2,1)S(1)}, bf16[192,2048]{1,0:T(8,128)(2,1)S(1)}, u32[]{:S(2)}, u32[]{:S(2)}) collective-permute-start(bf16[192,2048]{1,0:T(8,128)(2,1)S(1)} %get-tuple-element.98.refs_0_), channel_id=1, source_target_pairs={{0,4},{1,9},{2,6},{3,11},{4,0},{5,13},{6,2},{7,15},{8,12},{9,1},{1... | collective-permute-start | bytes 2359304 | tf_op jit(solution)/shard_map/ppermute | solution.py:316
  6.0 20.3 %collective-permute-start.1 = (bf16[192,2048]{1,0:T(8,128)(2,1)S(1)}, bf16[192,2048]{1,0:T(8,128)(2,1)S(1)}, u32[]{:S(2)}, u32[]{:S(2)}) collective-permute-start(bf16[192,2048]{1,0:T(8,128)(2,1)S(1)} %get-tuple-element.98.refs_0_), channel_id=1, source_target_pairs={{0,8},{1,5},{2,10},{3,7},{4,12},{5,1},{6,14},{7,3},{8,0},{9,13},{1... | collective-permute-start | bytes 2359304 | tf_op jit(solution)/shard_map/ppermute | solution.py:316
  7.5 33.4 %collective-permute-start.3 = (bf16[192,2048]{1,0:T(8,128)(2,1)S(1)}, bf16[192,2048]{1,0:T(8,128)(2,1)}, u32[]{:S(2)}, u32[]{:S(2)}) collective-permute-start(bf16[192,2048]{1,0:T(8,128)(2,1)S(1)} %get-tuple-element.98.refs_0_), channel_id=1, source_target_pairs={{8,16},{12,20},{16,8},{20,12},{9,17},{13,21},{17,9},{21,13},{10,18... | collective-permute-start | bytes 2359304 | tf_op jit(solution)/shard_map/ppermute | solution.py:271
  9.1 0.7 copy-start.6
  16.0 0.9 copy-start
  16.8 26.6 %collective-permute-start.7 = (bf16[192,2048]{1,0:T(8,128)(2,1)}, bf16[192,2048]{1,0:T(8,128)(2,1)}, u32[]{:S(2)}, u32[]{:S(2)}) collective-permute-start(bf16[192,2048]{1,0:T(8,128)(2,1)} %get-tuple-element.101.refs_0_), channel_id=1, source_target_pairs={{8,16},{12,20},{16,8},{20,12},{9,17},{13,21},{17,9},{21,13},{10,18... | collective-permute-start | bytes 2359304 | tf_op jit(solution)/shard_map/ppermute | solution.py:271
  18.4 29.4 %collective-permute-start.6 = (bf16[192,2048]{1,0:T(8,128)(2,1)}, bf16[192,2048]{1,0:T(8,128)(2,1)}, u32[]{:S(2)}, u32[]{:S(2)}) collective-permute-start(bf16[192,2048]{1,0:T(8,128)(2,1)} %get-tuple-element.101.refs_0_), channel_id=1, source_target_pairs={{0,8},{4,12},{8,0},{12,4},{16,24},{20,28},{24,16},{28,20},{1,9},{5... | collective-permute-start | bytes 2359304 | tf_op jit(solution)/shard_map/ppermute | solution.py:271
  23.7 2.5 copy-start.11
  23.7 24.3 %collective-permute-start.5 = (bf16[192,2048]{1,0:T(8,128)(2,1)}, bf16[192,2048]{1,0:T(8,128)(2,1)S(1)}, u32[]{:S(2)}, u32[]{:S(2)}) collective-permute-start(bf16[192,2048]{1,0:T(8,128)(2,1)} %get-tuple-element.101.refs_0_), channel_id=1, source_target_pairs={{0,4},{4,0},{8,12},{12,8},{16,20},{20,16},{24,28},{28,24},{1,5},{5... | collective-permute-start | bytes 2359304 | tf_op jit(solution)/shard_map/ppermute | solution.py:273
  26.2 0.9 copy-start.12
  27.1 13.8 %collective-permute-start = (f32[3,1,2048]{2,1,0:T(1,128)S(1)}, f32[3,1,2048]{2,1,0:T(1,128)S(1)}, u32[]{:S(2)}, u32[]{:S(2)}) collective-permute-start(f32[3,1,2048]{2,1,0:T(1,128)S(1)} %get-tuple-element.97.m0_ref), channel_id=1, source_target_pairs={{0,8},{4,12},{8,0},{12,4},{16,24},{20,28},{24,16},{28,20},{1,9},{5... | collective-permute-start | bytes 73736 | tf_op jit(solution)/shard_map/ppermute | solution.py:271
  41.0 37.7 %collective-permute-start.12 = (bf16[192,2048]{1,0:T(8,128)(2,1)}, bf16[192,2048]{1,0:T(8,128)(2,1)S(1)}, u32[]{:S(2)}, u32[]{:S(2)}) collective-permute-start(bf16[192,2048]{1,0:T(8,128)(2,1)} %copy-done), channel_id=1, source_target_pairs={{8,16},{12,20},{16,8},{20,12},{9,17},{13,21},{17,9},{21,13},{10,18... | collective-permute-start | bytes 2359304 | tf_op jit(solution)/shard_map/ppermute | solution.py:271
  41.7 38.0 %collective-permute-start.11 = (bf16[192,2048]{1,0:T(8,128)(2,1)}, bf16[192,2048]{1,0:T(8,128)(2,1)S(1)}, u32[]{:S(2)}, u32[]{:S(2)}) collective-permute-start(bf16[192,2048]{1,0:T(8,128)(2,1)} %copy-done), channel_id=1, source_target_pairs={{0,4},{4,0},{8,12},{12,8},{16,20},{20,16},{24,28},{28,24},{1,5},{5... | collective-permute-start | bytes 2359304 | tf_op jit(solution)/shard_map/ppermute | solution.py:273
  43.4 37.2 %collective-permute-start.10 = (bf16[192,2048]{1,0:T(8,128)(2,1)}, bf16[192,2048]{1,0:T(8,128)(2,1)}, u32[]{:S(2)}, u32[]{:S(2)}) collective-permute-start(bf16[192,2048]{1,0:T(8,128)(2,1)} %copy-done), channel_id=1, source_target_pairs={{0,8},{4,12},{8,0},{12,4},{16,24},{20,28},{24,16},{28,20},{1,9},{5... | collective-permute-start | bytes 2359304 | tf_op jit(solution)/shard_map/ppermute | solution.py:271
  47.8 16.6 %collective-permute-start.4 = (f32[6,1,2048]{2,1,0:T(1,128)S(1)}, f32[6,1,2048]{2,1,0:T(1,128)S(1)}, u32[]{:S(2)}, u32[]{:S(2)}) collective-permute-start(f32[6,1,2048]{2,1,0:T(1,128)S(1)} %pad_maximum_fusion), channel_id=1, source_target_pairs={{0,16},{4,20},{16,0},{20,4},{8,24},{12,28},{24,8},{28,12},{1,17},{... | collective-permute-start | bytes 147464 | tf_op jit(solution)/shard_map/ppermute | solution.py:271
  48.0 0.9 copy-start.2
  64.4 18.5 %collective-permute-start.23 = (bf16[192,2048]{1,0:T(8,128)(2,1)S(1)}, bf16[192,2048]{1,0:T(8,128)(2,1)S(1)}, u32[]{:S(2)}, u32[]{:S(2)}) collective-permute-start(bf16[192,2048]{1,0:T(8,128)(2,1)S(1)} %get-tuple-element.121.refs_1_), channel_id=1, source_target_pairs={{8,16},{12,20},{16,8},{20,12},{9,17},{13,21},{17,9},{21,13},{10,18... | collective-permute-start | bytes 2359304 | tf_op jit(solution)/shard_map/ppermute | solution.py:271
  65.2 3.8 %collective-permute-start.9 = (f32[2,1,2048]{2,1,0:T(1,128)S(1)}, f32[2,1,2048]{2,1,0:T(1,128)S(1)}, u32[]{:S(2)}, u32[]{:S(2)}) collective-permute-start(f32[2,1,2048]{2,1,0:T(1,128)S(1)} %get-tuple-element.104.most0_ref), channel_id=1, source_target_pairs={{0,4},{4,0},{8,12},{12,8},{16,20},{20,16},{24,28},{28,24},{1,5},{5... | collective-permute-start | bytes 49160 | tf_op jit(solution)/shard_map/ppermute | solution.py:273
  69.0 4.3 %collective-permute-start.8 = (bf16[16,2048]{1,0:T(8,128)(2,1)S(1)}, bf16[16,2048]{1,0:T(8,128)(2,1)S(1)}, u32[]{:S(2)}, u32[]{:S(2)}) collective-permute-start(bf16[16,2048]{1,0:T(8,128)(2,1)S(1)} %get-tuple-element.102.scale0_ref), channel_id=1, source_target_pairs={{0,4},{4,0},{8,12},{12,8},{16,20},{20,16},{24,28},{28,24},{1,5},{5... | collective-permute-start | bytes 196616 | tf_op jit(solution)/shard_map/ppermute | solution.py:273
  73.2 23.9 %collective-permute-start.20 = (bf16[192,2048]{1,0:T(8,128)(2,1)S(1)}, bf16[192,2048]{1,0:T(8,128)(2,1)}, u32[]{:S(2)}, u32[]{:S(2)}) collective-permute-start(bf16[192,2048]{1,0:T(8,128)(2,1)S(1)} %get-tuple-element.121.refs_1_), channel_id=1, source_target_pairs={{0,8},{4,12},{8,0},{12,4},{16,24},{20,28},{24,16},{28,20},{1,9},{5... | collective-permute-start | bytes 2359304 | tf_op jit(solution)/shard_map/ppermute | solution.py:271
  78.7 4.3 %copy-start.7 = (bf16[192,2048]{1,0:T(8,128)(2,1)}, bf16[192,2048]{1,0:T(8,128)(2,1)S(1)}, u32[]{:S(2)}) copy-start(bf16[192,2048]{1,0:T(8,128)(2,1)S(1)} %collective-permute-done.12) | copy-start | bytes 2359300
  78.7 20.5 %collective-permute-start.19 = (bf16[192,2048]{1,0:T(8,128)(2,1)S(1)}, bf16[192,2048]{1,0:T(8,128)(2,1)}, u32[]{:S(2)}, u32[]{:S(2)}) collective-permute-start(bf16[192,2048]{1,0:T(8,128)(2,1)S(1)} %get-tuple-element.121.refs_1_), channel_id=1, source_target_pairs={{0,4},{4,0},{8,12},{12,8},{16,20},{20,16},{24,28},{28,24},{1,5},{5... | collective-permute-start | bytes 2359304 | tf_op jit(solution)/shard_map/ppermute | solution.py:273
  79.7 0.9 copy-start.4
  80.6 35.4 %collective-permute-start.13 = (bf16[192,2048]{1,0:T(8,128)(2,1)}, bf16[192,2048]{1,0:T(8,128)(2,1)}, u32[]{:S(2)}, u32[]{:S(2)}) collective-permute-start(bf16[192,2048]{1,0:T(8,128)(2,1)} %collective-permute-done.10.refs_0_), channel_id=1, source_target_pairs={{0,4},{4,0},{8,12},{12,8},{16,20},{20,16},{24,28},{28,24},{1,5},{5... | collective-permute-start | bytes 2359304 | tf_op jit(solution)/shard_map/ppermute | solution.py:273
  81.6 48.9 %collective-permute-start.14 = (bf16[192,2048]{1,0:T(8,128)(2,1)}, bf16[192,2048]{1,0:T(8,128)(2,1)}, u32[]{:S(2)}, u32[]{:S(2)}) collective-permute-start(bf16[192,2048]{1,0:T(8,128)(2,1)} %collective-permute-done.3), channel_id=1, source_target_pairs={{8,0},{12,4},{16,24},{20,28},{9,1},{13,5},{17,25},{21,29},{10,2},{... | collective-permute-start | bytes 2359304 | tf_op jit(solution)/shard_map/ppermute | solution.py:271
  82.9 0.9 copy-start.9
  83.8 46.7 %collective-permute-start.15 = (bf16[192,2048]{1,0:T(8,128)(2,1)S(1)}, bf16[192,2048]{1,0:T(8,128)(2,1)}, u32[]{:S(2)}, u32[]{:S(2)}) collective-permute-start(bf16[192,2048]{1,0:T(8,128)(2,1)S(1)} %get-tuple-element.110.refs_0_), channel_id=1, source_target_pairs={{8,16},{12,20},{16,8},{20,12},{9,17},{13,21},{17,9},{21,13},{10,18... | collective-permute-start | bytes 2359304 | tf_op jit(solution)/shard_map/ppermute | solution.py:271
  85.5 1.1 copy-start.1
  99.2 34.6 %collective-permute-start.24 = (bf16[192,2048]{1,0:T(8,128)(2,1)}, bf16[192,2048]{1,0:T(8,128)(2,1)}, u32[]{:S(2)}, u32[]{:S(2)}) collective-permute-start(bf16[192,2048]{1,0:T(8,128)(2,1)} %collective-permute-done.7), channel_id=1, source_target_pairs={{8,0},{12,4},{16,24},{20,28},{9,1},{13,5},{17,25},{21,29},{10,2},{... | collective-permute-start | bytes 2359304 | tf_op jit(solution)/shard_map/ppermute | solution.py:271
  100.5 34.4 %collective-permute-start.25 = (bf16[192,2048]{1,0:T(8,128)(2,1)}, bf16[192,2048]{1,0:T(8,128)(2,1)}, u32[]{:S(2)}, u32[]{:S(2)}) collective-permute-start(bf16[192,2048]{1,0:T(8,128)(2,1)} %collective-permute-done.20.refs_0_), channel_id=1, source_target_pairs={{0,4},{4,0},{8,12},{12,8},{16,20},{20,16},{24,28},{28,24},{1,5},{5... | collective-permute-start | bytes 2359304 | tf_op jit(solution)/shard_map/ppermute | solution.py:273
  116.0 18.9 %collective-permute-start.26 = (bf16[192,2048]{1,0:T(8,128)(2,1)}, bf16[192,2048]{1,0:T(8,128)(2,1)}, u32[]{:S(2)}, u32[]{:S(2)}) collective-permute-start(bf16[192,2048]{1,0:T(8,128)(2,1)} %collective-permute-done.6.refs_0_), channel_id=1, source_target_pairs={{8,16},{12,20},{16,8},{20,12},{9,17},{13,21},{17,9},{21,13},{10,18... | collective-permute-start | bytes 2359304 | tf_op jit(solution)/shard_map/ppermute | solution.py:271
  117.6 3.5 %copy-start.3 = (bf16[192,2048]{1,0:T(8,128)(2,1)S(1)}, bf16[192,2048]{1,0:T(8,128)(2,1)}, u32[]{:S(2)}) copy-start(bf16[192,2048]{1,0:T(8,128)(2,1)} %copy-done.2) | copy-start | bytes 2359300
  121.2 4.7 %copy-start.5 = (bf16[192,2048]{1,0:T(8,128)(2,1)S(1)}, bf16[192,2048]{1,0:T(8,128)(2,1)}, u32[]{:S(2)}) copy-start(bf16[192,2048]{1,0:T(8,128)(2,1)} %copy-done.4) | copy-start | bytes 2359300
  125.8 6.7 %copy-start.8 = (bf16[192,2048]{1,0:T(8,128)(2,1)S(1)}, bf16[192,2048]{1,0:T(8,128)(2,1)}, u32[]{:S(2)}) copy-start(bf16[192,2048]{1,0:T(8,128)(2,1)} %copy-done.7) | copy-start | bytes 2359300
  125.9 11.4 %copy-start.10 = (bf16[192,2048]{1,0:T(8,128)(2,1)S(1)}, bf16[192,2048]{1,0:T(8,128)(2,1)}, u32[]{:S(2)}) copy-start(bf16[192,2048]{1,0:T(8,128)(2,1)} %copy-done.9) | copy-start | bytes 2359300
  130.6 8.0 %collective-permute-start.16 = (bf16[192,2048]{1,0:T(8,128)(2,1)}, bf16[192,2048]{1,0:T(8,128)(2,1)S(1)}, u32[]{:S(2)}, u32[]{:S(2)}) collective-permute-start(bf16[192,2048]{1,0:T(8,128)(2,1)} %collective-permute-done.10.refs_0_), channel_id=1, source_target_pairs={{8,16},{12,20},{16,8},{20,12},{9,17},{13,21},{17,9},{21,13},{10,18... | collective-permute-start | bytes 2359304 | tf_op jit(solution)/shard_map/ppermute | solution.py:271
  132.5 22.0 %collective-permute-start.17 = (bf16[192,2048]{1,0:T(8,128)(2,1)S(1)}, bf16[192,2048]{1,0:T(8,128)(2,1)S(1)}, u32[]{:S(2)}, u32[]{:S(2)}) collective-permute-start(bf16[192,2048]{1,0:T(8,128)(2,1)S(1)} %copy-done.8), channel_id=1, source_target_pairs={{8,0},{12,4},{16,24},{20,28},{9,1},{13,5},{17,25},{21,29},{10,2},{... | collective-permute-start | bytes 2359304 | tf_op jit(solution)/shard_map/ppermute | solution.py:271
  133.8 20.7 %collective-permute-start.18 = (bf16[192,2048]{1,0:T(8,128)(2,1)S(1)}, bf16[192,2048]{1,0:T(8,128)(2,1)S(1)}, u32[]{:S(2)}, u32[]{:S(2)}) collective-permute-start(bf16[192,2048]{1,0:T(8,128)(2,1)S(1)} %broadcast_select_fusion.6.refs_0_), channel_id=1, source_target_pairs={{0,4},{4,0},{8,12},{12,8},{16,20},{20,16},{24,28},{28,24},{1,5},{5... | collective-permute-start | bytes 2359304 | tf_op jit(solution)/shard_map/ppermute | solution.py:273
  136.1 35.0 %collective-permute-start.27 = (bf16[192,2048]{1,0:T(8,128)(2,1)S(1)}, bf16[192,2048]{1,0:T(8,128)(2,1)S(1)}, u32[]{:S(2)}, u32[]{:S(2)}) collective-permute-start(bf16[192,2048]{1,0:T(8,128)(2,1)S(1)} %broadcast_select_fusion.5.refs_0_), channel_id=1, source_target_pairs={{0,4},{4,0},{8,12},{12,8},{16,20},{20,16},{24,28},{28,24},{1,5},{5... | collective-permute-start | bytes 2359304 | tf_op jit(solution)/shard_map/ppermute | solution.py:273
  137.2 33.9 %collective-permute-start.30 = (bf16[192,2048]{1,0:T(8,128)(2,1)S(1)}, bf16[192,2048]{1,0:T(8,128)(2,1)S(1)}, u32[]{:S(2)}, u32[]{:S(2)}) collective-permute-start(bf16[192,2048]{1,0:T(8,128)(2,1)S(1)} %copy-done.10), channel_id=1, source_target_pairs={{8,0},{12,4},{16,24},{20,28},{9,1},{13,5},{17,25},{21,29},{10,2},{... | collective-permute-start | bytes 2359304 | tf_op jit(solution)/shard_map/ppermute | solution.py:271
  138.5 32.7 %collective-permute-start.31 = (bf16[192,2048]{1,0:T(8,128)(2,1)}, bf16[192,2048]{1,0:T(8,128)(2,1)S(1)}, u32[]{:S(2)}, u32[]{:S(2)}) collective-permute-start(bf16[192,2048]{1,0:T(8,128)(2,1)} %collective-permute-done.20.refs_0_), channel_id=1, source_target_pairs={{8,16},{12,20},{16,8},{20,12},{9,17},{13,21},{17,9},{21,13},{10,18... | collective-permute-start | bytes 2359304 | tf_op jit(solution)/shard_map/ppermute | solution.py:271
  154.6 33.3 %collective-permute-start.22 = (bf16[192,2048]{1,0:T(8,128)(2,1)}, bf16[192,2048]{1,0:T(8,128)(2,1)S(1)}, u32[]{:S(2)}, u32[]{:S(2)}) collective-permute-start(bf16[192,2048]{1,0:T(8,128)(2,1)} %collective-permute-done.15), channel_id=1, source_target_pairs={{8,0},{12,4},{16,24},{20,28},{9,1},{13,5},{17,25},{21,29},{10,2},{... | collective-permute-start | bytes 2359304 | tf_op jit(solution)/shard_map/ppermute | solution.py:271
  156.0 32.1 %collective-permute-start.21 = (bf16[192,2048]{1,0:T(8,128)(2,1)S(1)}, bf16[192,2048]{1,0:T(8,128)(2,1)S(1)}, u32[]{:S(2)}, u32[]{:S(2)}) collective-permute-start(bf16[192,2048]{1,0:T(8,128)(2,1)S(1)} %broadcast_select_fusion.7.refs_0_), channel_id=1, source_target_pairs={{0,4},{4,0},{8,12},{12,8},{16,20},{20,16},{24,28},{28,24},{1,5},{5... | collective-permute-start | bytes 2359304 | tf_op jit(solution)/shard_map/ppermute | solution.py:273
  171.3 33.6 %collective-permute-start.32 = (bf16[192,2048]{1,0:T(8,128)(2,1)S(1)}, bf16[192,2048]{1,0:T(8,128)(2,1)S(1)}, u32[]{:S(2)}, u32[]{:S(2)}) collective-permute-start(bf16[192,2048]{1,0:T(8,128)(2,1)S(1)} %broadcast_select_fusion.2.refs_0_), channel_id=1, source_target_pairs={{0,4},{4,0},{8,12},{12,8},{16,20},{20,16},{24,28},{28,24},{1,5},{5... | collective-permute-start | bytes 2359304 | tf_op jit(solution)/shard_map/ppermute | solution.py:273
  172.3 32.6 %collective-permute-start.33 = (bf16[192,2048]{1,0:T(8,128)(2,1)}, bf16[192,2048]{1,0:T(8,128)(2,1)S(1)}, u32[]{:S(2)}, u32[]{:S(2)}) collective-permute-start(bf16[192,2048]{1,0:T(8,128)(2,1)} %collective-permute-done.26), channel_id=1, source_target_pairs={{8,0},{12,4},{16,24},{20,28},{9,1},{13,5},{17,25},{21,29},{10,2},{... | collective-permute-start | bytes 2359304 | tf_op jit(solution)/shard_map/ppermute | solution.py:271
  188.0 33.5 %collective-permute-start.28 = (bf16[192,2048]{1,0:T(8,128)(2,1)S(1)}, bf16[192,2048]{1,0:T(8,128)(2,1)S(1)}, u32[]{:S(2)}, u32[]{:S(2)}) collective-permute-start(bf16[192,2048]{1,0:T(8,128)(2,1)S(1)} %collective-permute-done.16), channel_id=1, source_target_pairs={{8,0},{12,4},{16,24},{20,28},{9,1},{13,5},{17,25},{21,29},{10,2},{... | collective-permute-start | bytes 2359304 | tf_op jit(solution)/shard_map/ppermute | solution.py:271
  189.3 32.4 %collective-permute-start.29 = (bf16[192,2048]{1,0:T(8,128)(2,1)S(1)}, bf16[192,2048]{1,0:T(8,128)(2,1)S(1)}, u32[]{:S(2)}, u32[]{:S(2)}) collective-permute-start(bf16[192,2048]{1,0:T(8,128)(2,1)S(1)} %broadcast_select_fusion.3.refs_0_), channel_id=1, source_target_pairs={{0,4},{4,0},{8,12},{12,8},{16,20},{20,16},{24,28},{28,24},{1,5},{5... | collective-permute-start | bytes 2359304 | tf_op jit(solution)/shard_map/ppermute | solution.py:273
  204.9 33.5 %collective-permute-start.37 = (bf16[192,2048]{1,0:T(8,128)(2,1)S(1)}, bf16[192,2048]{1,0:T(8,128)(2,1)S(1)}, u32[]{:S(2)}, u32[]{:S(2)}) collective-permute-start(bf16[192,2048]{1,0:T(8,128)(2,1)S(1)} %collective-permute-done.31), channel_id=1, source_target_pairs={{8,0},{12,4},{16,24},{20,28},{9,1},{13,5},{17,25},{21,29},{10,2},{... | collective-permute-start | bytes 2359304 | tf_op jit(solution)/shard_map/ppermute | solution.py:271
  210.0 28.6 %collective-permute-start.36 = (bf16[192,2048]{1,0:T(8,128)(2,1)S(1)}, bf16[192,2048]{1,0:T(8,128)(2,1)S(1)}, u32[]{:S(2)}, u32[]{:S(2)}) collective-permute-start(bf16[192,2048]{1,0:T(8,128)(2,1)S(1)} %broadcast_select_fusion.1.refs_0_), channel_id=1, source_target_pairs={{0,4},{4,0},{8,12},{12,8},{16,20},{20,16},{24,28},{28,24},{1,5},{5... | collective-permute-start | bytes 2359304 | tf_op jit(solution)/shard_map/ppermute | solution.py:273
  225.3 28.9 %collective-permute-start.34 = (bf16[192,2048]{1,0:T(8,128)(2,1)S(1)}, bf16[192,2048]{1,0:T(8,128)(2,1)S(1)}, u32[]{:S(2)}, u32[]{:S(2)}) collective-permute-start(bf16[192,2048]{1,0:T(8,128)(2,1)S(1)} %broadcast_select_fusion.4.refs_0_), channel_id=1, source_target_pairs={{0,4},{4,0},{8,12},{12,8},{16,20},{20,16},{24,28},{28,24},{1,5},{5... | collective-permute-start | bytes 2359304 | tf_op jit(solution)/shard_map/ppermute | solution.py:273
  226.4 26.1 %collective-permute-start.35 = (bf16[192,2048]{1,0:T(8,128)(2,1)S(1)}, bf16[192,2048]{1,0:T(8,128)(2,1)S(1)}, u32[]{:S(2)}, u32[]{:S(2)}) collective-permute-start(bf16[192,2048]{1,0:T(8,128)(2,1)S(1)} %get-tuple-element.166.refs_0_), channel_id=1, source_target_pairs={{0,8},{4,12},{8,0},{12,4},{16,24},{20,28},{24,16},{28,20},{1,9},{5... | collective-permute-start | bytes 2359304 | tf_op jit(solution)/shard_map/ppermute | solution.py:271
  238.6 22.4 %collective-permute-start.38 = (bf16[192,2048]{1,0:T(8,128)(2,1)S(1)}, bf16[192,2048]{1,0:T(8,128)(2,1)S(1)}, u32[]{:S(2)}, u32[]{:S(2)}) collective-permute-start(bf16[192,2048]{1,0:T(8,128)(2,1)S(1)} %copy-done.3), channel_id=1, source_target_pairs={{0,8},{4,12},{8,0},{12,4},{16,24},{20,28},{24,16},{28,20},{1,9},{5... | collective-permute-start | bytes 2359304 | tf_op jit(solution)/shard_map/ppermute | solution.py:271
  240.4 20.5 %collective-permute-start.39 = (bf16[192,2048]{1,0:T(8,128)(2,1)S(1)}, bf16[192,2048]{1,0:T(8,128)(2,1)S(1)}, u32[]{:S(2)}, u32[]{:S(2)}) collective-permute-start(bf16[192,2048]{1,0:T(8,128)(2,1)S(1)} %broadcast_select_fusion.refs_0_), channel_id=1, source_target_pairs={{0,4},{4,0},{8,12},{12,8},{16,20},{20,16},{24,28},{28,24},{1,5},{5... | collective-permute-start | bytes 2359304 | tf_op jit(solution)/shard_map/ppermute | solution.py:273

commit v4 on v3

--- a/solution.py
+++ b/solution.py
@@ -178,16 +178,16 @@
     return jnp.where(y < 0, -x, x).astype(jnp.bfloat16)
 
 
-def decode_body(me_ref, r_ref, *refs, places, pieces):
+def decode_body(me_ref, r_ref, *refs, places, pieces, half_rows):
     count = len(places)
     chunks, (out_ref, token_ref, buffer, sems) = refs[:count], refs[-4:]
     rows = chunks[0].shape[0] // pieces
     me = me_ref[0]
     copies = []
-    for i, (shard_of, c) in enumerate(places):
+    for i, (shard_of, c, offset) in enumerate(places):
         shard = shard_of(me)
         ratio = r_ref[(shard ^ me) * 3 + SCALE_OF_CHUNK[c]]
-        start = (2 * shard + c // 2) * chunks[0].shape[0]
+        start = (2 * shard + c // 2) * half_rows + offset
         for p in range(pieces):
             part = pl.ds(p * rows, rows)
             buffer[i, part] = decoded(chunks[i][part], ratio)
@@ -200,12 +200,14 @@
         copy.wait()
 
 
-def decode(whole, chunks, ratios, me, places, pieces=4):
+def decode(whole, chunks, ratios, me, places):
     here = pl.BlockSpec(memory_space=pltpu.VMEM)
     there = pl.BlockSpec(memory_space=pl.ANY)
     begun = not isinstance(whole, jax.ShapeDtypeStruct)
+    half_rows, height = whole.shape[0] // 16, chunks[0].shape[0]
+    pieces = next(n for n in (4, 3, 1) if height % (16 * n) == 0)
     return pl.pallas_call(
-        functools.partial(decode_body, places=places, pieces=pieces),
+        functools.partial(decode_body, places=places, pieces=pieces, half_rows=half_rows),
         in_specs=[pl.BlockSpec(memory_space=pltpu.SMEM), here] + [here] * len(chunks) + [there] * begun,
         out_specs=[there, here],
         out_shape=[
@@ -261,6 +263,7 @@
 def local_plane(w_gate, avg_gate, w_up, avg_up, norm_gain):
     rows, columns = w_gate.shape
     block = min(columns, 1024)
+    cut = rows // 2 - rows // 128 * 16
     width = lax.axis_size("width")
     index = lax.axis_index("rows")
     outer = (index < 2) | (index >= 6)
@@ -285,29 +288,39 @@
     factors = ratios = None
     wholes, tokens, waiting = [None, None], [], []
 
+    def wait_for(chunk, shard_of, c, offset=0):
+        waiting.append((chunk, (shard_of, c, offset)))
+
     def arrived(k):
         got = [X[k]]
         if k < 4:
             got += [B[k], M[k]]
-            waiting.extend([(X[k], across_of, k), (B[k], buddy_of, k)])
+            wait_for(X[k], across_of, k)
+            wait_for(B[k], buddy_of, k)
         elif k < 8:
             got += [O[k], M[k]]
         elif k < 12:
             got += [O[k]]
         else:
-            got += [F[k - 12]]
-            waiting.append((F[k - 12], diagonal_of, k - 12))
+            got += [F[0]]
+            wait_for(F[0], diagonal_of, 0)
         if 4 <= k < 6:
-            waiting.append((X[k], diagonal_of, k - 2))
+            wait_for(X[k], diagonal_of, k - 2)
         if 6 <= k < 10:
-            waiting.append((X[k], near_across_of, k - 6))
+            wait_for(X[k], near_across_of, k - 6)
         if 10 <= k:
-            waiting.append((X[k], far_across_of, k - 10))
+            wait_for(X[k], far_across_of, k - 10)
         if 4 <= k < 12:
             j = k - 4
             V[j] = jnp.where(outer, O[k], M[j])
-            waiting.append((V[j], near_of if j < 4 else far_of, j % 4))
+            wait_for(V[j], near_of if j < 4 else far_of, j % 4)
         return got
+
+    def send_last(*ties):
+        parts = [slice(0, cut), slice(cut, rows // 2)]
+        for name, part in zip("ab", parts):
+            X[name] = across(after(jnp.where(outer, O[11][part], M[7][part]), *ties))
+            F[name] = buddies(after(X[1][part], *ties))
 
     def send_first():
         odd = lax.axis_index("width") % 2 == 1
@@ -346,15 +359,16 @@
     def settle(count):
         done = []
         for _ in range(min(count, len(waiting))):
-            chunk, shard_of, c = waiting.pop(0)
-            wholes[c % 2], token = decode(wholes[c % 2], [chunk], ratios, me, [(shard_of, c)])
+            chunk, place = waiting.pop(0)
+            t = place[1] % 2
+            wholes[t], token = decode(wholes[t], [chunk], ratios, me, [place])
             done.append(token)
         return done
 
     send_first()
     tables.append(buddies(maxima))
     send(1)
-    for k in range(14):
+    for k in range(13):
         got = arrived(k)
         if k == 0:
             got.append(tables[1])
@@ -367,17 +381,19 @@
         if k == 2:
             got += [far_scales, far_most]
             ratios, factors = ratios_of((scales, far_scales), (most, far_most))
-        if k + 2 < 14:
+        if k + 2 < 13:
             send(k + 2, *got, *tokens)
+        elif k + 2 == 13:
+            send_last(*got, *tokens)
         if k == 2:
             out = jax.ShapeDtypeStruct((8 * rows, columns), jnp.bfloat16)
-            wholes, tokens = zip(*[decode(out, own[t::2], ratios, me, [(own_of, t), (own_of, t + 2)]) for t in (0, 1)])
+            wholes, tokens = zip(*[decode(out, own[t::2], ratios, me, [(own_of, t, 0), (own_of, t + 2, 0)]) for t in (0, 1)])
             wholes = list(wholes)
         if k >= 3:
-            tokens = settle(3 if k < 13 else len(waiting) - 2)
-    chunks, shards_of, cs = zip(*waiting)
-    t = cs[0] % 2
-    wholes[t], _ = decode(wholes[t], chunks, ratios, me, list(zip(shards_of, cs)))
+            tokens = settle(3 if k < 12 else len(waiting))
+    for name, offset in (("a", 0), ("b", cut)):
+        places = [(diagonal_of, 1, offset), (far_across_of, 3, offset)]
+        wholes[1], _ = decode(wholes[1], [after(F[name], *tokens), after(X[name], *tokens)], ratios, me, places)
     return (*wholes, factors[0], factors[1])
 
 

time: 264 us -> 269 us (1.019); the launches traced: 263 us -> 266 us
  waiting for transfers between devices: 123 us -> 117 us
  starting transfers between devices: 58.7 us -> 64.5 us
    ppermute x23 -> x24, starting transfers between devices: 37.2 us -> 45.1 us  [hop(): return lax.ppermute(value, 'rows', both)]
    ppermute x23 -> x24, waiting for transfers between devices: 77 us -> 69.3 us  [hop(): return lax.ppermute(value, 'rows', both)]
    ppermute x15 -> x16, waiting for transfers between devices: 44.5 us -> 46.9 us  [local_plane(): lax.ppermute(value, 'rows', [(i, i ^ 1) for i in range(8)])]
    ppermute x15 -> x16, starting transfers between devices: 16.9 us -> 14.7 us  [local_plane(): lax.ppermute(value, 'rows', [(i, i ^ 1) for i in range(8)])]
    pallas_call x29 -> x30, Pallas kernels: 60.3 us -> 61.7 us  [decode(): pl.pallas_call(functools.partial(decode_body, places=places, pieces=piece...]
    unnamed x26 -> x24, local copies, waits for them, and re-layouts: 6.31 us -> 7.36 us
  transfers between devices with their start and end apart: 40 -> 42, of which waited for: 18 -> 19; matrix products, arithmetic and copies ran while one was open for 2% -> 2% of each run, Pallas kernels for 24% -> 24%
where the time goes in v4:
time: 269 us; the launch traced here: 266 us
  waiting for transfers between devices  117 us (43%)
  Pallas kernels  70.3 us (26%)
  starting transfers between devices  64.5 us (24%)
  local copies, waits for them, and re-layouts  8.03 us (3%)
  other arithmetic  4.57 us (2%)
    ppermute x24, waiting for transfers between devices, hop(): return lax.ppermute(value, 'rows', both)  69.3 us
    pallas_call x30, Pallas kernels, decode(): pl.pallas_call(functools.partial(decode_body, places=places, pieces=piece...  61.7 us
    ppermute x16, waiting for transfers between devices, local_plane(): lax.ppermute(value, 'rows', [(i, i ^ 1) for i in range(8)])  46.9 us
    ppermute x24, starting transfers between devices, hop(): return lax.ppermute(value, 'rows', both)  45.1 us
    ppermute x16, starting transfers between devices, local_plane(): lax.ppermute(value, 'rows', [(i, i ^ 1) for i in range(8)])  14.7 us
    unnamed x24, local copies, waits for them, and re-layouts  7.36 us
    pallas_call x1, Pallas kernels, encode_rest(): pl.pallas_call(encode_rest_body, grid=(columns // block,), in_specs=[pl.B...  6.22 us
  transfers between devices with their start and end apart: 42, of which 19 were waited for; matrix products, arithmetic and copies ran while one was open for 2% of the time, Pallas kernels for 24%

profile of v4, /device:TPU:0, one launch (start us, length us, event | category | flops | bytes accessed | tf_op | source)
XLA Modules:
  0.0 265.5 jit_solution(18410769701616871189)
XLA Ops:
  0.6 2.3 encode_first.1
  2.9 3.0 %collective-permute-start.2 = (bf16[192,2048]{1,0:T(8,128)(2,1)S(1)}, bf16[192,2048]{1,0:T(8,128)(2,1)}, u32[]{:S(2)}, u32[]{:S(2)}) collective-permute-start(bf16[192,2048]{1,0:T(8,128)(2,1)S(1)} %get-tuple-element.107.refs_0_), channel_id=1, source_target_pairs={{0,4},{1,9},{2,6},{3,11},{4,0},{5,13},{6,2},{7,15},{8,12},{9,1},{1... | collective-permute-start | bytes 2359304 | tf_op jit(solution)/shard_map/ppermute | solution.py:329
  6.0 1.6 collective-permute-start.1
  7.5 1.5 collective-permute-start.3
  9.8 6.2 %encode_rest.1 = (bf16[192,2048]{1,0:T(8,128)(2,1)}, bf16[192,2048]{1,0:T(8,128)(2,1)S(1)}, bf16[192,2048]{1,0:T(8,128)(2,1)S(1)}, f32[3,1,2048]{2,1,0:T(1,128)S(1)}) custom-call(f32[384]{0:T(512)S(1)} %copy-done.6, f32[384,2048]{1,0:T(8,128)} %wu1.1, f32[384,2048]{1,0:T(8,128)} %au1.1, f32[384,2048]{1,0:T(8,128)} %wg.1, f32[384,2048]{1,0:T(8,128)} %ag.1, ...), custom_call_target="tpu_custom_call" | custom-call | tf_op jit(solution)/shard_map/encode_rest/pallas_call | solution.py:73
  17.7 1.5 collective-permute-start.7
  19.3 4.0 %collective-permute-start.6 = (bf16[192,2048]{1,0:T(8,128)(2,1)}, bf16[192,2048]{1,0:T(8,128)(2,1)}, u32[]{:S(2)}, u32[]{:S(2)}) collective-permute-start(bf16[192,2048]{1,0:T(8,128)(2,1)} %get-tuple-element.110.refs_0_), channel_id=1, source_target_pairs={{0,8},{4,12},{8,0},{12,4},{16,24},{20,28},{24,16},{28,20},{1,9},{5... | collective-permute-start | bytes 2359304 | tf_op jit(solution)/shard_map/ppermute | solution.py:274
  23.8 2.5 collective-permute-start.5
  28.0 1.5 broadcast_select_fusion.8
  29.5 11.5 %collective-permute-done.m1_ref = f32[3,1,2048]{2,1,0:T(1,128)S(1)} collective-permute-done((f32[3,1,2048]{2,1,0:T(1,128)S(1)}, f32[3,1,2048]{2,1,0:T(1,128)S(1)}, u32[]{:S(2)}, u32[]{:S(2)}) %collective-permute-start) | collective-permute-done | bytes 24608 | tf_op jit(solution)/shard_map/ppermute | solution.py:274
  41.7 1.7 collective-permute-start.11
  43.4 4.3 %collective-permute-start.10 = (bf16[192,2048]{1,0:T(8,128)(2,1)}, bf16[192,2048]{1,0:T(8,128)(2,1)}, u32[]{:S(2)}, u32[]{:S(2)}) collective-permute-start(bf16[192,2048]{1,0:T(8,128)(2,1)} %copy-done.2), channel_id=1, source_target_pairs={{0,8},{4,12},{8,0},{12,4},{16,24},{20,28},{24,16},{28,20},{1,9},{5... | collective-permute-start | bytes 2359304 | tf_op jit(solution)/shard_map/ppermute | solution.py:274
  48.9 15.6 %collective-permute-done.4.m2_ref = f32[6,1,2048]{2,1,0:T(1,128)S(1)} collective-permute-done((f32[6,1,2048]{2,1,0:T(1,128)S(1)}, f32[6,1,2048]{2,1,0:T(1,128)S(1)}, u32[]{:S(2)}, u32[]{:S(2)}) %collective-permute-start.4) | collective-permute-done | bytes 49184 | tf_op jit(solution)/shard_map/ppermute | solution.py:274
  65.3 1.3 collective-permute-start.9
  66.6 2.5 collective-permute-done.9.most1_ref
  70.3 3.0 %collective-permute-done.8.scale1_ref = bf16[16,2048]{1,0:T(8,128)(2,1)S(1)} collective-permute-done((bf16[16,2048]{1,0:T(8,128)(2,1)S(1)}, bf16[16,2048]{1,0:T(8,128)(2,1)S(1)}, u32[]{:S(2)}, u32[]{:S(2)}) %collective-permute-start.8) | collective-permute-done | bytes 65568 | tf_op jit(solution)/shard_map/ppermute | solution.py:276
  73.3 5.8 %collective-permute-start.20 = (bf16[192,2048]{1,0:T(8,128)(2,1)}, bf16[192,2048]{1,0:T(8,128)(2,1)}, u32[]{:S(2)}, u32[]{:S(2)}) collective-permute-start(bf16[192,2048]{1,0:T(8,128)(2,1)} %copy-done), channel_id=1, source_target_pairs={{0,8},{4,12},{8,0},{12,4},{16,24},{20,28},{24,16},{28,20},{1,9},{5... | collective-permute-start | bytes 2359304 | tf_op jit(solution)/shard_map/ppermute | solution.py:274
  80.4 1.7 collective-permute-start.13
  84.3 1.5 collective-permute-start.15
  87.1 2.2 decode.30
  90.4 3.4 %decode.33 = (bf16[3072,2048]{1,0:T(8,128)(2,1)}, f32[8,128]{1,0:T(8,128)}) custom-call(s32[1]{0:T(128)} %bitcast.me_ref, f32[24,1,2048]{2,1,0:T(1,128)S(1)} %get-tuple-element.114.r_ref, bf16[192,2048]{1,0:T(8,128)(2,1)} %get-tuple-element.110.refs_0_, bf16[192,2048]{1,0:T(8,128)(2,1)S(1)} %copy-done.1), custom_call_target="tpu_custom_call" | custom-call | tf_op jit(solution)/shard_map/decode/pallas_call | solution.py:209
  93.8 4.0 %collective-permute-done.20.refs_0_ = bf16[192,2048]{1,0:T(8,128)(2,1)} collective-permute-done((bf16[192,2048]{1,0:T(8,128)(2,1)}, bf16[192,2048]{1,0:T(8,128)(2,1)}, u32[]{:S(2)}, u32[]{:S(2)}) %collective-permute-start.20) | collective-permute-done | bytes 786464 | tf_op jit(solution)/shard_map/ppermute | solution.py:274
  97.9 2.0 collective-permute-done.19.refs_0_
  101.6 15.1 %collective-permute-done.13.refs_0_ = bf16[192,2048]{1,0:T(8,128)(2,1)} collective-permute-done((bf16[192,2048]{1,0:T(8,128)(2,1)}, bf16[192,2048]{1,0:T(8,128)(2,1)}, u32[]{:S(2)}, u32[]{:S(2)}) %collective-permute-start.13) | collective-permute-done | bytes 786464 | tf_op jit(solution)/shard_map/ppermute | solution.py:276
  116.7 1.6 collective-permute-start.26
  118.3 1.8 decode.31
  120.1 1.8 decode.32
  121.8 1.8 decode.34
  123.6 2.9 %decode.35 = (bf16[3072,2048]{1,0:T(8,128)(2,1)}, f32[8,128]{1,0:T(8,128)}) custom-call(s32[1]{0:T(128)} %bitcast.me_ref, f32[24,1,2048]{2,1,0:T(1,128)S(1)} %get-tuple-element.114.r_ref, bf16[192,2048]{1,0:T(8,128)(2,1)} %collective-permute-done.6.refs_0_, bf16[3072,2048]{1,0:T(8,128)(2,1)} %get-tuple-element.131.refs_1_), custom_call_target="tpu_custom_call", output_to_operand_aliasing={{0}: (3, {})} | custom-call | tf_op jit(solution)/shard_map/decode/pallas_call | solution.py:209
  126.5 1.8 decode.38
  128.3 2.9 %decode.39 = (bf16[3072,2048]{1,0:T(8,128)(2,1)}, f32[8,128]{1,0:T(8,128)}) custom-call(s32[1]{0:T(128)} %bitcast.me_ref, f32[24,1,2048]{2,1,0:T(1,128)S(1)} %get-tuple-element.114.r_ref, bf16[192,2048]{1,0:T(8,128)(2,1)} %collective-permute-done.10.refs_0_, bf16[3072,2048]{1,0:T(8,128)(2,1)} %get-tuple-element.137.refs_1_), custom_call_target="tpu_custom_call", output_to_operand_aliasing={{0}: (3, {})} | custom-call | tf_op jit(solution)/shard_map/decode/pallas_call | solution.py:209
  133.2 1.3 collective-permute-start.17
  136.2 1.7 collective-permute-start.27
  140.2 2.9 %decode.36 = (bf16[3072,2048]{1,0:T(8,128)(2,1)}, f32[8,128]{1,0:T(8,128)}) custom-call(s32[1]{0:T(128)} %bitcast.me_ref, f32[24,1,2048]{2,1,0:T(1,128)S(1)} %get-tuple-element.114.r_ref, bf16[192,2048]{1,0:T(8,128)(2,1)} %collective-permute-done.19.refs_0_, bf16[3072,2048]{1,0:T(8,128)(2,1)} %get-tuple-element.132.refs_1_), custom_call_target="tpu_custom_call", output_to_operand_aliasing={{0}: (3, {})} | custom-call | tf_op jit(solution)/shard_map/decode/pallas_call | solution.py:209
  143.1 2.9 %decode.37 = (bf16[3072,2048]{1,0:T(8,128)(2,1)}, f32[8,128]{1,0:T(8,128)}) custom-call(s32[1]{0:T(128)} %bitcast.me_ref, f32[24,1,2048]{2,1,0:T(1,128)S(1)} %get-tuple-element.114.r_ref, bf16[192,2048]{1,0:T(8,128)(2,1)} %collective-permute-done.20.refs_0_, bf16[3072,2048]{1,0:T(8,128)(2,1)} %get-tuple-element.134.refs_1_), custom_call_target="tpu_custom_call", output_to_operand_aliasing={{0}: (3, {})} | custom-call | tf_op jit(solution)/shard_map/decode/pallas_call | solution.py:209
  146.0 2.9 %decode.40 = (bf16[3072,2048]{1,0:T(8,128)(2,1)}, f32[8,128]{1,0:T(8,128)}) custom-call(s32[1]{0:T(128)} %bitcast.me_ref, f32[24,1,2048]{2,1,0:T(1,128)S(1)} %get-tuple-element.114.r_ref, bf16[192,2048]{1,0:T(8,128)(2,1)} %collective-permute-done.13.refs_0_, bf16[3072,2048]{1,0:T(8,128)(2,1)} %get-tuple-element.138.refs_1_), custom_call_target="tpu_custom_call", output_to_operand_aliasing={{0}: (3, {})} | custom-call | tf_op jit(solution)/shard_map/decode/pallas_call | solution.py:209
  148.9 1.8 decode.41
  150.6 2.9 %decode.44 = (bf16[3072,2048]{1,0:T(8,128)(2,1)}, f32[8,128]{1,0:T(8,128)}) custom-call(s32[1]{0:T(128)} %bitcast.me_ref, f32[24,1,2048]{2,1,0:T(1,128)S(1)} %get-tuple-element.114.r_ref, bf16[192,2048]{1,0:T(8,128)(2,1)} %collective-permute-done.25.refs_0_, bf16[3072,2048]{1,0:T(8,128)(2,1)} %get-tuple-element.156.refs_1_), custom_call_target="tpu_custom_call", output_to_operand_aliasing={{0}: (3, {})} | custom-call | tf_op jit(solution)/shard_map/decode/pallas_call | solution.py:209
  153.5 1.8 decode.45
  156.7 1.8 decode.42
  158.5 1.8 decode.43
  160.7 11.2 %collective-permute-done.27.refs_0_ = bf16[192,2048]{1,0:T(8,128)(2,1)S(1)} collective-permute-done((bf16[192,2048]{1,0:T(8,128)(2,1)S(1)}, bf16[192,2048]{1,0:T(8,128)(2,1)S(1)}, u32[]{:S(2)}, u32[]{:S(2)}) %collective-permute-start.27) | collective-permute-done | bytes 786464 | tf_op jit(solution)/shard_map/ppermute | solution.py:276
  173.6 1.8 decode.46
  175.4 12.1 %collective-permute-done.22 = bf16[192,2048]{1,0:T(8,128)(2,1)S(1)} collective-permute-done((bf16[192,2048]{1,0:T(8,128)(2,1)}, bf16[192,2048]{1,0:T(8,128)(2,1)S(1)}, u32[]{:S(2)}, u32[]{:S(2)}) %collective-permute-start.22) | collective-permute-done | bytes 786464 | tf_op jit(solution)/shard_map/ppermute | solution.py:274
  191.0 1.8 decode.47
  192.8 1.8 decode.50
  194.6 1.8 decode.51
  196.3 9.2 %collective-permute-done.32.refs_0_ = bf16[192,2048]{1,0:T(8,128)(2,1)S(1)} collective-permute-done((bf16[192,2048]{1,0:T(8,128)(2,1)S(1)}, bf16[192,2048]{1,0:T(8,128)(2,1)S(1)}, u32[]{:S(2)}, u32[]{:S(2)}) %collective-permute-start.32) | collective-permute-done | bytes 786464 | tf_op jit(solution)/shard_map/ppermute | solution.py:276
  205.5 1.5 collective-permute-start.37
  207.0 1.8 decode.48
  208.9 1.8 decode.49
  211.1 10.1 %collective-permute-done.28 = bf16[192,2048]{1,0:T(8,128)(2,1)S(1)} collective-permute-done((bf16[192,2048]{1,0:T(8,128)(2,1)S(1)}, bf16[192,2048]{1,0:T(8,128)(2,1)S(1)}, u32[]{:S(2)}, u32[]{:S(2)}) %collective-permute-start.28) | collective-permute-done | bytes 786464 | tf_op jit(solution)/shard_map/ppermute | solution.py:274
  222.5 1.8 decode.52
  224.2 1.8 decode.53
  226.4 4.9 %collective-permute-start.35 = (bf16[192,2048]{1,0:T(8,128)(2,1)S(1)}, bf16[192,2048]{1,0:T(8,128)(2,1)S(1)}, u32[]{:S(2)}, u32[]{:S(2)}) collective-permute-start(bf16[192,2048]{1,0:T(8,128)(2,1)S(1)} %get-tuple-element.175.refs_0_), channel_id=1, source_target_pairs={{0,8},{4,12},{8,0},{12,4},{16,24},{20,28},{24,16},{28,20},{1,9},{5... | collective-permute-start | bytes 2359304 | tf_op jit(solution)/shard_map/ppermute | solution.py:274
  231.4 6.7 %collective-permute-done.37 = bf16[192,2048]{1,0:T(8,128)(2,1)S(1)} collective-permute-done((bf16[192,2048]{1,0:T(8,128)(2,1)S(1)}, bf16[192,2048]{1,0:T(8,128)(2,1)S(1)}, u32[]{:S(2)}, u32[]{:S(2)}) %collective-permute-start.37) | collective-permute-done | bytes 786464 | tf_op jit(solution)/shard_map/ppermute | solution.py:274
  239.2 4.5 %collective-permute-start.40 = (bf16[144,2048]{1,0:T(8,128)(2,1)S(1)}, bf16[144,2048]{1,0:T(8,128)(2,1)S(1)}, u32[]{:S(2)}, u32[]{:S(2)}) collective-permute-start(bf16[144,2048]{1,0:T(8,128)(2,1)S(1)} %slice.35), channel_id=1, source_target_pairs={{0,8},{4,12},{8,0},{12,4},{16,24},{20,28},{24,16},{28,20},{1,9},{5... | collective-permute-start | bytes 1769480 | tf_op jit(solution)/shard_map/ppermute | solution.py:274
  244.7 8.7 %collective-permute-done.35.refs_0_ = bf16[192,2048]{1,0:T(8,128)(2,1)S(1)} collective-permute-done((bf16[192,2048]{1,0:T(8,128)(2,1)S(1)}, bf16[192,2048]{1,0:T(8,128)(2,1)S(1)}, u32[]{:S(2)}, u32[]{:S(2)}) %collective-permute-start.35) | collective-permute-done | bytes 786464 | tf_op jit(solution)/shard_map/ppermute | solution.py:274
  253.7 1.8 decode.56
  255.4 1.8 decode.57
  257.2 1.8 decode.54
  259.0 1.8 decode.55
  261.8 2.0 decode.58
  263.8 1.5 decode.59
  (93 shorter events, 34.5 us)
Async XLA Ops:
  2.9 20.8 %collective-permute-start.2 = (bf16[192,2048]{1,0:T(8,128)(2,1)S(1)}, bf16[192,2048]{1,0:T(8,128)(2,1)}, u32[]{:S(2)}, u32[]{:S(2)}) collective-permute-start(bf16[192,2048]{1,0:T(8,128)(2,1)S(1)} %get-tuple-element.107.refs_0_), channel_id=1, source_target_pairs={{0,4},{1,9},{2,6},{3,11},{4,0},{5,13},{6,2},{7,15},{8,12},{9,1},{1... | collective-permute-start | bytes 2359304 | tf_op jit(solution)/shard_map/ppermute | solution.py:329
  6.0 20.4 %collective-permute-start.1 = (bf16[192,2048]{1,0:T(8,128)(2,1)S(1)}, bf16[192,2048]{1,0:T(8,128)(2,1)S(1)}, u32[]{:S(2)}, u32[]{:S(2)}) collective-permute-start(bf16[192,2048]{1,0:T(8,128)(2,1)S(1)} %get-tuple-element.107.refs_0_), channel_id=1, source_target_pairs={{0,8},{1,5},{2,10},{3,7},{4,12},{5,1},{6,14},{7,3},{8,0},{9,13},{1... | collective-permute-start | bytes 2359304 | tf_op jit(solution)/shard_map/ppermute | solution.py:329
  7.5 33.4 %collective-permute-start.3 = (bf16[192,2048]{1,0:T(8,128)(2,1)S(1)}, bf16[192,2048]{1,0:T(8,128)(2,1)}, u32[]{:S(2)}, u32[]{:S(2)}) collective-permute-start(bf16[192,2048]{1,0:T(8,128)(2,1)S(1)} %get-tuple-element.107.refs_0_), channel_id=1, source_target_pairs={{8,16},{12,20},{16,8},{20,12},{9,17},{13,21},{17,9},{21,13},{10,18... | collective-permute-start | bytes 2359304 | tf_op jit(solution)/shard_map/ppermute | solution.py:274
  9.1 0.7 copy-start.6
  16.0 0.9 copy-start
  16.9 0.9 copy-start.2
  17.7 25.7 %collective-permute-start.7 = (bf16[192,2048]{1,0:T(8,128)(2,1)}, bf16[192,2048]{1,0:T(8,128)(2,1)}, u32[]{:S(2)}, u32[]{:S(2)}) collective-permute-start(bf16[192,2048]{1,0:T(8,128)(2,1)} %get-tuple-element.110.refs_0_), channel_id=1, source_target_pairs={{8,16},{12,20},{16,8},{20,12},{9,17},{13,21},{17,9},{21,13},{10,18... | collective-permute-start | bytes 2359304 | tf_op jit(solution)/shard_map/ppermute | solution.py:274
  19.3 28.5 %collective-permute-start.6 = (bf16[192,2048]{1,0:T(8,128)(2,1)}, bf16[192,2048]{1,0:T(8,128)(2,1)}, u32[]{:S(2)}, u32[]{:S(2)}) collective-permute-start(bf16[192,2048]{1,0:T(8,128)(2,1)} %get-tuple-element.110.refs_0_), channel_id=1, source_target_pairs={{0,8},{4,12},{8,0},{12,4},{16,24},{20,28},{24,16},{28,20},{1,9},{5... | collective-permute-start | bytes 2359304 | tf_op jit(solution)/shard_map/ppermute | solution.py:274
  23.8 25.1 %collective-permute-start.5 = (bf16[192,2048]{1,0:T(8,128)(2,1)}, bf16[192,2048]{1,0:T(8,128)(2,1)S(1)}, u32[]{:S(2)}, u32[]{:S(2)}) collective-permute-start(bf16[192,2048]{1,0:T(8,128)(2,1)} %get-tuple-element.110.refs_0_), channel_id=1, source_target_pairs={{0,4},{4,0},{8,12},{12,8},{16,20},{20,16},{24,28},{28,24},{1,5},{5... | collective-permute-start | bytes 2359304 | tf_op jit(solution)/shard_map/ppermute | solution.py:276
  26.3 0.9 copy-start.11
  27.2 13.8 %collective-permute-start = (f32[3,1,2048]{2,1,0:T(1,128)S(1)}, f32[3,1,2048]{2,1,0:T(1,128)S(1)}, u32[]{:S(2)}, u32[]{:S(2)}) collective-permute-start(f32[3,1,2048]{2,1,0:T(1,128)S(1)} %get-tuple-element.106.m0_ref), channel_id=1, source_target_pairs={{0,8},{4,12},{8,0},{12,4},{16,24},{20,28},{24,16},{28,20},{1,9},{5... | collective-permute-start | bytes 73736 | tf_op jit(solution)/shard_map/ppermute | solution.py:274
  41.0 38.2 %collective-permute-start.12 = (bf16[192,2048]{1,0:T(8,128)(2,1)}, bf16[192,2048]{1,0:T(8,128)(2,1)S(1)}, u32[]{:S(2)}, u32[]{:S(2)}) collective-permute-start(bf16[192,2048]{1,0:T(8,128)(2,1)} %copy-done.2), channel_id=1, source_target_pairs={{8,16},{12,20},{16,8},{20,12},{9,17},{13,21},{17,9},{21,13},{10,18... | collective-permute-start | bytes 2359304 | tf_op jit(solution)/shard_map/ppermute | solution.py:274
  41.7 37.8 %collective-permute-start.11 = (bf16[192,2048]{1,0:T(8,128)(2,1)}, bf16[192,2048]{1,0:T(8,128)(2,1)S(1)}, u32[]{:S(2)}, u32[]{:S(2)}) collective-permute-start(bf16[192,2048]{1,0:T(8,128)(2,1)} %copy-done.2), channel_id=1, source_target_pairs={{0,4},{4,0},{8,12},{12,8},{16,20},{20,16},{24,28},{28,24},{1,5},{5... | collective-permute-start | bytes 2359304 | tf_op jit(solution)/shard_map/ppermute | solution.py:276
  43.4 37.0 %collective-permute-start.10 = (bf16[192,2048]{1,0:T(8,128)(2,1)}, bf16[192,2048]{1,0:T(8,128)(2,1)}, u32[]{:S(2)}, u32[]{:S(2)}) collective-permute-start(bf16[192,2048]{1,0:T(8,128)(2,1)} %copy-done.2), channel_id=1, source_target_pairs={{0,8},{4,12},{8,0},{12,4},{16,24},{20,28},{24,16},{28,20},{1,9},{5... | collective-permute-start | bytes 2359304 | tf_op jit(solution)/shard_map/ppermute | solution.py:274
  47.8 16.7 %collective-permute-start.4 = (f32[6,1,2048]{2,1,0:T(1,128)S(1)}, f32[6,1,2048]{2,1,0:T(1,128)S(1)}, u32[]{:S(2)}, u32[]{:S(2)}) collective-permute-start(f32[6,1,2048]{2,1,0:T(1,128)S(1)} %pad_maximum_fusion), channel_id=1, source_target_pairs={{0,16},{4,20},{16,0},{20,4},{8,24},{12,28},{24,8},{28,12},{1,17},{... | collective-permute-start | bytes 147464 | tf_op jit(solution)/shard_map/ppermute | solution.py:274
  64.5 18.9 %collective-permute-start.23 = (bf16[192,2048]{1,0:T(8,128)(2,1)}, bf16[192,2048]{1,0:T(8,128)(2,1)S(1)}, u32[]{:S(2)}, u32[]{:S(2)}) collective-permute-start(bf16[192,2048]{1,0:T(8,128)(2,1)} %copy-done), channel_id=1, source_target_pairs={{8,16},{12,20},{16,8},{20,12},{9,17},{13,21},{17,9},{21,13},{10,18... | collective-permute-start | bytes 2359304 | tf_op jit(solution)/shard_map/ppermute | solution.py:274
  65.3 3.8 %collective-permute-start.9 = (f32[2,1,2048]{2,1,0:T(1,128)S(1)}, f32[2,1,2048]{2,1,0:T(1,128)S(1)}, u32[]{:S(2)}, u32[]{:S(2)}) collective-permute-start(f32[2,1,2048]{2,1,0:T(1,128)S(1)} %get-tuple-element.113.most0_ref), channel_id=1, source_target_pairs={{0,4},{4,0},{8,12},{12,8},{16,20},{20,16},{24,28},{28,24},{1,5},{5... | collective-permute-start | bytes 49160 | tf_op jit(solution)/shard_map/ppermute | solution.py:276
  69.1 4.3 %collective-permute-start.8 = (bf16[16,2048]{1,0:T(8,128)(2,1)S(1)}, bf16[16,2048]{1,0:T(8,128)(2,1)S(1)}, u32[]{:S(2)}, u32[]{:S(2)}) collective-permute-start(bf16[16,2048]{1,0:T(8,128)(2,1)S(1)} %get-tuple-element.111.scale0_ref), channel_id=1, source_target_pairs={{0,4},{4,0},{8,12},{12,8},{16,20},{20,16},{24,28},{28,24},{1,5},{5... | collective-permute-start | bytes 196616 | tf_op jit(solution)/shard_map/ppermute | solution.py:276
  73.3 24.5 %collective-permute-start.20 = (bf16[192,2048]{1,0:T(8,128)(2,1)}, bf16[192,2048]{1,0:T(8,128)(2,1)}, u32[]{:S(2)}, u32[]{:S(2)}) collective-permute-start(bf16[192,2048]{1,0:T(8,128)(2,1)} %copy-done), channel_id=1, source_target_pairs={{0,8},{4,12},{8,0},{12,4},{16,24},{20,28},{24,16},{28,20},{1,9},{5... | collective-permute-start | bytes 2359304 | tf_op jit(solution)/shard_map/ppermute | solution.py:274
  79.2 4.2 %copy-start.7 = (bf16[192,2048]{1,0:T(8,128)(2,1)}, bf16[192,2048]{1,0:T(8,128)(2,1)S(1)}, u32[]{:S(2)}) copy-start(bf16[192,2048]{1,0:T(8,128)(2,1)S(1)} %collective-permute-done.12) | copy-start | bytes 2359300
  79.2 20.7 %collective-permute-start.19 = (bf16[192,2048]{1,0:T(8,128)(2,1)}, bf16[192,2048]{1,0:T(8,128)(2,1)}, u32[]{:S(2)}, u32[]{:S(2)}) collective-permute-start(bf16[192,2048]{1,0:T(8,128)(2,1)} %copy-done), channel_id=1, source_target_pairs={{0,4},{4,0},{8,12},{12,8},{16,20},{20,16},{24,28},{28,24},{1,5},{5... | collective-permute-start | bytes 2359304 | tf_op jit(solution)/shard_map/ppermute | solution.py:276
  79.5 0.9 copy-start.4
  80.4 36.3 %collective-permute-start.13 = (bf16[192,2048]{1,0:T(8,128)(2,1)}, bf16[192,2048]{1,0:T(8,128)(2,1)}, u32[]{:S(2)}, u32[]{:S(2)}) collective-permute-start(bf16[192,2048]{1,0:T(8,128)(2,1)} %collective-permute-done.10.refs_0_), channel_id=1, source_target_pairs={{0,4},{4,0},{8,12},{12,8},{16,20},{20,16},{24,28},{28,24},{1,5},{5... | collective-permute-start | bytes 2359304 | tf_op jit(solution)/shard_map/ppermute | solution.py:276
  82.1 49.1 %collective-permute-start.14 = (bf16[192,2048]{1,0:T(8,128)(2,1)}, bf16[192,2048]{1,0:T(8,128)(2,1)}, u32[]{:S(2)}, u32[]{:S(2)}) collective-permute-start(bf16[192,2048]{1,0:T(8,128)(2,1)} %collective-permute-done.3), channel_id=1, source_target_pairs={{8,0},{12,4},{16,24},{20,28},{9,1},{13,5},{17,25},{21,29},{10,2},{... | collective-permute-start | bytes 2359304 | tf_op jit(solution)/shard_map/ppermute | solution.py:274
  83.4 0.9 copy-start.9
  84.3 46.9 %collective-permute-start.15 = (bf16[192,2048]{1,0:T(8,128)(2,1)S(1)}, bf16[192,2048]{1,0:T(8,128)(2,1)}, u32[]{:S(2)}, u32[]{:S(2)}) collective-permute-start(bf16[192,2048]{1,0:T(8,128)(2,1)S(1)} %get-tuple-element.119.refs_0_), channel_id=1, source_target_pairs={{8,16},{12,20},{16,8},{20,12},{9,17},{13,21},{17,9},{21,13},{10,18... | collective-permute-start | bytes 2359304 | tf_op jit(solution)/shard_map/ppermute | solution.py:274
  85.9 1.1 copy-start.3
  89.3 1.1 copy-start.1
  99.9 34.6 %collective-permute-start.24 = (bf16[192,2048]{1,0:T(8,128)(2,1)}, bf16[192,2048]{1,0:T(8,128)(2,1)}, u32[]{:S(2)}, u32[]{:S(2)}) collective-permute-start(bf16[192,2048]{1,0:T(8,128)(2,1)} %collective-permute-done.7), channel_id=1, source_target_pairs={{8,0},{12,4},{16,24},{20,28},{9,1},{13,5},{17,25},{21,29},{10,2},{... | collective-permute-start | bytes 2359304 | tf_op jit(solution)/shard_map/ppermute | solution.py:274
  101.2 33.7 %collective-permute-start.25 = (bf16[192,2048]{1,0:T(8,128)(2,1)}, bf16[192,2048]{1,0:T(8,128)(2,1)}, u32[]{:S(2)}, u32[]{:S(2)}) collective-permute-start(bf16[192,2048]{1,0:T(8,128)(2,1)} %collective-permute-done.20.refs_0_), channel_id=1, source_target_pairs={{0,4},{4,0},{8,12},{12,8},{16,20},{20,16},{24,28},{28,24},{1,5},{5... | collective-permute-start | bytes 2359304 | tf_op jit(solution)/shard_map/ppermute | solution.py:276
  116.7 18.2 %collective-permute-start.26 = (bf16[192,2048]{1,0:T(8,128)(2,1)}, bf16[192,2048]{1,0:T(8,128)(2,1)}, u32[]{:S(2)}, u32[]{:S(2)}) collective-permute-start(bf16[192,2048]{1,0:T(8,128)(2,1)} %collective-permute-done.6.refs_0_), channel_id=1, source_target_pairs={{8,16},{12,20},{16,8},{20,12},{9,17},{13,21},{17,9},{21,13},{10,18... | collective-permute-start | bytes 2359304 | tf_op jit(solution)/shard_map/ppermute | solution.py:274
  121.8 4.7 %copy-start.5 = (bf16[192,2048]{1,0:T(8,128)(2,1)S(1)}, bf16[192,2048]{1,0:T(8,128)(2,1)}, u32[]{:S(2)}) copy-start(bf16[192,2048]{1,0:T(8,128)(2,1)} %copy-done.4) | copy-start | bytes 2359300
  126.5 6.7 %copy-start.8 = (bf16[192,2048]{1,0:T(8,128)(2,1)S(1)}, bf16[192,2048]{1,0:T(8,128)(2,1)}, u32[]{:S(2)}) copy-start(bf16[192,2048]{1,0:T(8,128)(2,1)} %copy-done.7) | copy-start | bytes 2359300
  126.5 11.4 %copy-start.10 = (bf16[192,2048]{1,0:T(8,128)(2,1)S(1)}, bf16[192,2048]{1,0:T(8,128)(2,1)}, u32[]{:S(2)}) copy-start(bf16[192,2048]{1,0:T(8,128)(2,1)} %copy-done.9) | copy-start | bytes 2359300
  131.2 8.0 %collective-permute-start.16 = (bf16[192,2048]{1,0:T(8,128)(2,1)}, bf16[192,2048]{1,0:T(8,128)(2,1)S(1)}, u32[]{:S(2)}, u32[]{:S(2)}) collective-permute-start(bf16[192,2048]{1,0:T(8,128)(2,1)} %collective-permute-done.10.refs_0_), channel_id=1, source_target_pairs={{8,16},{12,20},{16,8},{20,12},{9,17},{13,21},{17,9},{21,13},{10,18... | collective-permute-start | bytes 2359304 | tf_op jit(solution)/shard_map/ppermute | solution.py:274
  133.2 22.1 %collective-permute-start.17 = (bf16[192,2048]{1,0:T(8,128)(2,1)S(1)}, bf16[192,2048]{1,0:T(8,128)(2,1)S(1)}, u32[]{:S(2)}, u32[]{:S(2)}) collective-permute-start(bf16[192,2048]{1,0:T(8,128)(2,1)S(1)} %copy-done.8), channel_id=1, source_target_pairs={{8,0},{12,4},{16,24},{20,28},{9,1},{13,5},{17,25},{21,29},{10,2},{... | collective-permute-start | bytes 2359304 | tf_op jit(solution)/shard_map/ppermute | solution.py:274
  134.5 20.8 %collective-permute-start.18 = (bf16[192,2048]{1,0:T(8,128)(2,1)S(1)}, bf16[192,2048]{1,0:T(8,128)(2,1)S(1)}, u32[]{:S(2)}, u32[]{:S(2)}) collective-permute-start(bf16[192,2048]{1,0:T(8,128)(2,1)S(1)} %broadcast_select_fusion.6.refs_0_), channel_id=1, source_target_pairs={{0,4},{4,0},{8,12},{12,8},{16,20},{20,16},{24,28},{28,24},{1,5},{5... | collective-permute-start | bytes 2359304 | tf_op jit(solution)/shard_map/ppermute | solution.py:276
  136.2 35.7 %collective-permute-start.27 = (bf16[192,2048]{1,0:T(8,128)(2,1)S(1)}, bf16[192,2048]{1,0:T(8,128)(2,1)S(1)}, u32[]{:S(2)}, u32[]{:S(2)}) collective-permute-start(bf16[192,2048]{1,0:T(8,128)(2,1)S(1)} %broadcast_select_fusion.5.refs_0_), channel_id=1, source_target_pairs={{0,4},{4,0},{8,12},{12,8},{16,20},{20,16},{24,28},{28,24},{1,5},{5... | collective-permute-start | bytes 2359304 | tf_op jit(solution)/shard_map/ppermute | solution.py:276
  137.9 33.9 %collective-permute-start.30 = (bf16[192,2048]{1,0:T(8,128)(2,1)S(1)}, bf16[192,2048]{1,0:T(8,128)(2,1)S(1)}, u32[]{:S(2)}, u32[]{:S(2)}) collective-permute-start(bf16[192,2048]{1,0:T(8,128)(2,1)S(1)} %copy-done.10), channel_id=1, source_target_pairs={{8,0},{12,4},{16,24},{20,28},{9,1},{13,5},{17,25},{21,29},{10,2},{... | collective-permute-start | bytes 2359304 | tf_op jit(solution)/shard_map/ppermute | solution.py:274
  139.2 32.6 %collective-permute-start.31 = (bf16[192,2048]{1,0:T(8,128)(2,1)}, bf16[192,2048]{1,0:T(8,128)(2,1)S(1)}, u32[]{:S(2)}, u32[]{:S(2)}) collective-permute-start(bf16[192,2048]{1,0:T(8,128)(2,1)} %collective-permute-done.20.refs_0_), channel_id=1, source_target_pairs={{8,16},{12,20},{16,8},{20,12},{9,17},{13,21},{17,9},{21,13},{10,18... | collective-permute-start | bytes 2359304 | tf_op jit(solution)/shard_map/ppermute | solution.py:274
  155.3 32.2 %collective-permute-start.22 = (bf16[192,2048]{1,0:T(8,128)(2,1)}, bf16[192,2048]{1,0:T(8,128)(2,1)S(1)}, u32[]{:S(2)}, u32[]{:S(2)}) collective-permute-start(bf16[192,2048]{1,0:T(8,128)(2,1)} %collective-permute-done.15), channel_id=1, source_target_pairs={{8,0},{12,4},{16,24},{20,28},{9,1},{13,5},{17,25},{21,29},{10,2},{... | collective-permute-start | bytes 2359304 | tf_op jit(solution)/shard_map/ppermute | solution.py:274
  160.2 28.4 %collective-permute-start.21 = (bf16[192,2048]{1,0:T(8,128)(2,1)S(1)}, bf16[192,2048]{1,0:T(8,128)(2,1)S(1)}, u32[]{:S(2)}, u32[]{:S(2)}) collective-permute-start(bf16[192,2048]{1,0:T(8,128)(2,1)S(1)} %broadcast_select_fusion.7.refs_0_), channel_id=1, source_target_pairs={{0,4},{4,0},{8,12},{12,8},{16,20},{20,16},{24,28},{28,24},{1,5},{5... | collective-permute-start | bytes 2359304 | tf_op jit(solution)/shard_map/ppermute | solution.py:276
  171.9 33.6 %collective-permute-start.32 = (bf16[192,2048]{1,0:T(8,128)(2,1)S(1)}, bf16[192,2048]{1,0:T(8,128)(2,1)S(1)}, u32[]{:S(2)}, u32[]{:S(2)}) collective-permute-start(bf16[192,2048]{1,0:T(8,128)(2,1)S(1)} %broadcast_select_fusion.2.refs_0_), channel_id=1, source_target_pairs={{0,4},{4,0},{8,12},{12,8},{16,20},{20,16},{24,28},{28,24},{1,5},{5... | collective-permute-start | bytes 2359304 | tf_op jit(solution)/shard_map/ppermute | solution.py:276
  172.4 33.2 %collective-permute-start.33 = (bf16[192,2048]{1,0:T(8,128)(2,1)}, bf16[192,2048]{1,0:T(8,128)(2,1)S(1)}, u32[]{:S(2)}, u32[]{:S(2)}) collective-permute-start(bf16[192,2048]{1,0:T(8,128)(2,1)} %collective-permute-done.26), channel_id=1, source_target_pairs={{8,0},{12,4},{16,24},{20,28},{9,1},{13,5},{17,25},{21,29},{10,2},{... | collective-permute-start | bytes 2359304 | tf_op jit(solution)/shard_map/ppermute | solution.py:274
  188.7 32.6 %collective-permute-start.28 = (bf16[192,2048]{1,0:T(8,128)(2,1)S(1)}, bf16[192,2048]{1,0:T(8,128)(2,1)S(1)}, u32[]{:S(2)}, u32[]{:S(2)}) collective-permute-start(bf16[192,2048]{1,0:T(8,128)(2,1)S(1)} %collective-permute-done.16), channel_id=1, source_target_pairs={{8,0},{12,4},{16,24},{20,28},{9,1},{13,5},{17,25},{21,29},{10,2},{... | collective-permute-start | bytes 2359304 | tf_op jit(solution)/shard_map/ppermute | solution.py:274
  190.0 32.4 %collective-permute-start.29 = (bf16[192,2048]{1,0:T(8,128)(2,1)S(1)}, bf16[192,2048]{1,0:T(8,128)(2,1)S(1)}, u32[]{:S(2)}, u32[]{:S(2)}) collective-permute-start(bf16[192,2048]{1,0:T(8,128)(2,1)S(1)} %broadcast_select_fusion.3.refs_0_), channel_id=1, source_target_pairs={{0,4},{4,0},{8,12},{12,8},{16,20},{20,16},{24,28},{28,24},{1,5},{5... | collective-permute-start | bytes 2359304 | tf_op jit(solution)/shard_map/ppermute | solution.py:276
  205.5 32.6 %collective-permute-start.37 = (bf16[192,2048]{1,0:T(8,128)(2,1)S(1)}, bf16[192,2048]{1,0:T(8,128)(2,1)S(1)}, u32[]{:S(2)}, u32[]{:S(2)}) collective-permute-start(bf16[192,2048]{1,0:T(8,128)(2,1)S(1)} %collective-permute-done.31), channel_id=1, source_target_pairs={{8,0},{12,4},{16,24},{20,28},{9,1},{13,5},{17,25},{21,29},{10,2},{... | collective-permute-start | bytes 2359304 | tf_op jit(solution)/shard_map/ppermute | solution.py:274
  210.7 28.6 %collective-permute-start.36 = (bf16[192,2048]{1,0:T(8,128)(2,1)S(1)}, bf16[192,2048]{1,0:T(8,128)(2,1)S(1)}, u32[]{:S(2)}, u32[]{:S(2)}) collective-permute-start(bf16[192,2048]{1,0:T(8,128)(2,1)S(1)} %broadcast_select_fusion.1.refs_0_), channel_id=1, source_target_pairs={{0,4},{4,0},{8,12},{12,8},{16,20},{20,16},{24,28},{28,24},{1,5},{5... | collective-permute-start | bytes 2359304 | tf_op jit(solution)/shard_map/ppermute | solution.py:276
  226.0 33.0 %collective-permute-start.34 = (bf16[192,2048]{1,0:T(8,128)(2,1)S(1)}, bf16[192,2048]{1,0:T(8,128)(2,1)S(1)}, u32[]{:S(2)}, u32[]{:S(2)}) collective-permute-start(bf16[192,2048]{1,0:T(8,128)(2,1)S(1)} %broadcast_select_fusion.4.refs_0_), channel_id=1, source_target_pairs={{0,4},{4,0},{8,12},{12,8},{16,20},{20,16},{24,28},{28,24},{1,5},{5... | collective-permute-start | bytes 2359304 | tf_op jit(solution)/shard_map/ppermute | solution.py:276
  226.4 26.9 %collective-permute-start.35 = (bf16[192,2048]{1,0:T(8,128)(2,1)S(1)}, bf16[192,2048]{1,0:T(8,128)(2,1)S(1)}, u32[]{:S(2)}, u32[]{:S(2)}) collective-permute-start(bf16[192,2048]{1,0:T(8,128)(2,1)S(1)} %get-tuple-element.175.refs_0_), channel_id=1, source_target_pairs={{0,8},{4,12},{8,0},{12,4},{16,24},{20,28},{24,16},{28,20},{1,9},{5... | collective-permute-start | bytes 2359304 | tf_op jit(solution)/shard_map/ppermute | solution.py:274
  239.2 21.5 %collective-permute-start.40 = (bf16[144,2048]{1,0:T(8,128)(2,1)S(1)}, bf16[144,2048]{1,0:T(8,128)(2,1)S(1)}, u32[]{:S(2)}, u32[]{:S(2)}) collective-permute-start(bf16[144,2048]{1,0:T(8,128)(2,1)S(1)} %slice.35), channel_id=1, source_target_pairs={{0,8},{4,12},{8,0},{12,4},{16,24},{20,28},{24,16},{28,20},{1,9},{5... | collective-permute-start | bytes 1769480 | tf_op jit(solution)/shard_map/ppermute | solution.py:274
  243.7 17.1 %collective-permute-start.41 = (bf16[144,2048]{1,0:T(8,128)(2,1)S(1)}, bf16[144,2048]{1,0:T(8,128)(2,1)S(1)}, u32[]{:S(2)}, u32[]{:S(2)}) collective-permute-start(bf16[144,2048]{1,0:T(8,128)(2,1)S(1)} %slice_select_fusion), channel_id=1, source_target_pairs={{0,4},{4,0},{8,12},{12,8},{16,20},{20,16},{24,28},{28,24},{1,5},{5... | collective-permute-start | bytes 1769480 | tf_op jit(solution)/shard_map/ppermute | solution.py:276
  244.6 17.2 %collective-permute-start.38 = (bf16[48,2048]{1,0:T(8,128)(2,1)S(1)}, bf16[48,2048]{1,0:T(8,128)(2,1)S(1)}, u32[]{:S(2)}, u32[]{:S(2)}) collective-permute-start(bf16[48,2048]{1,0:T(8,128)(2,1)S(1)} %slice.32), channel_id=1, source_target_pairs={{0,8},{4,12},{8,0},{12,4},{16,24},{20,28},{24,16},{28,20},{1,9},{5... | collective-permute-start | bytes 589832 | tf_op jit(solution)/shard_map/ppermute | solution.py:274
  253.4 8.1 %collective-permute-start.39 = (bf16[48,2048]{1,0:T(8,128)(2,1)S(1)}, bf16[48,2048]{1,0:T(8,128)(2,1)S(1)}, u32[]{:S(2)}, u32[]{:S(2)}) collective-permute-start(bf16[48,2048]{1,0:T(8,128)(2,1)S(1)} %slice_select_fusion.1), channel_id=1, source_target_pairs={{0,4},{4,0},{8,12},{12,8},{16,20},{20,16},{24,28},{28,24},{1,5},{5... | collective-permute-start | bytes 589832 | tf_op jit(solution)/shard_map/ppermute | solution.py:276

commit v5 on v4

--- a/solution.py
+++ b/solution.py
@@ -14,7 +14,7 @@
 SCALE_OF_CHUNK = (0, 1, 2, 1)
 
 
-KERNEL_VMEM = 14 * 2**20
+MIB = 2**20
 
 
 def near_by(value):
@@ -49,7 +49,7 @@
     return jnp.where(x < 0, -y, y).astype(jnp.bfloat16)
 
 
-def encode_rest_body(gain_ref, wu0, au0, wg, ag, wu1, au1, first_ref, up0, gate, up1, m_ref):
+def encode_rest_body(gain_ref, wu0, au0, wg, ag, wu1, au1, first_ref, first_max_ref, own_ref, up0, gate, up1, m_ref):
     half_rows, width = wg.shape
     tall = tall_gain(gain_ref, width)
     top, bottom = tall[:half_rows], tall[half_rows:]
@@ -62,23 +62,25 @@
     m = largest(x)
     gate[...] = coded(x, m)
     m_ref[2] = m
-    m_ref[0] = first_ref[0]
-
-
-def encode_rest(w_gate, avg_gate, w_up, avg_up, gain, first_maxima, block):
+    m_ref[0] = first_max_ref[0]
+    own_ref[...] = first_ref[...]
+
+
+def encode_rest(w_gate, avg_gate, w_up, avg_up, gain, first, first_maxima, block):
     half_rows, columns = w_gate.shape[0] // 2, w_gate.shape[1]
     half = lambda h: [pl.BlockSpec((half_rows, block), lambda j: (h, j))] * 2
     stacked = lambda n: pl.BlockSpec((n, 1, block), lambda j: (0, 0, j))
-    chunk = jax.ShapeDtypeStruct((half_rows, columns), jnp.bfloat16)
+    whole = pl.BlockSpec((half_rows, block), lambda j: (0, j))
+    chunk = pltpu.HBM((half_rows, columns), jnp.bfloat16)
     return pl.pallas_call(
         encode_rest_body,
         grid=(columns // block,),
-        in_specs=[pl.BlockSpec(gain.shape, lambda j: (0,)), *half(0), *half(1), *half(1), stacked(1)],
-        out_specs=[pl.BlockSpec((half_rows, block), lambda j: (0, j))] * 3 + [stacked(3)],
-        out_shape=[chunk, chunk, chunk, jax.ShapeDtypeStruct((3, 1, columns), jnp.float32)],
-        compiler_params=pltpu.CompilerParams(vmem_limit_bytes=KERNEL_VMEM),
+        in_specs=[pl.BlockSpec(gain.shape, lambda j: (0,)), *half(0), *half(1), *half(1), whole, stacked(1)],
+        out_specs=[whole] * 4 + [stacked(3)],
+        out_shape=[chunk] * 4 + [jax.ShapeDtypeStruct((3, 1, columns), jnp.float32)],
+        compiler_params=pltpu.CompilerParams(vmem_limit_bytes=12 * MIB),
         name="encode_rest",
-    )(gain, *map(stay_out, (w_up, avg_up, w_gate, avg_gate, w_up, avg_up)), near_by(first_maxima))
+    )(gain, *map(stay_out, (w_up, avg_up, w_gate, avg_gate, w_up, avg_up)), near_by(first), near_by(first_maxima))
 
 
 def encode_first_body(g_ref, w_ref, a_ref, y_ref, m_ref, gain_ref, ws, avgs, sems, *, half):
@@ -122,7 +124,7 @@
             pltpu.VMEM((1, 1, columns), jnp.float32),
         ],
         scratch_shapes=[pltpu.VMEM(gain.shape, gain.dtype), held, held, pltpu.SemaphoreType.DMA((3, columns // width))],
-        compiler_params=pltpu.CompilerParams(vmem_limit_bytes=KERNEL_VMEM),
+        compiler_params=pltpu.CompilerParams(vmem_limit_bytes=6 * MIB),
         name="encode_first",
     )(stay_out(gain), stay_out(w), stay_out(avg))
 
@@ -143,7 +145,7 @@
             pltpu.VMEM((16, columns), jnp.bfloat16),
             pltpu.VMEM((2, 1, columns), jnp.float32),
         ],
-        compiler_params=pltpu.CompilerParams(vmem_limit_bytes=KERNEL_VMEM),
+        compiler_params=pltpu.CompilerParams(vmem_limit_bytes=4 * MIB),
         name="half_table",
     )(*map(near_by, maxima))
 
@@ -167,7 +169,7 @@
             pltpu.VMEM((24, 1, columns), jnp.float32),
             jax.ShapeDtypeStruct((2, columns), jnp.float32),
         ],
-        compiler_params=pltpu.CompilerParams(vmem_limit_bytes=KERNEL_VMEM),
+        compiler_params=pltpu.CompilerParams(vmem_limit_bytes=4 * MIB),
         name="ratios",
     )(*map(near_by, scales), *map(near_by, most))
 
@@ -219,7 +221,7 @@
             pltpu.SemaphoreType.DMA((len(chunks), pieces)),
         ],
         input_output_aliases={2 + len(chunks): 0} if begun else {},
-        compiler_params=pltpu.CompilerParams(vmem_limit_bytes=KERNEL_VMEM),
+        compiler_params=pltpu.CompilerParams(vmem_limit_bytes=4 * MIB),
         name="decode",
     )(me, near_by(ratios), *map(near_by, chunks), *[whole] * begun)
 
@@ -280,8 +282,7 @@
     skip = lambda value: hop(value, [(0, 2), (2, 0), (1, 3), (3, 1)])
 
     first, first_maxima = encode_first(w_gate, avg_gate, norm_gain, 0, block // 4)
-    *rest, maxima = encode_rest(w_gate, avg_gate, w_up, avg_up, norm_gain, first_maxima, block // 2)
-    own = [first, *rest]
+    *own, maxima = encode_rest(w_gate, avg_gate, w_up, avg_up, norm_gain, first, first_maxima, block // 2)
 
     X, B, M, O, V, F = {}, {}, {}, {}, {}, {}
     tables = [maxima]

time: 269 us -> 267 us (level)
    unnamed x24 -> x22, local copies, waits for them, and re-layouts: 7.36 us -> 7.03 us
  transfers between devices with their start and end apart: 42 -> 42, of which waited for: 19 -> 18; matrix products, arithmetic and copies ran while one was open for 2% -> 2% of each run, Pallas kernels for 24% -> 24%
where the time goes in v5:
time: 267 us; the launch traced here: 264 us
  waiting for transfers between devices  116 us (43%)
  Pallas kernels  68.5 us (26%)
  starting transfers between devices  65.5 us (25%)
  local copies, waits for them, and re-layouts  7.71 us (3%)
  other arithmetic  4.57 us (2%)
    ppermute x24, waiting for transfers between devices, hop(): return lax.ppermute(value, 'rows', both)  68 us
    pallas_call x30, Pallas kernels, decode(): pl.pallas_call(functools.partial(decode_body, places=places, pieces=piece...  59.4 us
    ppermute x16, waiting for transfers between devices, local_plane(): lax.ppermute(value, 'rows', [(i, i ^ 1) for i in range(8)])  46.4 us
    ppermute x24, starting transfers between devices, hop(): return lax.ppermute(value, 'rows', both)  43.6 us
    ppermute x16, starting transfers between devices, local_plane(): lax.ppermute(value, 'rows', [(i, i ^ 1) for i in range(8)])  17.3 us
    unnamed x22, local copies, waits for them, and re-layouts  7.03 us
    pallas_call x1, Pallas kernels, encode_rest(): pl.pallas_call(encode_rest_body, grid=(columns // block,), in_specs=[pl.B...  6.66 us
  transfers between devices with their start and end apart: 42, of which 18 were waited for; matrix products, arithmetic and copies ran while one was open for 2% of the time, Pallas kernels for 24%

profile of v5, /device:TPU:0, one launch (start us, length us, event | category | flops | bytes accessed | tf_op | source)
XLA Modules:
  0.0 263.9 jit_solution(3778369384596258760)
XLA Ops:
  0.6 2.3 encode_first.1
  2.9 3.0 %collective-permute-start.2 = (bf16[192,2048]{1,0:T(8,128)(2,1)S(1)}, bf16[192,2048]{1,0:T(8,128)(2,1)S(1)}, u32[]{:S(2)}, u32[]{:S(2)}) collective-permute-start(bf16[192,2048]{1,0:T(8,128)(2,1)S(1)} %get-tuple-element.106.first_ref), channel_id=1, source_target_pairs={{0,4},{1,9},{2,6},{3,11},{4,0},{5,13},{6,2},{7,15},{8,12},{9,1},{1... | collective-permute-start | bytes 2359304 | tf_op jit(solution)/shard_map/ppermute | solution.py:330
  6.0 1.6 collective-permute-start.1
  7.5 1.5 collective-permute-start.3
  9.8 6.7 %encode_rest.1 = (bf16[192,2048]{1,0:T(8,128)(2,1)}, bf16[192,2048]{1,0:T(8,128)(2,1)}, bf16[192,2048]{1,0:T(8,128)(2,1)}, bf16[192,2048]{1,0:T(8,128)(2,1)}, f32[3,1,2048]{2,1,0:T(1,128)S(1)}) custom-call(f32[384]{0:T(512)S(1)} %copy-done.6, f32[384,2048]{1,0:T(8,128)} %wu1.1, f32[384,2048]{1,0:T(8,128)} %au1.1, f32[384,2048]{1,0:T(8,128)} %wg.1, ...), custom_call_target="tpu_custom_call" | custom-call | tf_op jit(solution)/shard_map/encode_rest/pallas_call | solution.py:75
  16.4 1.6 collective-permute-start.7
  18.0 3.9 %collective-permute-start.6 = (bf16[192,2048]{1,0:T(8,128)(2,1)}, bf16[192,2048]{1,0:T(8,128)(2,1)}, u32[]{:S(2)}, u32[]{:S(2)}) collective-permute-start(bf16[192,2048]{1,0:T(8,128)(2,1)} %get-tuple-element.111.refs_0_), channel_id=1, source_target_pairs={{0,8},{4,12},{8,0},{12,4},{16,24},{20,28},{24,16},{28,20},{1,9},{5... | collective-permute-start | bytes 2359304 | tf_op jit(solution)/shard_map/ppermute | solution.py:276
  21.9 1.8 collective-permute-done.2
  23.7 2.5 collective-permute-start.5
  27.9 1.5 broadcast_select_fusion.8
  29.4 11.6 %collective-permute-done.m1_ref = f32[3,1,2048]{2,1,0:T(1,128)S(1)} collective-permute-done((f32[3,1,2048]{2,1,0:T(1,128)S(1)}, f32[3,1,2048]{2,1,0:T(1,128)S(1)}, u32[]{:S(2)}, u32[]{:S(2)}) %collective-permute-start) | collective-permute-done | bytes 24608 | tf_op jit(solution)/shard_map/ppermute | solution.py:276
  41.7 1.7 collective-permute-start.11
  43.4 4.3 %collective-permute-start.10 = (bf16[192,2048]{1,0:T(8,128)(2,1)}, bf16[192,2048]{1,0:T(8,128)(2,1)}, u32[]{:S(2)}, u32[]{:S(2)}) collective-permute-start(bf16[192,2048]{1,0:T(8,128)(2,1)} %get-tuple-element.117.refs_1_), channel_id=1, source_target_pairs={{0,8},{4,12},{8,0},{12,4},{16,24},{20,28},{24,16},{28,20},{1,9},{5... | collective-permute-start | bytes 2359304 | tf_op jit(solution)/shard_map/ppermute | solution.py:276
  48.2 16.2 %collective-permute-done.4.m2_ref = f32[6,1,2048]{2,1,0:T(1,128)S(1)} collective-permute-done((f32[6,1,2048]{2,1,0:T(1,128)S(1)}, f32[6,1,2048]{2,1,0:T(1,128)S(1)}, u32[]{:S(2)}, u32[]{:S(2)}) %collective-permute-start.4) | collective-permute-done | bytes 49184 | tf_op jit(solution)/shard_map/ppermute | solution.py:276
  64.4 1.6 collective-permute-start.23
  67.1 2.7 %collective-permute-done.9.most1_ref = f32[2,1,2048]{2,1,0:T(1,128)S(1)} collective-permute-done((f32[2,1,2048]{2,1,0:T(1,128)S(1)}, f32[2,1,2048]{2,1,0:T(1,128)S(1)}, u32[]{:S(2)}, u32[]{:S(2)}) %collective-permute-start.9) | collective-permute-done | bytes 16416 | tf_op jit(solution)/shard_map/ppermute | solution.py:278
  70.8 3.2 %collective-permute-done.8.scale1_ref = bf16[16,2048]{1,0:T(8,128)(2,1)S(1)} collective-permute-done((bf16[16,2048]{1,0:T(8,128)(2,1)S(1)}, bf16[16,2048]{1,0:T(8,128)(2,1)S(1)}, u32[]{:S(2)}, u32[]{:S(2)}) %collective-permute-start.8) | collective-permute-done | bytes 65568 | tf_op jit(solution)/shard_map/ppermute | solution.py:278
  74.1 4.6 %collective-permute-start.20 = (bf16[192,2048]{1,0:T(8,128)(2,1)}, bf16[192,2048]{1,0:T(8,128)(2,1)S(1)}, u32[]{:S(2)}, u32[]{:S(2)}) collective-permute-start(bf16[192,2048]{1,0:T(8,128)(2,1)} %get-tuple-element.132.refs_1_), channel_id=1, source_target_pairs={{0,8},{4,12},{8,0},{12,4},{16,24},{20,28},{24,16},{28,20},{1,9},{5... | collective-permute-start | bytes 2359304 | tf_op jit(solution)/shard_map/ppermute | solution.py:276
  82.9 1.6 collective-permute-start.15
  86.8 2.2 decode.33
  91.4 2.2 decode.30
  93.6 3.7 %collective-permute-done.20.refs_0_ = bf16[192,2048]{1,0:T(8,128)(2,1)S(1)} collective-permute-done((bf16[192,2048]{1,0:T(8,128)(2,1)}, bf16[192,2048]{1,0:T(8,128)(2,1)S(1)}, u32[]{:S(2)}, u32[]{:S(2)}) %collective-permute-start.20) | collective-permute-done | bytes 786464 | tf_op jit(solution)/shard_map/ppermute | solution.py:276
  97.3 2.1 collective-permute-done.19.refs_0_
  101.5 14.7 %collective-permute-done.13.refs_0_ = bf16[192,2048]{1,0:T(8,128)(2,1)} collective-permute-done((bf16[192,2048]{1,0:T(8,128)(2,1)}, bf16[192,2048]{1,0:T(8,128)(2,1)}, u32[]{:S(2)}, u32[]{:S(2)}) %collective-permute-start.13) | collective-permute-done | bytes 786464 | tf_op jit(solution)/shard_map/ppermute | solution.py:278
  116.2 1.5 collective-permute-start.26
  117.8 1.8 decode.31
  119.5 1.8 decode.32
  121.3 1.8 decode.34
  123.1 2.9 %decode.35 = (bf16[3072,2048]{1,0:T(8,128)(2,1)}, f32[8,128]{1,0:T(8,128)}) custom-call(s32[1]{0:T(128)} %bitcast.me_ref, f32[24,1,2048]{2,1,0:T(1,128)S(1)} %get-tuple-element.115.r_ref, bf16[192,2048]{1,0:T(8,128)(2,1)} %collective-permute-done.6.refs_0_, bf16[3072,2048]{1,0:T(8,128)(2,1)} %get-tuple-element.133.refs_1_), custom_call_target="tpu_custom_call", output_to_operand_aliasing={{0}: (3, {})} | custom-call | tf_op jit(solution)/shard_map/decode/pallas_call | solution.py:211
  126.0 1.8 decode.38
  127.8 2.9 %decode.39 = (bf16[3072,2048]{1,0:T(8,128)(2,1)}, f32[8,128]{1,0:T(8,128)}) custom-call(s32[1]{0:T(128)} %bitcast.me_ref, f32[24,1,2048]{2,1,0:T(1,128)S(1)} %get-tuple-element.115.r_ref, bf16[192,2048]{1,0:T(8,128)(2,1)} %collective-permute-done.10.refs_0_, bf16[3072,2048]{1,0:T(8,128)(2,1)} %get-tuple-element.139.refs_1_), custom_call_target="tpu_custom_call", output_to_operand_aliasing={{0}: (3, {})} | custom-call | tf_op jit(solution)/shard_map/decode/pallas_call | solution.py:211
  136.0 1.3 collective-permute-start.27
  139.6 2.9 %decode.36 = (bf16[3072,2048]{1,0:T(8,128)(2,1)}, f32[8,128]{1,0:T(8,128)}) custom-call(s32[1]{0:T(128)} %bitcast.me_ref, f32[24,1,2048]{2,1,0:T(1,128)S(1)} %get-tuple-element.115.r_ref, bf16[192,2048]{1,0:T(8,128)(2,1)} %collective-permute-done.19.refs_0_, bf16[3072,2048]{1,0:T(8,128)(2,1)} %get-tuple-element.134.refs_1_), custom_call_target="tpu_custom_call", output_to_operand_aliasing={{0}: (3, {})} | custom-call | tf_op jit(solution)/shard_map/decode/pallas_call | solution.py:211
  142.5 1.8 decode.37
  144.3 2.9 %decode.40 = (bf16[3072,2048]{1,0:T(8,128)(2,1)}, f32[8,128]{1,0:T(8,128)}) custom-call(s32[1]{0:T(128)} %bitcast.me_ref, f32[24,1,2048]{2,1,0:T(1,128)S(1)} %get-tuple-element.115.r_ref, bf16[192,2048]{1,0:T(8,128)(2,1)} %collective-permute-done.13.refs_0_, bf16[3072,2048]{1,0:T(8,128)(2,1)} %get-tuple-element.140.refs_1_), custom_call_target="tpu_custom_call", output_to_operand_aliasing={{0}: (3, {})} | custom-call | tf_op jit(solution)/shard_map/decode/pallas_call | solution.py:211
  147.2 1.8 decode.41
  149.0 2.9 %decode.44 = (bf16[3072,2048]{1,0:T(8,128)(2,1)}, f32[8,128]{1,0:T(8,128)}) custom-call(s32[1]{0:T(128)} %bitcast.me_ref, f32[24,1,2048]{2,1,0:T(1,128)S(1)} %get-tuple-element.115.r_ref, bf16[192,2048]{1,0:T(8,128)(2,1)} %collective-permute-done.25.refs_0_, bf16[3072,2048]{1,0:T(8,128)(2,1)} %get-tuple-element.158.refs_1_), custom_call_target="tpu_custom_call", output_to_operand_aliasing={{0}: (3, {})} | custom-call | tf_op jit(solution)/shard_map/decode/pallas_call | solution.py:211
  151.9 1.8 decode.45
  155.8 1.8 decode.42
  157.6 1.8 decode.43
  160.2 11.1 %collective-permute-done.27.refs_0_ = bf16[192,2048]{1,0:T(8,128)(2,1)S(1)} collective-permute-done((bf16[192,2048]{1,0:T(8,128)(2,1)S(1)}, bf16[192,2048]{1,0:T(8,128)(2,1)S(1)}, u32[]{:S(2)}, u32[]{:S(2)}) %collective-permute-start.27) | collective-permute-done | bytes 786464 | tf_op jit(solution)/shard_map/ppermute | solution.py:278
  173.5 1.8 decode.46
  175.3 11.9 %collective-permute-done.22 = bf16[192,2048]{1,0:T(8,128)(2,1)S(1)} collective-permute-done((bf16[192,2048]{1,0:T(8,128)(2,1)}, bf16[192,2048]{1,0:T(8,128)(2,1)S(1)}, u32[]{:S(2)}, u32[]{:S(2)}) %collective-permute-start.22) | collective-permute-done | bytes 786464 | tf_op jit(solution)/shard_map/ppermute | solution.py:276
  190.9 1.8 decode.47
  192.6 1.8 decode.50
  194.4 1.8 decode.51
  196.2 8.8 %collective-permute-done.32.refs_0_ = bf16[192,2048]{1,0:T(8,128)(2,1)S(1)} collective-permute-done((bf16[192,2048]{1,0:T(8,128)(2,1)S(1)}, bf16[192,2048]{1,0:T(8,128)(2,1)S(1)}, u32[]{:S(2)}, u32[]{:S(2)}) %collective-permute-start.32) | collective-permute-done | bytes 786464 | tf_op jit(solution)/shard_map/ppermute | solution.py:278
  205.0 1.5 collective-permute-start.37
  206.5 1.8 decode.48
  208.4 1.8 decode.49
  211.0 9.9 %collective-permute-done.28 = bf16[192,2048]{1,0:T(8,128)(2,1)S(1)} collective-permute-done((bf16[192,2048]{1,0:T(8,128)(2,1)S(1)}, bf16[192,2048]{1,0:T(8,128)(2,1)S(1)}, u32[]{:S(2)}, u32[]{:S(2)}) %collective-permute-start.28) | collective-permute-done | bytes 786464 | tf_op jit(solution)/shard_map/ppermute | solution.py:276
  221.9 1.8 decode.52
  223.7 1.8 decode.53
  226.3 4.4 %collective-permute-start.35 = (bf16[192,2048]{1,0:T(8,128)(2,1)S(1)}, bf16[192,2048]{1,0:T(8,128)(2,1)S(1)}, u32[]{:S(2)}, u32[]{:S(2)}) collective-permute-start(bf16[192,2048]{1,0:T(8,128)(2,1)S(1)} %get-tuple-element.177.refs_0_), channel_id=1, source_target_pairs={{0,8},{4,12},{8,0},{12,4},{16,24},{20,28},{24,16},{28,20},{1,9},{5... | collective-permute-start | bytes 2359304 | tf_op jit(solution)/shard_map/ppermute | solution.py:276
  230.7 7.0 %collective-permute-done.37 = bf16[192,2048]{1,0:T(8,128)(2,1)S(1)} collective-permute-done((bf16[192,2048]{1,0:T(8,128)(2,1)S(1)}, bf16[192,2048]{1,0:T(8,128)(2,1)S(1)}, u32[]{:S(2)}, u32[]{:S(2)}) %collective-permute-start.37) | collective-permute-done | bytes 786464 | tf_op jit(solution)/shard_map/ppermute | solution.py:276
  238.7 4.6 %collective-permute-start.40 = (bf16[144,2048]{1,0:T(8,128)(2,1)S(1)}, bf16[144,2048]{1,0:T(8,128)(2,1)S(1)}, u32[]{:S(2)}, u32[]{:S(2)}) collective-permute-start(bf16[144,2048]{1,0:T(8,128)(2,1)S(1)} %slice.35), channel_id=1, source_target_pairs={{0,8},{4,12},{8,0},{12,4},{16,24},{20,28},{24,16},{28,20},{1,9},{5... | collective-permute-start | bytes 1769480 | tf_op jit(solution)/shard_map/ppermute | solution.py:276
  243.9 7.8 %collective-permute-done.35.refs_0_ = bf16[192,2048]{1,0:T(8,128)(2,1)S(1)} collective-permute-done((bf16[192,2048]{1,0:T(8,128)(2,1)S(1)}, bf16[192,2048]{1,0:T(8,128)(2,1)S(1)}, u32[]{:S(2)}, u32[]{:S(2)}) %collective-permute-start.35) | collective-permute-done | bytes 786464 | tf_op jit(solution)/shard_map/ppermute | solution.py:276
  251.7 1.3 collective-permute-start.39
  253.1 1.8 decode.56
  254.9 1.8 decode.57
  256.6 1.8 decode.54
  258.4 1.8 decode.55
  260.2 2.0 decode.58
  262.2 1.5 decode.59
  (91 shorter events, 37.6 us)
Async XLA Ops:
  2.9 20.8 %collective-permute-start.2 = (bf16[192,2048]{1,0:T(8,128)(2,1)S(1)}, bf16[192,2048]{1,0:T(8,128)(2,1)S(1)}, u32[]{:S(2)}, u32[]{:S(2)}) collective-permute-start(bf16[192,2048]{1,0:T(8,128)(2,1)S(1)} %get-tuple-element.106.first_ref), channel_id=1, source_target_pairs={{0,4},{1,9},{2,6},{3,11},{4,0},{5,13},{6,2},{7,15},{8,12},{9,1},{1... | collective-permute-start | bytes 2359304 | tf_op jit(solution)/shard_map/ppermute | solution.py:330
  6.0 20.3 %collective-permute-start.1 = (bf16[192,2048]{1,0:T(8,128)(2,1)S(1)}, bf16[192,2048]{1,0:T(8,128)(2,1)S(1)}, u32[]{:S(2)}, u32[]{:S(2)}) collective-permute-start(bf16[192,2048]{1,0:T(8,128)(2,1)S(1)} %get-tuple-element.106.first_ref), channel_id=1, source_target_pairs={{0,8},{1,5},{2,10},{3,7},{4,12},{5,1},{6,14},{7,3},{8,0},{9,13},{1... | collective-permute-start | bytes 2359304 | tf_op jit(solution)/shard_map/ppermute | solution.py:330
  7.5 33.4 %collective-permute-start.3 = (bf16[192,2048]{1,0:T(8,128)(2,1)S(1)}, bf16[192,2048]{1,0:T(8,128)(2,1)}, u32[]{:S(2)}, u32[]{:S(2)}) collective-permute-start(bf16[192,2048]{1,0:T(8,128)(2,1)S(1)} %get-tuple-element.106.first_ref), channel_id=1, source_target_pairs={{8,16},{12,20},{16,8},{20,12},{9,17},{13,21},{17,9},{21,13},{10,18... | collective-permute-start | bytes 2359304 | tf_op jit(solution)/shard_map/ppermute | solution.py:276
  9.1 0.7 copy-start.6
  16.4 27.0 %collective-permute-start.7 = (bf16[192,2048]{1,0:T(8,128)(2,1)}, bf16[192,2048]{1,0:T(8,128)(2,1)}, u32[]{:S(2)}, u32[]{:S(2)}) collective-permute-start(bf16[192,2048]{1,0:T(8,128)(2,1)} %get-tuple-element.111.refs_0_), channel_id=1, source_target_pairs={{8,16},{12,20},{16,8},{20,12},{9,17},{13,21},{17,9},{21,13},{10,18... | collective-permute-start | bytes 2359304 | tf_op jit(solution)/shard_map/ppermute | solution.py:276
  18.0 29.8 %collective-permute-start.6 = (bf16[192,2048]{1,0:T(8,128)(2,1)}, bf16[192,2048]{1,0:T(8,128)(2,1)}, u32[]{:S(2)}, u32[]{:S(2)}) collective-permute-start(bf16[192,2048]{1,0:T(8,128)(2,1)} %get-tuple-element.111.refs_0_), channel_id=1, source_target_pairs={{0,8},{4,12},{8,0},{12,4},{16,24},{20,28},{24,16},{28,20},{1,9},{5... | collective-permute-start | bytes 2359304 | tf_op jit(solution)/shard_map/ppermute | solution.py:276
  23.7 2.5 copy-start.9
  23.7 24.5 %collective-permute-start.5 = (bf16[192,2048]{1,0:T(8,128)(2,1)}, bf16[192,2048]{1,0:T(8,128)(2,1)S(1)}, u32[]{:S(2)}, u32[]{:S(2)}) collective-permute-start(bf16[192,2048]{1,0:T(8,128)(2,1)} %get-tuple-element.111.refs_0_), channel_id=1, source_target_pairs={{0,4},{4,0},{8,12},{12,8},{16,20},{20,16},{24,28},{28,24},{1,5},{5... | collective-permute-start | bytes 2359304 | tf_op jit(solution)/shard_map/ppermute | solution.py:278
  26.2 0.9 copy-start.10
  27.2 13.8 %collective-permute-start = (f32[3,1,2048]{2,1,0:T(1,128)S(1)}, f32[3,1,2048]{2,1,0:T(1,128)S(1)}, u32[]{:S(2)}, u32[]{:S(2)}) collective-permute-start(f32[3,1,2048]{2,1,0:T(1,128)S(1)} %get-tuple-element.108.m0_ref), channel_id=1, source_target_pairs={{0,8},{4,12},{8,0},{12,4},{16,24},{20,28},{24,16},{28,20},{1,9},{5... | collective-permute-start | bytes 73736 | tf_op jit(solution)/shard_map/ppermute | solution.py:276
  41.0 37.7 %collective-permute-start.12 = (bf16[192,2048]{1,0:T(8,128)(2,1)}, bf16[192,2048]{1,0:T(8,128)(2,1)S(1)}, u32[]{:S(2)}, u32[]{:S(2)}) collective-permute-start(bf16[192,2048]{1,0:T(8,128)(2,1)} %get-tuple-element.117.refs_1_), channel_id=1, source_target_pairs={{8,16},{12,20},{16,8},{20,12},{9,17},{13,21},{17,9},{21,13},{10,18... | collective-permute-start | bytes 2359304 | tf_op jit(solution)/shard_map/ppermute | solution.py:276
  41.7 37.7 %collective-permute-start.11 = (bf16[192,2048]{1,0:T(8,128)(2,1)}, bf16[192,2048]{1,0:T(8,128)(2,1)S(1)}, u32[]{:S(2)}, u32[]{:S(2)}) collective-permute-start(bf16[192,2048]{1,0:T(8,128)(2,1)} %get-tuple-element.117.refs_1_), channel_id=1, source_target_pairs={{0,4},{4,0},{8,12},{12,8},{16,20},{20,16},{24,28},{28,24},{1,5},{5... | collective-permute-start | bytes 2359304 | tf_op jit(solution)/shard_map/ppermute | solution.py:278
  43.4 36.9 %collective-permute-start.10 = (bf16[192,2048]{1,0:T(8,128)(2,1)}, bf16[192,2048]{1,0:T(8,128)(2,1)}, u32[]{:S(2)}, u32[]{:S(2)}) collective-permute-start(bf16[192,2048]{1,0:T(8,128)(2,1)} %get-tuple-element.117.refs_1_), channel_id=1, source_target_pairs={{0,8},{4,12},{8,0},{12,4},{16,24},{20,28},{24,16},{28,20},{1,9},{5... | collective-permute-start | bytes 2359304 | tf_op jit(solution)/shard_map/ppermute | solution.py:276
  47.8 16.6 %collective-permute-start.4 = (f32[6,1,2048]{2,1,0:T(1,128)S(1)}, f32[6,1,2048]{2,1,0:T(1,128)S(1)}, u32[]{:S(2)}, u32[]{:S(2)}) collective-permute-start(f32[6,1,2048]{2,1,0:T(1,128)S(1)} %pad_maximum_fusion), channel_id=1, source_target_pairs={{0,16},{4,20},{16,0},{20,4},{8,24},{12,28},{24,8},{28,12},{1,17},{... | collective-permute-start | bytes 147464 | tf_op jit(solution)/shard_map/ppermute | solution.py:276
  64.4 18.5 %collective-permute-start.23 = (bf16[192,2048]{1,0:T(8,128)(2,1)}, bf16[192,2048]{1,0:T(8,128)(2,1)}, u32[]{:S(2)}, u32[]{:S(2)}) collective-permute-start(bf16[192,2048]{1,0:T(8,128)(2,1)} %get-tuple-element.132.refs_1_), channel_id=1, source_target_pairs={{8,16},{12,20},{16,8},{20,12},{9,17},{13,21},{17,9},{21,13},{10,18... | collective-permute-start | bytes 2359304 | tf_op jit(solution)/shard_map/ppermute | solution.py:276
  66.0 3.8 %collective-permute-start.9 = (f32[2,1,2048]{2,1,0:T(1,128)S(1)}, f32[2,1,2048]{2,1,0:T(1,128)S(1)}, u32[]{:S(2)}, u32[]{:S(2)}) collective-permute-start(f32[2,1,2048]{2,1,0:T(1,128)S(1)} %get-tuple-element.114.most0_ref), channel_id=1, source_target_pairs={{0,4},{4,0},{8,12},{12,8},{16,20},{20,16},{24,28},{28,24},{1,5},{5... | collective-permute-start | bytes 49160 | tf_op jit(solution)/shard_map/ppermute | solution.py:278
  69.8 4.3 %collective-permute-start.8 = (bf16[16,2048]{1,0:T(8,128)(2,1)S(1)}, bf16[16,2048]{1,0:T(8,128)(2,1)S(1)}, u32[]{:S(2)}, u32[]{:S(2)}) collective-permute-start(bf16[16,2048]{1,0:T(8,128)(2,1)S(1)} %get-tuple-element.112.scale0_ref), channel_id=1, source_target_pairs={{0,4},{4,0},{8,12},{12,8},{16,20},{20,16},{24,28},{28,24},{1,5},{5... | collective-permute-start | bytes 196616 | tf_op jit(solution)/shard_map/ppermute | solution.py:278
  74.1 23.2 %collective-permute-start.20 = (bf16[192,2048]{1,0:T(8,128)(2,1)}, bf16[192,2048]{1,0:T(8,128)(2,1)S(1)}, u32[]{:S(2)}, u32[]{:S(2)}) collective-permute-start(bf16[192,2048]{1,0:T(8,128)(2,1)} %get-tuple-element.132.refs_1_), channel_id=1, source_target_pairs={{0,8},{4,12},{8,0},{12,4},{16,24},{20,28},{24,16},{28,20},{1,9},{5... | collective-permute-start | bytes 2359304 | tf_op jit(solution)/shard_map/ppermute | solution.py:276
  78.7 4.2 %copy-start.7 = (bf16[192,2048]{1,0:T(8,128)(2,1)}, bf16[192,2048]{1,0:T(8,128)(2,1)S(1)}, u32[]{:S(2)}) copy-start(bf16[192,2048]{1,0:T(8,128)(2,1)S(1)} %collective-permute-done.12) | copy-start | bytes 2359300
  78.7 20.7 %collective-permute-start.19 = (bf16[192,2048]{1,0:T(8,128)(2,1)}, bf16[192,2048]{1,0:T(8,128)(2,1)}, u32[]{:S(2)}, u32[]{:S(2)}) collective-permute-start(bf16[192,2048]{1,0:T(8,128)(2,1)} %get-tuple-element.132.refs_1_), channel_id=1, source_target_pairs={{0,4},{4,0},{8,12},{12,8},{16,20},{20,16},{24,28},{28,24},{1,5},{5... | collective-permute-start | bytes 2359304 | tf_op jit(solution)/shard_map/ppermute | solution.py:278
  79.4 0.9 copy-start.4
  80.3 35.9 %collective-permute-start.13 = (bf16[192,2048]{1,0:T(8,128)(2,1)}, bf16[192,2048]{1,0:T(8,128)(2,1)}, u32[]{:S(2)}, u32[]{:S(2)}) collective-permute-start(bf16[192,2048]{1,0:T(8,128)(2,1)} %collective-permute-done.10.refs_0_), channel_id=1, source_target_pairs={{0,4},{4,0},{8,12},{12,8},{16,20},{20,16},{24,28},{28,24},{1,5},{5... | collective-permute-start | bytes 2359304 | tf_op jit(solution)/shard_map/ppermute | solution.py:278
  81.6 49.1 %collective-permute-start.14 = (bf16[192,2048]{1,0:T(8,128)(2,1)}, bf16[192,2048]{1,0:T(8,128)(2,1)}, u32[]{:S(2)}, u32[]{:S(2)}) collective-permute-start(bf16[192,2048]{1,0:T(8,128)(2,1)} %collective-permute-done.3), channel_id=1, source_target_pairs={{8,0},{12,4},{16,24},{20,28},{9,1},{13,5},{17,25},{21,29},{10,2},{... | collective-permute-start | bytes 2359304 | tf_op jit(solution)/shard_map/ppermute | solution.py:276
  82.9 47.8 %collective-permute-start.15 = (bf16[192,2048]{1,0:T(8,128)(2,1)S(1)}, bf16[192,2048]{1,0:T(8,128)(2,1)}, u32[]{:S(2)}, u32[]{:S(2)}) collective-permute-start(bf16[192,2048]{1,0:T(8,128)(2,1)S(1)} %get-tuple-element.120.refs_0_), channel_id=1, source_target_pairs={{8,16},{12,20},{16,8},{20,12},{9,17},{13,21},{17,9},{21,13},{10,18... | collective-permute-start | bytes 2359304 | tf_op jit(solution)/shard_map/ppermute | solution.py:276
  84.6 1.1 copy-start
  85.7 1.1 copy-start.3
  89.1 1.1 copy-start.1
  90.2 1.1 copy-start.2
  99.4 34.6 %collective-permute-start.24 = (bf16[192,2048]{1,0:T(8,128)(2,1)}, bf16[192,2048]{1,0:T(8,128)(2,1)}, u32[]{:S(2)}, u32[]{:S(2)}) collective-permute-start(bf16[192,2048]{1,0:T(8,128)(2,1)} %collective-permute-done.7), channel_id=1, source_target_pairs={{8,0},{12,4},{16,24},{20,28},{9,1},{13,5},{17,25},{21,29},{10,2},{... | collective-permute-start | bytes 2359304 | tf_op jit(solution)/shard_map/ppermute | solution.py:276
  100.7 34.1 %collective-permute-start.25 = (bf16[192,2048]{1,0:T(8,128)(2,1)S(1)}, bf16[192,2048]{1,0:T(8,128)(2,1)}, u32[]{:S(2)}, u32[]{:S(2)}) collective-permute-start(bf16[192,2048]{1,0:T(8,128)(2,1)S(1)} %collective-permute-done.20.refs_0_), channel_id=1, source_target_pairs={{0,4},{4,0},{8,12},{12,8},{16,20},{20,16},{24,28},{28,24},{1,5},{5... | collective-permute-start | bytes 2359304 | tf_op jit(solution)/shard_map/ppermute | solution.py:278
  116.2 18.5 %collective-permute-start.26 = (bf16[192,2048]{1,0:T(8,128)(2,1)}, bf16[192,2048]{1,0:T(8,128)(2,1)}, u32[]{:S(2)}, u32[]{:S(2)}) collective-permute-start(bf16[192,2048]{1,0:T(8,128)(2,1)} %collective-permute-done.6.refs_0_), channel_id=1, source_target_pairs={{8,16},{12,20},{16,8},{20,12},{9,17},{13,21},{17,9},{21,13},{10,18... | collective-permute-start | bytes 2359304 | tf_op jit(solution)/shard_map/ppermute | solution.py:276
  121.3 4.7 %copy-start.5 = (bf16[192,2048]{1,0:T(8,128)(2,1)S(1)}, bf16[192,2048]{1,0:T(8,128)(2,1)}, u32[]{:S(2)}) copy-start(bf16[192,2048]{1,0:T(8,128)(2,1)} %copy-done.4) | copy-start | bytes 2359300
  126.0 6.7 %copy-start.8 = (bf16[192,2048]{1,0:T(8,128)(2,1)S(1)}, bf16[192,2048]{1,0:T(8,128)(2,1)}, u32[]{:S(2)}) copy-start(bf16[192,2048]{1,0:T(8,128)(2,1)} %copy-done.7) | copy-start | bytes 2359300
  130.7 7.9 %collective-permute-start.16 = (bf16[192,2048]{1,0:T(8,128)(2,1)}, bf16[192,2048]{1,0:T(8,128)(2,1)S(1)}, u32[]{:S(2)}, u32[]{:S(2)}) collective-permute-start(bf16[192,2048]{1,0:T(8,128)(2,1)} %collective-permute-done.10.refs_0_), channel_id=1, source_target_pairs={{8,16},{12,20},{16,8},{20,12},{9,17},{13,21},{17,9},{21,13},{10,18... | collective-permute-start | bytes 2359304 | tf_op jit(solution)/shard_map/ppermute | solution.py:276
  132.7 21.0 %collective-permute-start.17 = (bf16[192,2048]{1,0:T(8,128)(2,1)S(1)}, bf16[192,2048]{1,0:T(8,128)(2,1)S(1)}, u32[]{:S(2)}, u32[]{:S(2)}) collective-permute-start(bf16[192,2048]{1,0:T(8,128)(2,1)S(1)} %copy-done.8), channel_id=1, source_target_pairs={{8,0},{12,4},{16,24},{20,28},{9,1},{13,5},{17,25},{21,29},{10,2},{... | collective-permute-start | bytes 2359304 | tf_op jit(solution)/shard_map/ppermute | solution.py:276
  134.0 20.5 %collective-permute-start.18 = (bf16[192,2048]{1,0:T(8,128)(2,1)S(1)}, bf16[192,2048]{1,0:T(8,128)(2,1)S(1)}, u32[]{:S(2)}, u32[]{:S(2)}) collective-permute-start(bf16[192,2048]{1,0:T(8,128)(2,1)S(1)} %broadcast_select_fusion.6.refs_0_), channel_id=1, source_target_pairs={{0,4},{4,0},{8,12},{12,8},{16,20},{20,16},{24,28},{28,24},{1,5},{5... | collective-permute-start | bytes 2359304 | tf_op jit(solution)/shard_map/ppermute | solution.py:278
  136.0 35.3 %collective-permute-start.27 = (bf16[192,2048]{1,0:T(8,128)(2,1)S(1)}, bf16[192,2048]{1,0:T(8,128)(2,1)S(1)}, u32[]{:S(2)}, u32[]{:S(2)}) collective-permute-start(bf16[192,2048]{1,0:T(8,128)(2,1)S(1)} %broadcast_select_fusion.5.refs_0_), channel_id=1, source_target_pairs={{0,4},{4,0},{8,12},{12,8},{16,20},{20,16},{24,28},{28,24},{1,5},{5... | collective-permute-start | bytes 2359304 | tf_op jit(solution)/shard_map/ppermute | solution.py:278
  137.3 34.0 %collective-permute-start.30 = (bf16[192,2048]{1,0:T(8,128)(2,1)}, bf16[192,2048]{1,0:T(8,128)(2,1)S(1)}, u32[]{:S(2)}, u32[]{:S(2)}) collective-permute-start(bf16[192,2048]{1,0:T(8,128)(2,1)} %collective-permute-done.23), channel_id=1, source_target_pairs={{8,0},{12,4},{16,24},{20,28},{9,1},{13,5},{17,25},{21,29},{10,2},{... | collective-permute-start | bytes 2359304 | tf_op jit(solution)/shard_map/ppermute | solution.py:276
  138.6 32.7 %collective-permute-start.31 = (bf16[192,2048]{1,0:T(8,128)(2,1)S(1)}, bf16[192,2048]{1,0:T(8,128)(2,1)S(1)}, u32[]{:S(2)}, u32[]{:S(2)}) collective-permute-start(bf16[192,2048]{1,0:T(8,128)(2,1)S(1)} %collective-permute-done.20.refs_0_), channel_id=1, source_target_pairs={{8,16},{12,20},{16,8},{20,12},{9,17},{13,21},{17,9},{21,13},{10,18... | collective-permute-start | bytes 2359304 | tf_op jit(solution)/shard_map/ppermute | solution.py:276
  154.4 32.7 %collective-permute-start.22 = (bf16[192,2048]{1,0:T(8,128)(2,1)}, bf16[192,2048]{1,0:T(8,128)(2,1)S(1)}, u32[]{:S(2)}, u32[]{:S(2)}) collective-permute-start(bf16[192,2048]{1,0:T(8,128)(2,1)} %collective-permute-done.15), channel_id=1, source_target_pairs={{8,0},{12,4},{16,24},{20,28},{9,1},{13,5},{17,25},{21,29},{10,2},{... | collective-permute-start | bytes 2359304 | tf_op jit(solution)/shard_map/ppermute | solution.py:276
  159.4 28.8 %collective-permute-start.21 = (bf16[192,2048]{1,0:T(8,128)(2,1)S(1)}, bf16[192,2048]{1,0:T(8,128)(2,1)S(1)}, u32[]{:S(2)}, u32[]{:S(2)}) collective-permute-start(bf16[192,2048]{1,0:T(8,128)(2,1)S(1)} %broadcast_select_fusion.7.refs_0_), channel_id=1, source_target_pairs={{0,4},{4,0},{8,12},{12,8},{16,20},{20,16},{24,28},{28,24},{1,5},{5... | collective-permute-start | bytes 2359304 | tf_op jit(solution)/shard_map/ppermute | solution.py:278
  171.4 33.6 %collective-permute-start.32 = (bf16[192,2048]{1,0:T(8,128)(2,1)S(1)}, bf16[192,2048]{1,0:T(8,128)(2,1)S(1)}, u32[]{:S(2)}, u32[]{:S(2)}) collective-permute-start(bf16[192,2048]{1,0:T(8,128)(2,1)S(1)} %broadcast_select_fusion.2.refs_0_), channel_id=1, source_target_pairs={{0,4},{4,0},{8,12},{12,8},{16,20},{20,16},{24,28},{28,24},{1,5},{5... | collective-permute-start | bytes 2359304 | tf_op jit(solution)/shard_map/ppermute | solution.py:278
  172.2 32.8 %collective-permute-start.33 = (bf16[192,2048]{1,0:T(8,128)(2,1)}, bf16[192,2048]{1,0:T(8,128)(2,1)S(1)}, u32[]{:S(2)}, u32[]{:S(2)}) collective-permute-start(bf16[192,2048]{1,0:T(8,128)(2,1)} %collective-permute-done.26), channel_id=1, source_target_pairs={{8,0},{12,4},{16,24},{20,28},{9,1},{13,5},{17,25},{21,29},{10,2},{... | collective-permute-start | bytes 2359304 | tf_op jit(solution)/shard_map/ppermute | solution.py:276
  188.2 32.7 %collective-permute-start.28 = (bf16[192,2048]{1,0:T(8,128)(2,1)S(1)}, bf16[192,2048]{1,0:T(8,128)(2,1)S(1)}, u32[]{:S(2)}, u32[]{:S(2)}) collective-permute-start(bf16[192,2048]{1,0:T(8,128)(2,1)S(1)} %collective-permute-done.16), channel_id=1, source_target_pairs={{8,0},{12,4},{16,24},{20,28},{9,1},{13,5},{17,25},{21,29},{10,2},{... | collective-permute-start | bytes 2359304 | tf_op jit(solution)/shard_map/ppermute | solution.py:276
  189.4 32.4 %collective-permute-start.29 = (bf16[192,2048]{1,0:T(8,128)(2,1)S(1)}, bf16[192,2048]{1,0:T(8,128)(2,1)S(1)}, u32[]{:S(2)}, u32[]{:S(2)}) collective-permute-start(bf16[192,2048]{1,0:T(8,128)(2,1)S(1)} %broadcast_select_fusion.3.refs_0_), channel_id=1, source_target_pairs={{0,4},{4,0},{8,12},{12,8},{16,20},{20,16},{24,28},{28,24},{1,5},{5... | collective-permute-start | bytes 2359304 | tf_op jit(solution)/shard_map/ppermute | solution.py:278
  205.0 32.7 %collective-permute-start.37 = (bf16[192,2048]{1,0:T(8,128)(2,1)S(1)}, bf16[192,2048]{1,0:T(8,128)(2,1)S(1)}, u32[]{:S(2)}, u32[]{:S(2)}) collective-permute-start(bf16[192,2048]{1,0:T(8,128)(2,1)S(1)} %collective-permute-done.31), channel_id=1, source_target_pairs={{8,0},{12,4},{16,24},{20,28},{9,1},{13,5},{17,25},{21,29},{10,2},{... | collective-permute-start | bytes 2359304 | tf_op jit(solution)/shard_map/ppermute | solution.py:276
  210.2 28.6 %collective-permute-start.36 = (bf16[192,2048]{1,0:T(8,128)(2,1)S(1)}, bf16[192,2048]{1,0:T(8,128)(2,1)S(1)}, u32[]{:S(2)}, u32[]{:S(2)}) collective-permute-start(bf16[192,2048]{1,0:T(8,128)(2,1)S(1)} %broadcast_select_fusion.1.refs_0_), channel_id=1, source_target_pairs={{0,4},{4,0},{8,12},{12,8},{16,20},{20,16},{24,28},{28,24},{1,5},{5... | collective-permute-start | bytes 2359304 | tf_op jit(solution)/shard_map/ppermute | solution.py:278
  225.5 32.9 %collective-permute-start.34 = (bf16[192,2048]{1,0:T(8,128)(2,1)S(1)}, bf16[192,2048]{1,0:T(8,128)(2,1)S(1)}, u32[]{:S(2)}, u32[]{:S(2)}) collective-permute-start(bf16[192,2048]{1,0:T(8,128)(2,1)S(1)} %broadcast_select_fusion.4.refs_0_), channel_id=1, source_target_pairs={{0,4},{4,0},{8,12},{12,8},{16,20},{20,16},{24,28},{28,24},{1,5},{5... | collective-permute-start | bytes 2359304 | tf_op jit(solution)/shard_map/ppermute | solution.py:278
  226.3 25.4 %collective-permute-start.35 = (bf16[192,2048]{1,0:T(8,128)(2,1)S(1)}, bf16[192,2048]{1,0:T(8,128)(2,1)S(1)}, u32[]{:S(2)}, u32[]{:S(2)}) collective-permute-start(bf16[192,2048]{1,0:T(8,128)(2,1)S(1)} %get-tuple-element.177.refs_0_), channel_id=1, source_target_pairs={{0,8},{4,12},{8,0},{12,4},{16,24},{20,28},{24,16},{28,20},{1,9},{5... | collective-permute-start | bytes 2359304 | tf_op jit(solution)/shard_map/ppermute | solution.py:276
  238.7 21.5 %collective-permute-start.40 = (bf16[144,2048]{1,0:T(8,128)(2,1)S(1)}, bf16[144,2048]{1,0:T(8,128)(2,1)S(1)}, u32[]{:S(2)}, u32[]{:S(2)}) collective-permute-start(bf16[144,2048]{1,0:T(8,128)(2,1)S(1)} %slice.35), channel_id=1, source_target_pairs={{0,8},{4,12},{8,0},{12,4},{16,24},{20,28},{24,16},{28,20},{1,9},{5... | collective-permute-start | bytes 1769480 | tf_op jit(solution)/shard_map/ppermute | solution.py:276
  243.3 16.9 %collective-permute-start.41 = (bf16[144,2048]{1,0:T(8,128)(2,1)S(1)}, bf16[144,2048]{1,0:T(8,128)(2,1)S(1)}, u32[]{:S(2)}, u32[]{:S(2)}) collective-permute-start(bf16[144,2048]{1,0:T(8,128)(2,1)S(1)} %slice_select_fusion), channel_id=1, source_target_pairs={{0,4},{4,0},{8,12},{12,8},{16,20},{20,16},{24,28},{28,24},{1,5},{5... | collective-permute-start | bytes 1769480 | tf_op jit(solution)/shard_map/ppermute | solution.py:278
  243.9 16.3 %collective-permute-start.38 = (bf16[48,2048]{1,0:T(8,128)(2,1)S(1)}, bf16[48,2048]{1,0:T(8,128)(2,1)S(1)}, u32[]{:S(2)}, u32[]{:S(2)}) collective-permute-start(bf16[48,2048]{1,0:T(8,128)(2,1)S(1)} %slice.32), channel_id=1, source_target_pairs={{0,8},{4,12},{8,0},{12,4},{16,24},{20,28},{24,16},{28,20},{1,9},{5... | collective-permute-start | bytes 589832 | tf_op jit(solution)/shard_map/ppermute | solution.py:276
  251.7 8.5 %collective-permute-start.39 = (bf16[48,2048]{1,0:T(8,128)(2,1)S(1)}, bf16[48,2048]{1,0:T(8,128)(2,1)S(1)}, u32[]{:S(2)}, u32[]{:S(2)}) collective-permute-start(bf16[48,2048]{1,0:T(8,128)(2,1)S(1)} %slice_select_fusion.1), channel_id=1, source_target_pairs={{0,4},{4,0},{8,12},{12,8},{16,20},{20,16},{24,28},{28,24},{1,5},{5... | collective-permute-start | bytes 589832 | tf_op jit(solution)/shard_map/ppermute | solution.py:278

commit v6 on v5

--- a/solution.py
+++ b/solution.py
@@ -49,7 +49,8 @@
     return jnp.where(x < 0, -y, y).astype(jnp.bfloat16)
 
 
-def encode_rest_body(gain_ref, wu0, au0, wg, ag, wu1, au1, first_ref, first_max_ref, own_ref, up0, gate, up1, m_ref):
+def encode_rest_body(gain_ref, wu0, au0, wg, ag, wu1, au1, *refs):
+    firsts, first_maxima, (own_ref, up0, gate, up1, m_ref) = refs[:2], refs[2:4], refs[4:]
     half_rows, width = wg.shape
     tall = tall_gain(gain_ref, width)
     top, bottom = tall[:half_rows], tall[half_rows:]
@@ -62,35 +63,43 @@
     m = largest(x)
     gate[...] = coded(x, m)
     m_ref[2] = m
-    m_ref[0] = first_max_ref[0]
-    own_ref[...] = first_ref[...]
-
-
-def encode_rest(w_gate, avg_gate, w_up, avg_up, gain, first, first_maxima, block):
+    for side in (0, 1):
+
+        @pl.when(pl.program_id(0) // (pl.num_programs(0) // 2) == side)
+        def _(side=side):
+            m_ref[0] = first_maxima[side][0]
+            own_ref[...] = firsts[side][...]
+
+
+def encode_rest(w_gate, avg_gate, w_up, avg_up, gain, firsts, first_maxima, block):
     half_rows, columns = w_gate.shape[0] // 2, w_gate.shape[1]
     half = lambda h: [pl.BlockSpec((half_rows, block), lambda j: (h, j))] * 2
     stacked = lambda n: pl.BlockSpec((n, 1, block), lambda j: (0, 0, j))
     whole = pl.BlockSpec((half_rows, block), lambda j: (0, j))
+    steps = columns // block
+    at = [lambda j: jnp.minimum(j, steps // 2 - 1), lambda j: jnp.maximum(j - steps // 2, 0)]
+    first_specs = [pl.BlockSpec((half_rows, block), lambda j, f=f: (0, f(j))) for f in at]
+    max_specs = [pl.BlockSpec((1, 1, block), lambda j, f=f: (0, 0, f(j))) for f in at]
     chunk = pltpu.HBM((half_rows, columns), jnp.bfloat16)
     return pl.pallas_call(
         encode_rest_body,
-        grid=(columns // block,),
-        in_specs=[pl.BlockSpec(gain.shape, lambda j: (0,)), *half(0), *half(1), *half(1), whole, stacked(1)],
+        grid=(steps,),
+        in_specs=[pl.BlockSpec(gain.shape, lambda j: (0,)), *half(0), *half(1), *half(1), *first_specs, *max_specs],
         out_specs=[whole] * 4 + [stacked(3)],
         out_shape=[chunk] * 4 + [jax.ShapeDtypeStruct((3, 1, columns), jnp.float32)],
         compiler_params=pltpu.CompilerParams(vmem_limit_bytes=12 * MIB),
         name="encode_rest",
-    )(gain, *map(stay_out, (w_up, avg_up, w_gate, avg_gate, w_up, avg_up)), near_by(first), near_by(first_maxima))
-
-
-def encode_first_body(g_ref, w_ref, a_ref, y_ref, m_ref, gain_ref, ws, avgs, sems, *, half):
-    half_rows, _ = y_ref.shape
+    )(gain, *map(stay_out, (w_up, avg_up, w_gate, avg_gate, w_up, avg_up)), *map(near_by, (*firsts, *first_maxima)))
+
+
+def encode_first_body(g_ref, w_ref, a_ref, y_ref, m_ref, gain_ref, ws, avgs, sems, *, half, side):
+    half_rows, columns = y_ref.shape
     steps, _, width = ws.shape
     copies = []
     gain_copy = pltpu.make_async_copy(g_ref, gain_ref, sems.at[2, 0])
     gain_copy.start()
     for j in range(steps):
-        source = (pl.ds(half * half_rows, half_rows), pl.ds(j * width, width))
+        source = (pl.ds(half * half_rows, half_rows), pl.ds(side * columns + j * width, width))
         pair = [
             pltpu.make_async_copy(ref.at[source], held.at[j], sems.at[i, j])
             for i, (ref, held) in enumerate(((w_ref, ws), (a_ref, avgs)))
@@ -110,13 +119,13 @@
         m_ref[0, :, part] = m
 
 
-def encode_first(w, avg, gain, half, width):
-    half_rows, columns = w.shape[0] // 2, w.shape[1]
+def encode_first(w, avg, gain, half, side, width):
+    half_rows, columns = w.shape[0] // 2, w.shape[1] // 2
     here = pl.BlockSpec(memory_space=pltpu.VMEM)
     there = pl.BlockSpec(memory_space=pl.ANY)
     held = pltpu.VMEM((columns // width, half_rows, width), jnp.float32)
     return pl.pallas_call(
-        functools.partial(encode_first_body, half=half),
+        functools.partial(encode_first_body, half=half, side=side),
         in_specs=[there, there, there],
         out_specs=[here, here],
         out_shape=[
@@ -281,8 +290,12 @@
     middle = lambda value: hop(value, [(1, 2), (2, 1)])
     skip = lambda value: hop(value, [(0, 2), (2, 0), (1, 3), (3, 1)])
 
-    first, first_maxima = encode_first(w_gate, avg_gate, norm_gain, 0, block // 4)
-    *own, maxima = encode_rest(w_gate, avg_gate, w_up, avg_up, norm_gain, first, first_maxima, block // 2)
+    firsts, first_maxima = [], []
+    for side in (0, 1):
+        first, m = encode_first(w_gate, avg_gate, norm_gain, 0, side, block // 4)
+        firsts.append(first)
+        first_maxima.append(m)
+    *own, maxima = encode_rest(w_gate, avg_gate, w_up, avg_up, norm_gain, firsts, first_maxima, block // 2)
 
     X, B, M, O, V, F = {}, {}, {}, {}, {}, {}
     tables = [maxima]
@@ -295,16 +308,16 @@
     def arrived(k):
         got = [X[k]]
         if k < 4:
-            got += [B[k], M[k]]
+            got += [B[k]]
             wait_for(X[k], across_of, k)
             wait_for(B[k], buddy_of, k)
-        elif k < 8:
-            got += [O[k], M[k]]
         elif k < 12:
             got += [O[k]]
         else:
             got += [F[0]]
             wait_for(F[0], diagonal_of, 0)
+        if 1 <= k <= 8:
+            got.append(M[k - 1])
         if 4 <= k < 6:
             wait_for(X[k], diagonal_of, k - 2)
         if 6 <= k < 10:
@@ -327,16 +340,19 @@
         odd = lax.axis_index("width") % 2 == 1
         cores = [(row, column) for row in range(8) for column in range(width)]
         flat = lambda row, column: row * width + column
-        swap = lambda turn: lax.ppermute(
-            first,
+        swap = lambda half, turn: lax.ppermute(
+            half,
             ("rows", "width"),
             [(flat(r, c), flat(r ^ (1 if (c + turn) % 2 == 0 else 2), c)) for r, c in cores],
         )
-        one = swap(0)
-        two = swap(1)
-        M[0] = middle(first)
+        one, two = [], []
+        for half in firsts:
+            one.append(swap(half, 0))
+            two.append(swap(half, 1))
+        one, two = (jnp.concatenate(halves, axis=1) for halves in (one, two))
         X[0] = jnp.where(odd, two, one)
         B[0] = jnp.where(odd, one, two)
+        M[0] = middle(own[0])
 
     def send(k, *ties):
         tie = lambda value: after(value, *ties) if ties else value

time: 267 us -> 269 us (level)
  waiting for transfers between devices: 116 us -> 126 us
  starting transfers between devices: 65.5 us -> 60.9 us
    ppermute x24, waiting for transfers between devices: 68 us -> 89.8 us  [hop(): return lax.ppermute(value, 'rows', both)]
    ppermute x16, waiting for transfers between devices: 46.4 us -> 33.7 us  [local_plane(): lax.ppermute(value, 'rows', [(i, i ^ 1) for i in range(8)])]
    ppermute x24, starting transfers between devices: 43.6 us -> 39.9 us  [hop(): return lax.ppermute(value, 'rows', both)]
    ppermute x16, starting transfers between devices: 17.3 us -> 14.3 us  [local_plane(): lax.ppermute(value, 'rows', [(i, i ^ 1) for i in range(8)])]
    ppermute x2 -> x4, starting transfers between devices: 4.61 us -> 6.72 us  [send_first(): lax.ppermute(half, ('rows', 'width'), [(flat(r, c), flat(r ^ (1 if (c + t...]
    pallas_call x2 -> x3, Pallas kernels: 8.96 us -> 10.3 us  [the longest x1 6.94 us: encode_rest(): pl.pallas_call(encode_rest_body, grid=(steps,), in_specs=[pl.BlockSpec(ga...]
    unnamed x22 -> x24, local copies, waits for them, and re-layouts: 7.03 us -> 6.45 us
  transfers between devices with their start and end apart: 42 -> 44, of which waited for: 18 -> 20; matrix products, arithmetic and copies ran while one was open for 2% -> 1% of each run, Pallas kernels for 24% -> 23%
where the time goes in v6:
time: 269 us; the launch traced here: 266 us
  waiting for transfers between devices  126 us (47%)
  Pallas kernels  67.6 us (25%)
  starting transfers between devices  60.9 us (23%)
  local copies, waits for them, and re-layouts  7.18 us (3%)
  other arithmetic  3.19 us (1%)
    ppermute x24, waiting for transfers between devices, hop(): return lax.ppermute(value, 'rows', both)  89.8 us
    pallas_call x30, Pallas kernels, decode(): pl.pallas_call(functools.partial(decode_body, places=places, pieces=piece...  57.1 us
    ppermute x24, starting transfers between devices, hop(): return lax.ppermute(value, 'rows', both)  39.9 us
    ppermute x16, waiting for transfers between devices, local_plane(): lax.ppermute(value, 'rows', [(i, i ^ 1) for i in range(8)])  33.7 us
    ppermute x16, starting transfers between devices, local_plane(): lax.ppermute(value, 'rows', [(i, i ^ 1) for i in range(8)])  14.3 us
    pallas_call x1, Pallas kernels, encode_rest(): pl.pallas_call(encode_rest_body, grid=(steps,), in_specs=[pl.BlockSpec(ga...  6.94 us
    ppermute x4, starting transfers between devices, send_first(): lax.ppermute(half, ('rows', 'width'), [(flat(r, c), flat(r ^ (1 if (c + t...  6.72 us
    unnamed x24, local copies, waits for them, and re-layouts  6.45 us
  transfers between devices with their start and end apart: 44, of which 20 were waited for; matrix products, arithmetic and copies ran while one was open for 1% of the time, Pallas kernels for 23%

profile of v6, /device:TPU:0, one launch (start us, length us, event | category | flops | bytes accessed | tf_op | source)
XLA Modules:
  0.0 266.4 jit_solution(12456316548675593730)
XLA Ops:
  0.6 1.7 encode_first.2
  2.4 3.0 %collective-permute-start.3 = (bf16[192,1024]{1,0:T(8,128)(2,1)S(1)}, bf16[192,1024]{1,0:T(8,128)(2,1)S(1)}, u32[]{:S(2)}, u32[]{:S(2)}) collective-permute-start(bf16[192,1024]{1,0:T(8,128)(2,1)S(1)} %get-tuple-element.108.refs_0_), channel_id=1, source_target_pairs={{0,4},{1,9},{2,6},{3,11},{4,0},{5,13},{6,2},{7,15},{8,12},{9,1},{1... | collective-permute-start | bytes 1179656 | tf_op jit(solution)/shard_map/ppermute | solution.py:343
  5.4 1.6 collective-permute-start.1
  7.0 1.7 encode_first.3
  8.7 6.9 %encode_rest.1 = (bf16[192,2048]{1,0:T(8,128)(2,1)}, bf16[192,2048]{1,0:T(8,128)(2,1)}, bf16[192,2048]{1,0:T(8,128)(2,1)}, bf16[192,2048]{1,0:T(8,128)(2,1)}, f32[3,1,2048]{2,1,0:T(1,128)S(1)}) custom-call(f32[384]{0:T(512)S(1)} %copy-done.8, f32[384,2048]{1,0:T(8,128)} %wu1.1, f32[384,2048]{1,0:T(8,128)} %au1.1, f32[384,2048]{1,0:T(8,128)} %wg.1, ...), custom_call_target="tpu_custom_call" | custom-call | tf_op jit(solution)/shard_map/encode_rest/pallas_call | solution.py:84
  16.3 1.9 collective-permute-start.2
  18.2 1.5 collective-permute-done.m1_ref
  20.5 4.4 %collective-permute-start.7 = (bf16[192,2048]{1,0:T(8,128)(2,1)}, bf16[192,2048]{1,0:T(8,128)(2,1)S(1)}, u32[]{:S(2)}, u32[]{:S(2)}) collective-permute-start(bf16[192,2048]{1,0:T(8,128)(2,1)} %get-tuple-element.115.refs_0_), channel_id=1, source_target_pairs={{0,8},{4,12},{8,0},{12,4},{16,24},{20,28},{24,16},{28,20},{1,9},{5... | collective-permute-start | bytes 2359304 | tf_op jit(solution)/shard_map/ppermute | solution.py:285
  25.6 2.5 collective-permute-done.4
  28.1 1.5 collective-permute-start.8
  29.8 3.5 %collective-permute-start.5 = (f32[6,1,2048]{2,1,0:T(1,128)S(1)}, f32[6,1,2048]{2,1,0:T(1,128)S(1)}, u32[]{:S(2)}, u32[]{:S(2)}) collective-permute-start(f32[6,1,2048]{2,1,0:T(1,128)S(1)} %pad_maximum_fusion), channel_id=1, source_target_pairs={{0,16},{4,20},{16,0},{20,4},{8,24},{12,28},{24,8},{28,12},{1,17},{... | collective-permute-start | bytes 147464 | tf_op jit(solution)/shard_map/ppermute | solution.py:285
  33.3 25.7 %collective-permute-done.5.m2_ref = f32[6,1,2048]{2,1,0:T(1,128)S(1)} collective-permute-done((f32[6,1,2048]{2,1,0:T(1,128)S(1)}, f32[6,1,2048]{2,1,0:T(1,128)S(1)}, u32[]{:S(2)}, u32[]{:S(2)}) %collective-permute-start.5) | collective-permute-done | bytes 49184 | tf_op jit(solution)/shard_map/ppermute | solution.py:285
  60.5 1.5 collective-permute-start.9
  62.5 1.5 collective-permute-start.18
  64.1 14.2 %collective-permute-done.10.most1_ref = f32[2,1,2048]{2,1,0:T(1,128)S(1)} collective-permute-done((f32[2,1,2048]{2,1,0:T(1,128)S(1)}, f32[2,1,2048]{2,1,0:T(1,128)S(1)}, u32[]{:S(2)}, u32[]{:S(2)}) %collective-permute-start.10) | collective-permute-done | bytes 16416 | tf_op jit(solution)/shard_map/ppermute | solution.py:287
  79.8 1.6 collective-permute-start.16
  82.7 1.6 collective-permute-start.14
  86.6 2.2 decode.30
  91.1 2.2 decode.33
  93.3 5.6 %collective-permute-done.22.refs_0_ = bf16[192,2048]{1,0:T(8,128)(2,1)S(1)} collective-permute-done((bf16[192,2048]{1,0:T(8,128)(2,1)}, bf16[192,2048]{1,0:T(8,128)(2,1)S(1)}, u32[]{:S(2)}, u32[]{:S(2)}) %collective-permute-start.22) | collective-permute-done | bytes 786464 | tf_op jit(solution)/shard_map/ppermute | solution.py:285
  100.3 1.8 decode.31
  102.1 1.8 decode.32
  103.9 1.8 decode.34
  105.7 1.8 decode.35
  108.2 1.8 decode.38
  109.9 2.9 %decode.39 = (bf16[3072,2048]{1,0:T(8,128)(2,1)}, f32[8,128]{1,0:T(8,128)}) custom-call(s32[1]{0:T(128)} %bitcast.me_ref, f32[24,1,2048]{2,1,0:T(1,128)S(1)} %get-tuple-element.120.r_ref, bf16[192,2048]{1,0:T(8,128)(2,1)} %collective-permute-done.11.refs_0_, bf16[3072,2048]{1,0:T(8,128)(2,1)} %get-tuple-element.145.refs_1_), custom_call_target="tpu_custom_call", output_to_operand_aliasing={{0}: (3, {})} | custom-call | tf_op jit(solution)/shard_map/decode/pallas_call | solution.py:220
  113.6 2.3 collective-permute-done.15
  119.0 13.8 %collective-permute-done.28 = bf16[192,2048]{1,0:T(8,128)(2,1)} collective-permute-done((bf16[192,2048]{1,0:T(8,128)(2,1)}, bf16[192,2048]{1,0:T(8,128)(2,1)}, u32[]{:S(2)}, u32[]{:S(2)}) %collective-permute-start.28) | collective-permute-done | bytes 786464 | tf_op jit(solution)/shard_map/ppermute | solution.py:285
  136.7 1.6 collective-permute-start.30
  138.3 2.9 %decode.36 = (bf16[3072,2048]{1,0:T(8,128)(2,1)}, f32[8,128]{1,0:T(8,128)}) custom-call(s32[1]{0:T(128)} %bitcast.me_ref, f32[24,1,2048]{2,1,0:T(1,128)S(1)} %get-tuple-element.120.r_ref, bf16[192,2048]{1,0:T(8,128)(2,1)} %collective-permute-done.21.refs_0_, bf16[3072,2048]{1,0:T(8,128)(2,1)} %get-tuple-element.140.refs_1_), custom_call_target="tpu_custom_call", output_to_operand_aliasing={{0}: (3, {})} | custom-call | tf_op jit(solution)/shard_map/decode/pallas_call | solution.py:220
  141.2 1.8 decode.37
  143.0 2.9 %decode.40 = (bf16[3072,2048]{1,0:T(8,128)(2,1)}, f32[8,128]{1,0:T(8,128)}) custom-call(s32[1]{0:T(128)} %bitcast.me_ref, f32[24,1,2048]{2,1,0:T(1,128)S(1)} %get-tuple-element.120.r_ref, bf16[192,2048]{1,0:T(8,128)(2,1)} %collective-permute-done.14.refs_0_, bf16[3072,2048]{1,0:T(8,128)(2,1)} %get-tuple-element.146.refs_1_), custom_call_target="tpu_custom_call", output_to_operand_aliasing={{0}: (3, {})} | custom-call | tf_op jit(solution)/shard_map/decode/pallas_call | solution.py:220
  145.9 1.8 decode.41
  147.7 1.8 decode.44
  149.4 1.8 decode.45
  154.5 1.8 decode.42
  156.3 1.8 decode.43
  158.7 7.6 %collective-permute-done.33 = bf16[192,2048]{1,0:T(8,128)(2,1)S(1)} collective-permute-done((bf16[192,2048]{1,0:T(8,128)(2,1)}, bf16[192,2048]{1,0:T(8,128)(2,1)S(1)}, u32[]{:S(2)}, u32[]{:S(2)}) %collective-permute-start.33) | collective-permute-done | bytes 786464 | tf_op jit(solution)/shard_map/ppermute | solution.py:285
  166.3 3.7 %collective-permute-done.30.refs_0_ = bf16[192,2048]{1,0:T(8,128)(2,1)S(1)} collective-permute-done((bf16[192,2048]{1,0:T(8,128)(2,1)S(1)}, bf16[192,2048]{1,0:T(8,128)(2,1)S(1)}, u32[]{:S(2)}, u32[]{:S(2)}) %collective-permute-start.30) | collective-permute-done | bytes 786464 | tf_op jit(solution)/shard_map/ppermute | solution.py:287
  172.0 1.8 decode.46
  173.8 11.6 %collective-permute-done.26 = bf16[192,2048]{1,0:T(8,128)(2,1)S(1)} collective-permute-done((bf16[192,2048]{1,0:T(8,128)(2,1)S(1)}, bf16[192,2048]{1,0:T(8,128)(2,1)S(1)}, u32[]{:S(2)}, u32[]{:S(2)}) %collective-permute-start.26) | collective-permute-done | bytes 786464 | tf_op jit(solution)/shard_map/ppermute | solution.py:285
  189.5 1.8 decode.47
  191.2 1.8 decode.50
  193.0 1.8 decode.51
  194.8 8.9 %collective-permute-done.34.refs_0_ = bf16[192,2048]{1,0:T(8,128)(2,1)S(1)} collective-permute-done((bf16[192,2048]{1,0:T(8,128)(2,1)S(1)}, bf16[192,2048]{1,0:T(8,128)(2,1)S(1)}, u32[]{:S(2)}, u32[]{:S(2)}) %collective-permute-start.34) | collective-permute-done | bytes 786464 | tf_op jit(solution)/shard_map/ppermute | solution.py:287
  203.7 1.5 collective-permute-start.39
  205.2 1.8 decode.48
  207.1 1.8 decode.49
  209.4 9.6 %collective-permute-done.31 = bf16[192,2048]{1,0:T(8,128)(2,1)S(1)} collective-permute-done((bf16[192,2048]{1,0:T(8,128)(2,1)S(1)}, bf16[192,2048]{1,0:T(8,128)(2,1)S(1)}, u32[]{:S(2)}, u32[]{:S(2)}) %collective-permute-start.31) | collective-permute-done | bytes 786464 | tf_op jit(solution)/shard_map/ppermute | solution.py:285
  219.1 1.5 collective-permute-done.32.refs_0_
  220.6 1.8 decode.52
  222.4 1.8 decode.53
  224.8 6.9 %collective-permute-start.37 = (bf16[192,2048]{1,0:T(8,128)(2,1)S(1)}, bf16[192,2048]{1,0:T(8,128)(2,1)S(1)}, u32[]{:S(2)}, u32[]{:S(2)}) collective-permute-start(bf16[192,2048]{1,0:T(8,128)(2,1)S(1)} %get-tuple-element.181.refs_0_), channel_id=1, source_target_pairs={{0,8},{4,12},{8,0},{12,4},{16,24},{20,28},{24,16},{28,20},{1,9},{5... | collective-permute-start | bytes 2359304 | tf_op jit(solution)/shard_map/ppermute | solution.py:285
  231.7 4.2 %collective-permute-done.39 = bf16[192,2048]{1,0:T(8,128)(2,1)S(1)} collective-permute-done((bf16[192,2048]{1,0:T(8,128)(2,1)S(1)}, bf16[192,2048]{1,0:T(8,128)(2,1)S(1)}, u32[]{:S(2)}, u32[]{:S(2)}) %collective-permute-start.39) | collective-permute-done | bytes 786464 | tf_op jit(solution)/shard_map/ppermute | solution.py:285
  237.4 5.7 %collective-permute-start.42 = (bf16[144,2048]{1,0:T(8,128)(2,1)S(1)}, bf16[144,2048]{1,0:T(8,128)(2,1)S(1)}, u32[]{:S(2)}, u32[]{:S(2)}) collective-permute-start(bf16[144,2048]{1,0:T(8,128)(2,1)S(1)} %slice.35), channel_id=1, source_target_pairs={{0,8},{4,12},{8,0},{12,4},{16,24},{20,28},{24,16},{28,20},{1,9},{5... | collective-permute-start | bytes 1769480 | tf_op jit(solution)/shard_map/ppermute | solution.py:285
  243.1 1.8 collective-permute-start.43
  245.0 7.8 %collective-permute-done.37.refs_0_ = bf16[192,2048]{1,0:T(8,128)(2,1)S(1)} collective-permute-done((bf16[192,2048]{1,0:T(8,128)(2,1)S(1)}, bf16[192,2048]{1,0:T(8,128)(2,1)S(1)}, u32[]{:S(2)}, u32[]{:S(2)}) %collective-permute-start.37) | collective-permute-done | bytes 786464 | tf_op jit(solution)/shard_map/ppermute | solution.py:285
  252.8 1.5 collective-permute-start.41
  254.4 1.8 decode.56
  256.2 1.8 decode.57
  257.9 1.8 decode.54
  259.7 1.8 decode.55
  262.7 2.0 decode.58
  264.8 1.5 decode.59
  (100 shorter events, 35.8 us)
Async XLA Ops:
  0.6 8.1 %copy-start.8 = (f32[384]{0:T(512)S(1)}, f32[384]{0:T(512)}, u32[]{:S(2)}) copy-start(f32[384]{0:T(512)} %gain_ref.1) | copy-start | bytes 4612
  2.4 18.1 %collective-permute-start.3 = (bf16[192,1024]{1,0:T(8,128)(2,1)S(1)}, bf16[192,1024]{1,0:T(8,128)(2,1)S(1)}, u32[]{:S(2)}, u32[]{:S(2)}) collective-permute-start(bf16[192,1024]{1,0:T(8,128)(2,1)S(1)} %get-tuple-element.108.refs_0_), channel_id=1, source_target_pairs={{0,4},{1,9},{2,6},{3,11},{4,0},{5,13},{6,2},{7,15},{8,12},{9,1},{1... | collective-permute-start | bytes 1179656 | tf_op jit(solution)/shard_map/ppermute | solution.py:343
  5.4 19.6 %collective-permute-start.1 = (bf16[192,1024]{1,0:T(8,128)(2,1)S(1)}, bf16[192,1024]{1,0:T(8,128)(2,1)S(1)}, u32[]{:S(2)}, u32[]{:S(2)}) collective-permute-start(bf16[192,1024]{1,0:T(8,128)(2,1)S(1)} %get-tuple-element.108.refs_0_), channel_id=1, source_target_pairs={{0,8},{1,5},{2,10},{3,7},{4,12},{5,1},{6,14},{7,3},{8,0},{9,13},{1... | collective-permute-start | bytes 1179656 | tf_op jit(solution)/shard_map/ppermute | solution.py:343
  15.6 4.1 %collective-permute-start = (f32[3,1,2048]{2,1,0:T(1,128)S(1)}, f32[3,1,2048]{2,1,0:T(1,128)S(1)}, u32[]{:S(2)}, u32[]{:S(2)}) collective-permute-start(f32[3,1,2048]{2,1,0:T(1,128)S(1)} %get-tuple-element.112.m0_ref), channel_id=1, source_target_pairs={{0,8},{4,12},{8,0},{12,4},{16,24},{20,28},{24,16},{28,20},{1,9},{5... | collective-permute-start | bytes 73736 | tf_op jit(solution)/shard_map/ppermute | solution.py:285
  16.1 12.0 %collective-permute-start.4 = (bf16[192,1024]{1,0:T(8,128)(2,1)S(1)}, bf16[192,1024]{1,0:T(8,128)(2,1)S(1)}, u32[]{:S(2)}, u32[]{:S(2)}) collective-permute-start(bf16[192,1024]{1,0:T(8,128)(2,1)S(1)} %get-tuple-element.109.refs_1_), channel_id=1, source_target_pairs={{0,4},{1,9},{2,6},{3,11},{4,0},{5,13},{6,2},{7,15},{8,12},{9,1},{1... | collective-permute-start | bytes 1179656 | tf_op jit(solution)/shard_map/ppermute | solution.py:343
  16.3 13.4 %collective-permute-start.2 = (bf16[192,1024]{1,0:T(8,128)(2,1)S(1)}, bf16[192,1024]{1,0:T(8,128)(2,1)S(1)}, u32[]{:S(2)}, u32[]{:S(2)}) collective-permute-start(bf16[192,1024]{1,0:T(8,128)(2,1)S(1)} %get-tuple-element.109.refs_1_), channel_id=1, source_target_pairs={{0,8},{1,5},{2,10},{3,7},{4,12},{5,1},{6,14},{7,3},{8,0},{9,13},{1... | collective-permute-start | bytes 1179656 | tf_op jit(solution)/shard_map/ppermute | solution.py:343
  19.7 42.8 %collective-permute-start.13 = (bf16[192,2048]{1,0:T(8,128)(2,1)}, bf16[192,2048]{1,0:T(8,128)(2,1)S(1)}, u32[]{:S(2)}, u32[]{:S(2)}) collective-permute-start(bf16[192,2048]{1,0:T(8,128)(2,1)} %get-tuple-element.115.refs_0_), channel_id=1, source_target_pairs={{8,16},{12,20},{16,8},{20,12},{9,17},{13,21},{17,9},{21,13},{10,18... | collective-permute-start | bytes 2359304 | tf_op jit(solution)/shard_map/ppermute | solution.py:285
  20.5 39.0 %collective-permute-start.7 = (bf16[192,2048]{1,0:T(8,128)(2,1)}, bf16[192,2048]{1,0:T(8,128)(2,1)S(1)}, u32[]{:S(2)}, u32[]{:S(2)}) collective-permute-start(bf16[192,2048]{1,0:T(8,128)(2,1)} %get-tuple-element.115.refs_0_), channel_id=1, source_target_pairs={{0,8},{4,12},{8,0},{12,4},{16,24},{20,28},{24,16},{28,20},{1,9},{5... | collective-permute-start | bytes 2359304 | tf_op jit(solution)/shard_map/ppermute | solution.py:285
  25.0 35.6 %collective-permute-start.6 = (bf16[192,2048]{1,0:T(8,128)(2,1)}, bf16[192,2048]{1,0:T(8,128)(2,1)S(1)}, u32[]{:S(2)}, u32[]{:S(2)}) collective-permute-start(bf16[192,2048]{1,0:T(8,128)(2,1)} %get-tuple-element.115.refs_0_), channel_id=1, source_target_pairs={{0,4},{4,0},{8,12},{12,8},{16,20},{20,16},{24,28},{28,24},{1,5},{5... | collective-permute-start | bytes 2359304 | tf_op jit(solution)/shard_map/ppermute | solution.py:287
  28.1 31.4 %collective-permute-start.8 = (bf16[192,2048]{1,0:T(8,128)(2,1)}, bf16[192,2048]{1,0:T(8,128)(2,1)}, u32[]{:S(2)}, u32[]{:S(2)}) collective-permute-start(bf16[192,2048]{1,0:T(8,128)(2,1)} %get-tuple-element.116.refs_0_), channel_id=1, source_target_pairs={{8,16},{12,20},{16,8},{20,12},{9,17},{13,21},{17,9},{21,13},{10,18... | collective-permute-start | bytes 2359304 | tf_op jit(solution)/shard_map/ppermute | solution.py:285
  29.8 29.1 %collective-permute-start.5 = (f32[6,1,2048]{2,1,0:T(1,128)S(1)}, f32[6,1,2048]{2,1,0:T(1,128)S(1)}, u32[]{:S(2)}, u32[]{:S(2)}) collective-permute-start(f32[6,1,2048]{2,1,0:T(1,128)S(1)} %pad_maximum_fusion), channel_id=1, source_target_pairs={{0,16},{4,20},{16,0},{20,4},{8,24},{12,28},{24,8},{28,12},{1,17},{... | collective-permute-start | bytes 147464 | tf_op jit(solution)/shard_map/ppermute | solution.py:285
  58.9 19.9 %collective-permute-start.12 = (bf16[192,2048]{1,0:T(8,128)(2,1)}, bf16[192,2048]{1,0:T(8,128)(2,1)S(1)}, u32[]{:S(2)}, u32[]{:S(2)}) collective-permute-start(bf16[192,2048]{1,0:T(8,128)(2,1)} %get-tuple-element.122.refs_1_), channel_id=1, source_target_pairs={{0,4},{4,0},{8,12},{12,8},{16,20},{20,16},{24,28},{28,24},{1,5},{5... | collective-permute-start | bytes 2359304 | tf_op jit(solution)/shard_map/ppermute | solution.py:287
  59.5 21.8 %collective-permute-start.11 = (bf16[192,2048]{1,0:T(8,128)(2,1)}, bf16[192,2048]{1,0:T(8,128)(2,1)}, u32[]{:S(2)}, u32[]{:S(2)}) collective-permute-start(bf16[192,2048]{1,0:T(8,128)(2,1)} %get-tuple-element.122.refs_1_), channel_id=1, source_target_pairs={{0,8},{4,12},{8,0},{12,4},{16,24},{20,28},{24,16},{28,20},{1,9},{5... | collective-permute-start | bytes 2359304 | tf_op jit(solution)/shard_map/ppermute | solution.py:285
  59.6 1.0 copy-start.4
  60.5 17.8 %collective-permute-start.9 = (bf16[16,2048]{1,0:T(8,128)(2,1)S(1)}, bf16[16,2048]{1,0:T(8,128)(2,1)S(1)}, u32[]{:S(2)}, u32[]{:S(2)}) collective-permute-start(bf16[16,2048]{1,0:T(8,128)(2,1)S(1)} %get-tuple-element.117.scale0_ref), channel_id=1, source_target_pairs={{0,4},{4,0},{8,12},{12,8},{16,20},{20,16},{24,28},{28,24},{1,5},{5... | collective-permute-start | bytes 196616 | tf_op jit(solution)/shard_map/ppermute | solution.py:287
  62.0 16.3 %collective-permute-start.10 = (f32[2,1,2048]{2,1,0:T(1,128)S(1)}, f32[2,1,2048]{2,1,0:T(1,128)S(1)}, u32[]{:S(2)}, u32[]{:S(2)}) collective-permute-start(f32[2,1,2048]{2,1,0:T(1,128)S(1)} %get-tuple-element.119.most0_ref), channel_id=1, source_target_pairs={{0,4},{4,0},{8,12},{12,8},{16,20},{20,16},{24,28},{28,24},{1,5},{5... | collective-permute-start | bytes 49160 | tf_op jit(solution)/shard_map/ppermute | solution.py:287
  62.5 16.3 %copy-start.9 = (bf16[192,2048]{1,0:T(8,128)(2,1)}, bf16[192,2048]{1,0:T(8,128)(2,1)S(1)}, u32[]{:S(2)}) copy-start(bf16[192,2048]{1,0:T(8,128)(2,1)S(1)} %collective-permute-done.13) | copy-start | bytes 2359300
  62.5 20.2 %collective-permute-start.18 = (bf16[192,2048]{1,0:T(8,128)(2,1)}, bf16[192,2048]{1,0:T(8,128)(2,1)}, u32[]{:S(2)}, u32[]{:S(2)}) collective-permute-start(bf16[192,2048]{1,0:T(8,128)(2,1)} %get-tuple-element.122.refs_1_), channel_id=1, source_target_pairs={{8,16},{12,20},{16,8},{20,12},{9,17},{13,21},{17,9},{21,13},{10,18... | collective-permute-start | bytes 2359304 | tf_op jit(solution)/shard_map/ppermute | solution.py:285
  78.3 20.6 %collective-permute-start.22 = (bf16[192,2048]{1,0:T(8,128)(2,1)}, bf16[192,2048]{1,0:T(8,128)(2,1)S(1)}, u32[]{:S(2)}, u32[]{:S(2)}) collective-permute-start(bf16[192,2048]{1,0:T(8,128)(2,1)} %get-tuple-element.126.refs_1_), channel_id=1, source_target_pairs={{0,8},{4,12},{8,0},{12,4},{16,24},{20,28},{24,16},{28,20},{1,9},{5... | collective-permute-start | bytes 2359304 | tf_op jit(solution)/shard_map/ppermute | solution.py:285
  78.3 20.7 %collective-permute-start.21 = (bf16[192,2048]{1,0:T(8,128)(2,1)}, bf16[192,2048]{1,0:T(8,128)(2,1)}, u32[]{:S(2)}, u32[]{:S(2)}) collective-permute-start(bf16[192,2048]{1,0:T(8,128)(2,1)} %get-tuple-element.126.refs_1_), channel_id=1, source_target_pairs={{0,4},{4,0},{8,12},{12,8},{16,20},{20,16},{24,28},{28,24},{1,5},{5... | collective-permute-start | bytes 2359304 | tf_op jit(solution)/shard_map/ppermute | solution.py:287
  78.8 0.9 copy-start.6
  79.8 33.1 %collective-permute-start.16 = (bf16[192,2048]{1,0:T(8,128)(2,1)}, bf16[192,2048]{1,0:T(8,128)(2,1)}, u32[]{:S(2)}, u32[]{:S(2)}) collective-permute-start(bf16[192,2048]{1,0:T(8,128)(2,1)} %get-tuple-element.126.refs_1_), channel_id=1, source_target_pairs={{8,16},{12,20},{16,8},{20,12},{9,17},{13,21},{17,9},{21,13},{10,18... | collective-permute-start | bytes 2359304 | tf_op jit(solution)/shard_map/ppermute | solution.py:285
  81.3 34.6 %collective-permute-start.15 = (bf16[192,2048]{1,0:T(8,128)(2,1)}, bf16[192,2048]{1,0:T(8,128)(2,1)}, u32[]{:S(2)}, u32[]{:S(2)}) collective-permute-start(bf16[192,2048]{1,0:T(8,128)(2,1)} %collective-permute-done.8), channel_id=1, source_target_pairs={{8,0},{12,4},{16,24},{20,28},{9,1},{13,5},{17,25},{21,29},{10,2},{... | collective-permute-start | bytes 2359304 | tf_op jit(solution)/shard_map/ppermute | solution.py:285
  82.7 34.9 %collective-permute-start.14 = (bf16[192,2048]{1,0:T(8,128)(2,1)}, bf16[192,2048]{1,0:T(8,128)(2,1)}, u32[]{:S(2)}, u32[]{:S(2)}) collective-permute-start(bf16[192,2048]{1,0:T(8,128)(2,1)} %collective-permute-done.11.refs_0_), channel_id=1, source_target_pairs={{0,4},{4,0},{8,12},{12,8},{16,20},{20,16},{24,28},{28,24},{1,5},{5... | collective-permute-start | bytes 2359304 | tf_op jit(solution)/shard_map/ppermute | solution.py:287
  84.3 1.1 copy-start.2
  85.4 1.1 copy-start.3
  88.8 1.1 copy-start
  89.9 1.1 copy-start.1
  99.0 33.7 %collective-permute-start.28 = (bf16[192,2048]{1,0:T(8,128)(2,1)}, bf16[192,2048]{1,0:T(8,128)(2,1)}, u32[]{:S(2)}, u32[]{:S(2)}) collective-permute-start(bf16[192,2048]{1,0:T(8,128)(2,1)} %copy-done.9), channel_id=1, source_target_pairs={{8,0},{12,4},{16,24},{20,28},{9,1},{13,5},{17,25},{21,29},{10,2},{... | collective-permute-start | bytes 2359304 | tf_op jit(solution)/shard_map/ppermute | solution.py:285
  102.1 3.6 %copy-start.5 = (bf16[192,2048]{1,0:T(8,128)(2,1)S(1)}, bf16[192,2048]{1,0:T(8,128)(2,1)}, u32[]{:S(2)}) copy-start(bf16[192,2048]{1,0:T(8,128)(2,1)} %copy-done.4) | copy-start | bytes 2359300
  103.9 4.3 %copy-start.7 = (bf16[192,2048]{1,0:T(8,128)(2,1)S(1)}, bf16[192,2048]{1,0:T(8,128)(2,1)}, u32[]{:S(2)}) copy-start(bf16[192,2048]{1,0:T(8,128)(2,1)} %copy-done.6) | copy-start | bytes 2359300
  107.4 27.1 %collective-permute-start.25 = (bf16[192,2048]{1,0:T(8,128)(2,1)S(1)}, bf16[192,2048]{1,0:T(8,128)(2,1)S(1)}, u32[]{:S(2)}, u32[]{:S(2)}) collective-permute-start(bf16[192,2048]{1,0:T(8,128)(2,1)S(1)} %get-tuple-element.149.refs_0_), channel_id=1, source_target_pairs={{8,16},{12,20},{16,8},{20,12},{9,17},{13,21},{17,9},{21,13},{10,18... | collective-permute-start | bytes 2359304 | tf_op jit(solution)/shard_map/ppermute | solution.py:285
  108.2 25.1 %copy-start.10 = (bf16[192,2048]{1,0:T(8,128)(2,1)S(1)}, bf16[192,2048]{1,0:T(8,128)(2,1)}, u32[]{:S(2)}) copy-start(bf16[192,2048]{1,0:T(8,128)(2,1)} %copy-done.9) | copy-start | bytes 2359300
  112.8 23.9 %collective-permute-start.23 = (bf16[192,2048]{1,0:T(8,128)(2,1)S(1)}, bf16[192,2048]{1,0:T(8,128)(2,1)S(1)}, u32[]{:S(2)}, u32[]{:S(2)}) collective-permute-start(bf16[192,2048]{1,0:T(8,128)(2,1)S(1)} %copy-done.5), channel_id=1, source_target_pairs={{8,16},{12,20},{16,8},{20,12},{9,17},{13,21},{17,9},{21,13},{10,18... | collective-permute-start | bytes 2359304 | tf_op jit(solution)/shard_map/ppermute | solution.py:285
  115.9 19.3 %collective-permute-start.27 = (bf16[192,2048]{1,0:T(8,128)(2,1)S(1)}, bf16[192,2048]{1,0:T(8,128)(2,1)S(1)}, u32[]{:S(2)}, u32[]{:S(2)}) collective-permute-start(bf16[192,2048]{1,0:T(8,128)(2,1)S(1)} %collective-permute-done.22.refs_0_), channel_id=1, source_target_pairs={{0,4},{4,0},{8,12},{12,8},{16,20},{20,16},{24,28},{28,24},{1,5},{5... | collective-permute-start | bytes 2359304 | tf_op jit(solution)/shard_map/ppermute | solution.py:287
  117.7 33.6 %collective-permute-start.19 = (bf16[192,2048]{1,0:T(8,128)(2,1)}, bf16[192,2048]{1,0:T(8,128)(2,1)S(1)}, u32[]{:S(2)}, u32[]{:S(2)}) collective-permute-start(bf16[192,2048]{1,0:T(8,128)(2,1)} %collective-permute-done.18), channel_id=1, source_target_pairs={{8,0},{12,4},{16,24},{20,28},{9,1},{13,5},{17,25},{21,29},{10,2},{... | collective-permute-start | bytes 2359304 | tf_op jit(solution)/shard_map/ppermute | solution.py:285
  132.7 20.4 %collective-permute-start.20 = (bf16[192,2048]{1,0:T(8,128)(2,1)S(1)}, bf16[192,2048]{1,0:T(8,128)(2,1)S(1)}, u32[]{:S(2)}, u32[]{:S(2)}) collective-permute-start(bf16[192,2048]{1,0:T(8,128)(2,1)S(1)} %broadcast_select_fusion.6.refs_0_), channel_id=1, source_target_pairs={{0,4},{4,0},{8,12},{12,8},{16,20},{20,16},{24,28},{28,24},{1,5},{5... | collective-permute-start | bytes 2359304 | tf_op jit(solution)/shard_map/ppermute | solution.py:287
  134.5 23.6 %collective-permute-start.17 = (bf16[192,2048]{1,0:T(8,128)(2,1)}, bf16[192,2048]{1,0:T(8,128)(2,1)S(1)}, u32[]{:S(2)}, u32[]{:S(2)}) collective-permute-start(bf16[192,2048]{1,0:T(8,128)(2,1)} %collective-permute-done.11.refs_0_), channel_id=1, source_target_pairs={{8,16},{12,20},{16,8},{20,12},{9,17},{13,21},{17,9},{21,13},{10,18... | collective-permute-start | bytes 2359304 | tf_op jit(solution)/shard_map/ppermute | solution.py:285
  135.2 31.1 %collective-permute-start.33 = (bf16[192,2048]{1,0:T(8,128)(2,1)}, bf16[192,2048]{1,0:T(8,128)(2,1)S(1)}, u32[]{:S(2)}, u32[]{:S(2)}) collective-permute-start(bf16[192,2048]{1,0:T(8,128)(2,1)} %collective-permute-done.16), channel_id=1, source_target_pairs={{8,0},{12,4},{16,24},{20,28},{9,1},{13,5},{17,25},{21,29},{10,2},{... | collective-permute-start | bytes 2359304 | tf_op jit(solution)/shard_map/ppermute | solution.py:285
  136.7 33.3 %collective-permute-start.30 = (bf16[192,2048]{1,0:T(8,128)(2,1)S(1)}, bf16[192,2048]{1,0:T(8,128)(2,1)S(1)}, u32[]{:S(2)}, u32[]{:S(2)}) collective-permute-start(bf16[192,2048]{1,0:T(8,128)(2,1)S(1)} %broadcast_select_fusion.5.refs_0_), channel_id=1, source_target_pairs={{0,4},{4,0},{8,12},{12,8},{16,20},{20,16},{24,28},{28,24},{1,5},{5... | collective-permute-start | bytes 2359304 | tf_op jit(solution)/shard_map/ppermute | solution.py:287
  151.2 34.2 %collective-permute-start.29 = (bf16[192,2048]{1,0:T(8,128)(2,1)S(1)}, bf16[192,2048]{1,0:T(8,128)(2,1)S(1)}, u32[]{:S(2)}, u32[]{:S(2)}) collective-permute-start(bf16[192,2048]{1,0:T(8,128)(2,1)S(1)} %collective-permute-done.22.refs_0_), channel_id=1, source_target_pairs={{8,16},{12,20},{16,8},{20,12},{9,17},{13,21},{17,9},{21,13},{10,18... | collective-permute-start | bytes 2359304 | tf_op jit(solution)/shard_map/ppermute | solution.py:285
  153.1 32.2 %collective-permute-start.26 = (bf16[192,2048]{1,0:T(8,128)(2,1)S(1)}, bf16[192,2048]{1,0:T(8,128)(2,1)S(1)}, u32[]{:S(2)}, u32[]{:S(2)}) collective-permute-start(bf16[192,2048]{1,0:T(8,128)(2,1)S(1)} %collective-permute-done.25), channel_id=1, source_target_pairs={{8,0},{12,4},{16,24},{20,28},{9,1},{13,5},{17,25},{21,29},{10,2},{... | collective-permute-start | bytes 2359304 | tf_op jit(solution)/shard_map/ppermute | solution.py:285
  158.1 28.8 %collective-permute-start.24 = (bf16[192,2048]{1,0:T(8,128)(2,1)S(1)}, bf16[192,2048]{1,0:T(8,128)(2,1)S(1)}, u32[]{:S(2)}, u32[]{:S(2)}) collective-permute-start(bf16[192,2048]{1,0:T(8,128)(2,1)S(1)} %broadcast_select_fusion.7.refs_0_), channel_id=1, source_target_pairs={{0,4},{4,0},{8,12},{12,8},{16,20},{20,16},{24,28},{28,24},{1,5},{5... | collective-permute-start | bytes 2359304 | tf_op jit(solution)/shard_map/ppermute | solution.py:287
  170.1 33.6 %collective-permute-start.34 = (bf16[192,2048]{1,0:T(8,128)(2,1)S(1)}, bf16[192,2048]{1,0:T(8,128)(2,1)S(1)}, u32[]{:S(2)}, u32[]{:S(2)}) collective-permute-start(bf16[192,2048]{1,0:T(8,128)(2,1)S(1)} %broadcast_select_fusion.2.refs_0_), channel_id=1, source_target_pairs={{0,4},{4,0},{8,12},{12,8},{16,20},{20,16},{24,28},{28,24},{1,5},{5... | collective-permute-start | bytes 2359304 | tf_op jit(solution)/shard_map/ppermute | solution.py:287
  170.7 33.0 %collective-permute-start.35 = (bf16[192,2048]{1,0:T(8,128)(2,1)S(1)}, bf16[192,2048]{1,0:T(8,128)(2,1)S(1)}, u32[]{:S(2)}, u32[]{:S(2)}) collective-permute-start(bf16[192,2048]{1,0:T(8,128)(2,1)S(1)} %collective-permute-done.23), channel_id=1, source_target_pairs={{8,0},{12,4},{16,24},{20,28},{9,1},{13,5},{17,25},{21,29},{10,2},{... | collective-permute-start | bytes 2359304 | tf_op jit(solution)/shard_map/ppermute | solution.py:285
  186.9 32.2 %collective-permute-start.31 = (bf16[192,2048]{1,0:T(8,128)(2,1)S(1)}, bf16[192,2048]{1,0:T(8,128)(2,1)S(1)}, u32[]{:S(2)}, u32[]{:S(2)}) collective-permute-start(bf16[192,2048]{1,0:T(8,128)(2,1)S(1)} %collective-permute-done.17), channel_id=1, source_target_pairs={{8,0},{12,4},{16,24},{20,28},{9,1},{13,5},{17,25},{21,29},{10,2},{... | collective-permute-start | bytes 2359304 | tf_op jit(solution)/shard_map/ppermute | solution.py:285
  188.1 32.4 %collective-permute-start.32 = (bf16[192,2048]{1,0:T(8,128)(2,1)S(1)}, bf16[192,2048]{1,0:T(8,128)(2,1)S(1)}, u32[]{:S(2)}, u32[]{:S(2)}) collective-permute-start(bf16[192,2048]{1,0:T(8,128)(2,1)S(1)} %broadcast_select_fusion.3.refs_0_), channel_id=1, source_target_pairs={{0,4},{4,0},{8,12},{12,8},{16,20},{20,16},{24,28},{28,24},{1,5},{5... | collective-permute-start | bytes 2359304 | tf_op jit(solution)/shard_map/ppermute | solution.py:287
  203.7 32.2 %collective-permute-start.39 = (bf16[192,2048]{1,0:T(8,128)(2,1)S(1)}, bf16[192,2048]{1,0:T(8,128)(2,1)S(1)}, u32[]{:S(2)}, u32[]{:S(2)}) collective-permute-start(bf16[192,2048]{1,0:T(8,128)(2,1)S(1)} %collective-permute-done.29), channel_id=1, source_target_pairs={{8,0},{12,4},{16,24},{20,28},{9,1},{13,5},{17,25},{21,29},{10,2},{... | collective-permute-start | bytes 2359304 | tf_op jit(solution)/shard_map/ppermute | solution.py:285
  208.8 28.6 %collective-permute-start.38 = (bf16[192,2048]{1,0:T(8,128)(2,1)S(1)}, bf16[192,2048]{1,0:T(8,128)(2,1)S(1)}, u32[]{:S(2)}, u32[]{:S(2)}) collective-permute-start(bf16[192,2048]{1,0:T(8,128)(2,1)S(1)} %broadcast_select_fusion.1.refs_0_), channel_id=1, source_target_pairs={{0,4},{4,0},{8,12},{12,8},{16,20},{20,16},{24,28},{28,24},{1,5},{5... | collective-permute-start | bytes 2359304 | tf_op jit(solution)/shard_map/ppermute | solution.py:287
  224.2 35.5 %collective-permute-start.36 = (bf16[192,2048]{1,0:T(8,128)(2,1)S(1)}, bf16[192,2048]{1,0:T(8,128)(2,1)S(1)}, u32[]{:S(2)}, u32[]{:S(2)}) collective-permute-start(bf16[192,2048]{1,0:T(8,128)(2,1)S(1)} %broadcast_select_fusion.4.refs_0_), channel_id=1, source_target_pairs={{0,4},{4,0},{8,12},{12,8},{16,20},{20,16},{24,28},{28,24},{1,5},{5... | collective-permute-start | bytes 2359304 | tf_op jit(solution)/shard_map/ppermute | solution.py:287
  224.8 28.0 %collective-permute-start.37 = (bf16[192,2048]{1,0:T(8,128)(2,1)S(1)}, bf16[192,2048]{1,0:T(8,128)(2,1)S(1)}, u32[]{:S(2)}, u32[]{:S(2)}) collective-permute-start(bf16[192,2048]{1,0:T(8,128)(2,1)S(1)} %get-tuple-element.181.refs_0_), channel_id=1, source_target_pairs={{0,8},{4,12},{8,0},{12,4},{16,24},{20,28},{24,16},{28,20},{1,9},{5... | collective-permute-start | bytes 2359304 | tf_op jit(solution)/shard_map/ppermute | solution.py:285
  237.4 25.3 %collective-permute-start.42 = (bf16[144,2048]{1,0:T(8,128)(2,1)S(1)}, bf16[144,2048]{1,0:T(8,128)(2,1)S(1)}, u32[]{:S(2)}, u32[]{:S(2)}) collective-permute-start(bf16[144,2048]{1,0:T(8,128)(2,1)S(1)} %slice.35), channel_id=1, source_target_pairs={{0,8},{4,12},{8,0},{12,4},{16,24},{20,28},{24,16},{28,20},{1,9},{5... | collective-permute-start | bytes 1769480 | tf_op jit(solution)/shard_map/ppermute | solution.py:285
  243.1 19.6 %collective-permute-start.43 = (bf16[144,2048]{1,0:T(8,128)(2,1)S(1)}, bf16[144,2048]{1,0:T(8,128)(2,1)S(1)}, u32[]{:S(2)}, u32[]{:S(2)}) collective-permute-start(bf16[144,2048]{1,0:T(8,128)(2,1)S(1)} %slice_select_fusion), channel_id=1, source_target_pairs={{0,4},{4,0},{8,12},{12,8},{16,20},{20,16},{24,28},{28,24},{1,5},{5... | collective-permute-start | bytes 1769480 | tf_op jit(solution)/shard_map/ppermute | solution.py:287
  244.9 17.8 %collective-permute-start.40 = (bf16[48,2048]{1,0:T(8,128)(2,1)S(1)}, bf16[48,2048]{1,0:T(8,128)(2,1)S(1)}, u32[]{:S(2)}, u32[]{:S(2)}) collective-permute-start(bf16[48,2048]{1,0:T(8,128)(2,1)S(1)} %slice.32), channel_id=1, source_target_pairs={{0,8},{4,12},{8,0},{12,4},{16,24},{20,28},{24,16},{28,20},{1,9},{5... | collective-permute-start | bytes 589832 | tf_op jit(solution)/shard_map/ppermute | solution.py:285
  252.8 10.0 %collective-permute-start.41 = (bf16[48,2048]{1,0:T(8,128)(2,1)S(1)}, bf16[48,2048]{1,0:T(8,128)(2,1)S(1)}, u32[]{:S(2)}, u32[]{:S(2)}) collective-permute-start(bf16[48,2048]{1,0:T(8,128)(2,1)S(1)} %slice_select_fusion.1), channel_id=1, source_target_pairs={{0,4},{4,0},{8,12},{12,8},{16,20},{20,16},{24,28},{28,24},{1,5},{5... | collective-permute-start | bytes 589832 | tf_op jit(solution)/shard_map/ppermute | solution.py:287
